TPU v7x, 32 devices: a whole 2x2x4 slice. The times are simulated.
32 devices in a mesh: lat: 8 (over z, core), lon: 4 (over y, x).
Axes of the slice: x: 2, y: 2, z: 4, core: 2. Of those that a mesh axis runs over, the one named last changes fastest.
Arguments:
- forcing: float32 [16, 1024, 2048], P(None, 'lat', 'lon'), may hold values from -6 to 6
- metric_lon: float32 [1024, 2048], P('lat', 'lon'), may hold values from -0.5 to 0.5
- metric_lat: float32 [1024, 2048], P('lat', 'lon'), may hold values from -0.5 to 0.5
- lon_weights: float32 [2048], P('lon'), may hold values from 0.5 to 2
- eigen_basis: float32 [2048, 2048], replicated, may hold values from -0.125 to 0.125
- lower_mult: float32 [16, 1024, 2048], P('lon', 'lat'), may hold values from -1 to 0
- pivot_inverse: float32 [16, 1024, 2048], P('lon', 'lat'), may hold values from 0 to 2
- upper_coef: float32 [16, 1024, 2048], P('lon', 'lat'), may hold values from -8388608 to 0
Outputs:
- solution: float32 [16, 1024, 2048], P(None, 'lat', 'lon')
All inputs are finite; a program needn't handle non-finite values.
Results may differ from a plain program's by a relative error of at most 0.000082.
Values sent between devices are 32-bit elements; how exact they have to be, the bound alone decides.
No kernel may reach another device: no remote copies, remote signals or barrier semaphores. Data moves between devices by JAX's collectives and lax.ppermute only.
A program may use at most 128 MiB of HBM per device.

v0:
```python
import jax
import jax.numpy as jnp
from jax import lax
from jax.sharding import PartitionSpec as P


def padded(shard, sides, width, wrap):
    for axis, dim in sides:
        count, length = (lax.axis_size(axis), shard.shape[dim])
        up = [(i, (i + 1) % count) for i in range(count if wrap else count - 1)]
        down = [(j, i) for i, j in up]
        last = lax.slice_in_dim(shard, length - width, length, axis=dim)
        initial = lax.slice_in_dim(shard, 0, width, axis=dim)
        before = lax.ppermute(last, axis, up)
        after = lax.ppermute(initial, axis, down)
        shard = jnp.concatenate([before, shard, after], axis=dim)
    return shard


def prefix(part, axis, combine, identity, reverse):
    count = lax.axis_size(axis)
    place = lax.axis_index(axis)
    ahead = count - 1 - place if reverse else place
    gathered = jax.tree.map(lambda a: lax.all_gather(a, axis), part)
    state = jax.tree.map(lambda a, e: jnp.zeros_like(a) + jnp.asarray(e, a.dtype), part, identity)

    def one(hop, state):
        source = count - 1 - hop if reverse else hop
        return combine(
            state, jax.tree.map(lambda a: lax.dynamic_index_in_dim(a, source, 0, False), gathered)
        )

    return lax.fori_loop(0, ahead, one, state)


def compose(earlier, later):
    return (later[0] * earlier[0], later[0] * earlier[1] + later[1])


def band_recurrence(factor, source, reverse_order):
    modes, rows, columns = factor.shape
    block = min(8, rows)
    groups = rows // block
    factor_blocks = factor.reshape(modes, groups, block, columns)
    source_blocks = source.reshape(modes, groups, block, columns)
    order = list(range(block))
    if reverse_order:
        order = order[::-1]
    running_scale = jnp.ones((modes, groups, columns), jnp.float32)
    running_shift = jnp.zeros((modes, groups, columns), jnp.float32)
    scale_rows = [None] * block
    shift_rows = [None] * block
    for position in order:
        step_factor = factor_blocks[:, :, position, :]
        running_scale = step_factor * running_scale
        running_shift = step_factor * running_shift + source_blocks[:, :, position, :]
        scale_rows[position] = running_scale
        shift_rows[position] = running_shift
    group_order = list(range(groups))
    if reverse_order:
        group_order = group_order[::-1]
    carry_scale = jnp.ones((modes, columns), jnp.float32)
    carry_shift = jnp.zeros((modes, columns), jnp.float32)
    enter_scale = [None] * groups
    enter_shift = [None] * groups
    for group in group_order:
        enter_scale[group] = carry_scale
        enter_shift[group] = carry_shift
        carry_scale, carry_shift = compose(
            (carry_scale, carry_shift), (running_scale[:, group, :], running_shift[:, group, :])
        )
    local_scale = jnp.stack(scale_rows, axis=2)
    local_shift = jnp.stack(shift_rows, axis=2)
    group_scale = jnp.stack(enter_scale, axis=1)[:, :, None, :]
    group_shift = jnp.stack(enter_shift, axis=1)[:, :, None, :]
    full_scale = (local_scale * group_scale).reshape(modes, rows, columns)
    full_shift = (local_shift + local_scale * group_shift).reshape(modes, rows, columns)
    return (full_scale, full_shift, (carry_scale, carry_shift))


def per_device(
    forcing, metric_lon, metric_lat, lon_weights, eigen_basis, lower_mult, pivot_inverse, upper_coef
):
    wrapped = padded(forcing, (("lon", 2),), 1, True)
    stacked = padded(forcing, (("lat", 1),), 1, False)
    source_term = (
        forcing
        + metric_lon * (wrapped[:, :, :-2] + wrapped[:, :, 2:])
        + metric_lat * (stacked[:, :-2, :] + stacked[:, 2:, :])
    )
    weighted = source_term * lon_weights
    spectral = jnp.einsum(
        "kji,im->kjm",
        lax.all_to_all(weighted, "lon", split_axis=0, concat_axis=2, tiled=True),
        eigen_basis,
        precision=lax.Precision.HIGHEST,
    )
    down_scale, down_shift, down_summary = band_recurrence(-lower_mult, spectral, False)
    identity = (jnp.ones_like(down_summary[0]), jnp.zeros_like(down_summary[1]))
    entering = prefix(down_summary, "lat", compose, identity, False)[1]
    sweep = down_shift + down_scale * entering[:, None, :]
    up_factor = -(upper_coef * pivot_inverse)
    up_source = pivot_inverse * sweep
    up_scale, up_shift, up_summary = band_recurrence(up_factor, up_source, True)
    identity_up = (jnp.ones_like(up_summary[0]), jnp.zeros_like(up_summary[1]))
    arriving = prefix(up_summary, "lat", compose, identity_up, True)[1]
    modal = up_shift + up_scale * arriving[:, None, :]
    on_grid = jnp.einsum("kjm,im->kji", modal, eigen_basis, precision=lax.Precision.HIGHEST)
    return lax.all_to_all(on_grid, "lon", split_axis=2, concat_axis=0, tiled=True)


def solution(mesh):
    placed = (
        P(None, "lat", "lon"),
        P("lat", "lon"),
        P("lat", "lon"),
        P("lon"),
        P(),
        P("lon", "lat", None),
        P("lon", "lat", None),
        P("lon", "lat", None),
    )
    return jax.shard_map(
        per_device, mesh=mesh, in_specs=placed, out_specs=P(None, "lat", "lon"), check_vma=False
    )
```

profile of v0, /device:TPU:0, one launch (start us, length us, event | category | flops | bytes accessed | tf_op | source)
XLA Modules:
  0.0 419.0 jit_solution(2387320634835779536)
XLA Ops:
  0.0 1.1 fusion.112
  1.1 2.4 collective-permute-start.2
  3.5 1.4 collective-permute-start.3
  5.0 1.9 fusion.111
  7.2 2.3 collective-permute-start
  10.9 1.3 collective-permute-done
  12.5 1.0 collective-permute-done.1
  14.0 12.0 %fusion.7 = f32[16,128,512]{2,1,0:T(8,128)} fusion(f32[16,1,512]{2,1,0:T(1,128)S(1)} %collective-permute-done.3, f32[16,128,512]{2,1,0:T(8,128)} %param.12, f32[16,1,512]{2,1,0:T(1,128)S(1)} %collective-permute-done.2, f32[16,128,1]{2,1,0:T(8,128)S(1)} %copy.77, f32[16,128,1]{2,1,0:T(8,128)S(1)} %copy.75, f32[512]{0:T(512)S(1)} %copy-done.88, ...), kind=kLoop, calls=%fused_computation.12 | loop fusion | flops 11534336 | bytes 8996864 | tf_op jit(solution)/shard_map/mul | solution.py:91
  26.0 5.4 %all-to-all-start = ((f32[16,128,512]{2,1,0:T(8,128)}), f32[16,128,512]{2,1,0:T(8,128)}, u32[]{:S(2)}, u32[]{:S(2)}) async-start(f32[16,128,512]{2,1,0:T(8,128)} %fusion.7), calls=%async_computation | async-start | bytes 8388608 | tf_op jit(solution)/shard_map/all_to_all | solution.py:94
  31.4 4.8 %negate_bitcast_fusion = f32[4,16,8,2048]{3,2,1,0:T(8,128)} fusion(f32[4,128,2048]{2,1,0:T(8,128)} %param.17), kind=kLoop, calls=%fused_computation.31 | loop fusion | flops 1048576 | bytes 8388608 | tf_op jit(solution)/shard_map/reshape | solution.py:44
  36.2 44.0 %all-to-all-done = f32[16,128,512]{2,1,0:T(8,128)} async-done(((f32[16,128,512]{2,1,0:T(8,128)}), f32[16,128,512]{2,1,0:T(8,128)}, u32[]{:S(2)}, u32[]{:S(2)}) %all-to-all-start) | async-done | bytes 4194336 | tf_op jit(solution)/shard_map/all_to_all | solution.py:94
  80.2 6.9 %copy.406 = f32[4,4,128,512]{3,0,2,1:T(4,128)} copy(f32[4,4,128,512]{3,2,1,0:T(8,128)} %bitcast.6) | data formatting | bytes 8388608 | tf_op jit(solution)/shard_map/all_to_all | solution.py:94
  87.1 6.1 %dot_general.8 = f32[4,16,8,2048]{3,2,1,0:T(8,128)} reshape(f32[4,128,4,512]{3,2,1,0:T(4,128)} %bitcast.617) | data formatting | bytes 8388608 | tf_op jit(solution)/shard_map/kji,im->kjm/dot_general | solution.py:92
  93.2 31.6 %fusion = f32[4,16,8,2048]{3,2,1,0:T(8,128)S(1)} fusion(f32[4,16,8,2048]{3,2,1,0:T(8,128)} %dot_general.8, f32[2048,2048]{1,0:T(8,128)} %param.16), kind=kOutput, calls=%fused_computation.4 | convolution fusion | flops 25769803776 | bytes 25165824 | tf_op jit(solution)/shard_map/kji,im->kjm/dot_general | solution.py:92
  124.8 6.3 %fusion.110 = (f32[4,16,1,2048]{3,2,1,0:T(1,128)S(1)}, f32[4,16,1,2048]{3,2,1,0:T(1,128)S(1)}, f32[4,16,1,2048]{3,2,1,0:T(1,128)S(1)}, f32[4,16,1,2048]{3,2,1,0:...) fusion(f32[4,16,8,2048]{3,2,1,0:T(8,128)S(1)} %fusion, ...), kind=kLoop, calls=%fused_computation.298 | loop fusion | bytes 16777216 | tf_op jit(solution)/shard_map/slice | solution.py:56
  131.1 4.1 bitcast_add_fusion.2
  137.5 1.3 multiply_add_fusion.31
  138.8 1.3 fusion.54
  140.1 15.2 %all_gather.17 = f32[8,4,2048]{2,1,0:T(4,128)S(1)} all-gather(f32[1,4,2048]{2,1,0:T(4,128)S(1)} %copy.97), channel_id=1, replica_groups=mesh['lat'=8,'lon'=4] {'lat'}, dimensions={0}, use_global_device_ids=true | all-gather | bytes 294912 | tf_op jit(solution)/shard_map/all_gather | solution.py:24
  155.3 15.3 %all_gather.16 = f32[8,4,2048]{2,1,0:T(4,128)} all-gather(f32[1,4,2048]{2,1,0:T(4,128)S(1)} %copy.96), channel_id=1, replica_groups=mesh['lat'=8,'lon'=4] {'lat'}, dimensions={0}, use_global_device_ids=true | all-gather | bytes 294912 | tf_op jit(solution)/shard_map/all_gather | solution.py:24
  170.9 3.0 constant_dynamic-update-slice_fusion.5
  173.9 2.9 constant_dynamic-update-slice_fusion.4
  176.8 2.4 constant_dynamic-update-slice_fusion.3
  179.3 1.4 constant_dynamic-update-slice_fusion.2
  180.7 2.0 constant_dynamic-update-slice_fusion.1
  182.9 1.4 constant_dynamic-update-slice_fusion
  184.4 1.9 fusion.46
  188.2 6.8 %multiply_add_fusion.1 = (f32[4,16,8,2048]{3,1,0,2:T(8,128)S(1)}, f32[4,16,8,2048]{3,1,0,2:T(8,128)}) fusion(f32[4,16,8,2048]{3,1,0,2:T(8,128)} %get-tuple-element.299, f32[4,16,8,2048]{3,1,0,2:T(8,128)} %get-tuple-element.300, f32[4,16,2048]{2,1,0:T(8,128)S(1)} %stack.18, f32[4,16,2048]{2,1,0:T(8,128)S(1)} %stack.19), kind=kLoop, calls=%fused_computation.30 | loop fusion | flops 3145728 | bytes 17825792 | tf_op jit(solution)/shard_map/add | solution.py:77
  195.0 15.0 %fusion.16 = (f32[4,16,8,2048]{3,2,1,0:T(8,128)}, f32[4,16,8,2048]{3,2,1,0:T(8,128)}) fusion(f32[4,128,2048]{2,1,0:T(8,128)} %param.18, f32[4,16,8,2048]{3,1,0,2:T(8,128)} %get-tuple-element.268, f32[4,16,8,2048]{3,1,0,2:T(8,128)S(1)} %get-tuple-element.267, f32[4,2048]{1,0:T(4,128)S(1)} %get-tuple-element.133, f32[4,128,2048]{2,1,0:T(8,128)} %param.19), kind=kLoop, calls=%fused_computation.25 | loop fusion | flops 5242880 | bytes 25198592 | tf_op jit(solution)/shard_map/reshape | solution.py:45
  210.0 16.9 %fusion.109 = (f32[4,16,1,2048]{3,2,1,0:T(1,128)S(1)}, f32[4,16,1,2048]{3,2,1,0:T(1,128)S(1)}, f32[4,16,1,2048]{3,2,1,0:T(1,128)S(1)}, f32[4,16,1,2048]{3,2,1,0:...) fusion(f32[4,16,8,2048]{3,2,1,0:T(8,128)} %get-tuple-element.265), kind=kLoop, calls=%fused_computation.297 | loop fusion | bytes 8388608 | tf_op jit(solution)/shard_map/slice | solution.py:56
  226.9 3.0 fusion.114
  230.0 4.1 bitcast_add_fusion.3
  234.5 1.0 slice_multiply_fusion.13
  236.3 1.4 multiply_add_fusion.16
  237.6 6.0 %add_dynamic-update-slice_fusion = (f32[4,16,8,2048]{3,1,0,2:T(8,128)}, f32[4,16,1,2048]{3,1,0,2:T(8,128)}, f32[4,16,1,2048]{3,1,0,2:T(8,128)}, f32[4,16,1,2048]...) fusion(f32[4,16,1,2048]{3,2,1,0:T(1,128)S(1)} %get-tuple-element.264, ...), kind=kLoop, calls=%fused_computation.85 | loop fusion | flops 3014654 | bytes 12058624
  243.6 19.1 %all_gather.19 = f32[8,4,2048]{2,1,0:T(4,128)S(1)} all-gather(f32[1,4,2048]{2,1,0:T(4,128)S(1)} %copy.109), channel_id=1, replica_groups=mesh['lat'=8,'lon'=4] {'lat'}, dimensions={0}, use_global_device_ids=true | all-gather | bytes 294912 | tf_op jit(solution)/shard_map/all_gather | solution.py:24
  262.7 15.3 %all_gather.18 = f32[8,4,2048]{2,1,0:T(4,128)} all-gather(f32[1,4,2048]{2,1,0:T(4,128)S(1)} %copy.108), channel_id=1, replica_groups=mesh['lat'=8,'lon'=4] {'lat'}, dimensions={0}, use_global_device_ids=true | all-gather | bytes 294912 | tf_op jit(solution)/shard_map/all_gather | solution.py:24
  278.0 5.6 %while.27 = (s32[]{:T(128)}, f32[4,2048]{1,0:T(4,128)S(1)}, s32[]{:T(128)}, f32[8,4,2048]{2,1,0:T(4,128)}, f32[8,4,2048]{2,1,0:T(4,128)S(1)}, /*index=5*/s32[]{:T(128)}, s32[]{:T(128)}, s32[]{:T(128)}, s32[]{:T(128)}) while((s32[]{:T(128)}, f32[4,2048]{1,0:T(4,128)S(1)}, s32[]{:T(128)}, f32[8,4,2048]{2,1,0:T(4,128)}, ...), condition=%wide.region_3.4_spmd, body=%wide.region_2.3_spmd.sunk | while | flops 16390 | bytes 131215 | solution.py:33
  283.7 3.1 constant_dynamic-update-slice_fusion.14
  286.7 1.9 constant_dynamic-update-slice_fusion.17
  289.5 1.4 constant_dynamic-update-slice_fusion.12
  292.8 1.9 constant_dynamic-update-slice_fusion.10
  295.6 1.6 fusion.53
  300.0 4.5 %multiply_add_fusion = (f32[4,16,8,2048]{3,1,0,2:T(8,128)S(1)}, f32[4,16,8,2048]{3,1,0,2:T(8,128)S(1)}) fusion(f32[4,16,8,2048]{3,1,0,2:T(8,128)} %get-tuple-element.306, f32[4,16,8,2048]{3,1,0,2:T(8,128)} %copy_dynamic-update-slice_fusion.1, f32[4,16,2048]{2,1,0:T(8,128)S(1)} %stack.22, f32[4,16,2048]{2,1,0:T(8,128)S(1)} %stack.23), kind=kLoop, calls=%fused_computation.29 | loop fusion | flops 3145728 | bytes 17825792 | tf_op jit(solution)/shard_map/add | solution.py:77
  304.5 50.1 %fusion.2 = f32[4,128,2048]{2,1,0:T(8,128)} fusion(f32[2048,2048]{1,0:T(8,128)} %param.16, f32[4,16,8,2048]{3,1,0,2:T(8,128)S(1)} %get-tuple-element.251, f32[4,16,8,2048]{3,1,0,2:T(8,128)S(1)} %get-tuple-element.250, f32[4,2048]{1,0:T(4,128)S(1)} %get-tuple-element.134), kind=kOutput, calls=%fused_computation.6 | convolution fusion | flops 25771900928 | bytes 29392896 | tf_op jit(solution)/shard_map/kjm,im->kji/dot_general | solution.py:108
  354.7 5.3 %copy.110 = f32[4,128,2048]{1,0,2:T(4,128)} copy(f32[4,128,2048]{2,1,0:T(8,128)} %fusion.2) | data formatting | bytes 8388608 | tf_op jit(solution)/shard_map/kjm,im->kji/dot_general | solution.py:108
  359.9 53.5 %all_to_all.33 = f32[4,128,2048]{1,0,2:T(4,128)} all-to-all(f32[4,128,2048]{1,0,2:T(4,128)} %copy.110), channel_id=1, replica_groups=mesh['lat'=8,'lon'=4] {'lon'}, dimensions={2} | all-to-all | bytes 8388608 | tf_op jit(solution)/shard_map/all_to_all | solution.py:109
  413.5 5.2 %copy.111 = f32[4,4,128,512]{3,2,1,0:T(8,128)} copy(f32[4,4,128,512]{2,1,3,0:T(4,128)} %bitcast.618) | data formatting | bytes 8388608 | tf_op jit(solution)/shard_map/all_to_all | solution.py:109
  (215 shorter events, 19.2 us)
Async XLA Ops:
  1.1 12.8 %collective-permute-start.2 = (f32[16,1,512]{2,1,0:T(1,128)S(1)}, f32[16,1,512]{2,1,0:T(1,128)S(1)}, u32[]{:S(2)}, u32[]{:S(2)}) collective-permute-start(f32[16,1,512]{2,1,0:T(1,128)S(1)} %get-tuple-element.281), channel_id=1, source_target_pairs={{0,4},{4,8},{8,12},{12,16},{16,20},{20,24},{24,28},{1,5},{5,9},{9,... | collective-permute-start | bytes 98312 | tf_op jit(solution)/shard_map/ppermute | solution.py:14
  3.5 10.5 %copy-start.29 = (f32[128,512]{1,0:T(8,128)S(1)}, f32[128,512]{1,0:T(8,128)}, u32[]{:S(2)}) copy-start(f32[128,512]{1,0:T(8,128)} %param.14) | copy-start | bytes 786436
  3.5 10.4 %copy-start.30 = (f32[128,512]{1,0:T(8,128)S(1)}, f32[128,512]{1,0:T(8,128)}, u32[]{:S(2)}) copy-start(f32[128,512]{1,0:T(8,128)} %param.13) | copy-start | bytes 786436
  3.5 10.4 %copy-start.88 = (f32[512]{0:T(512)S(1)}, f32[512]{0:T(512)}, u32[]{:S(2)}) copy-start(f32[512]{0:T(512)} %param.15) | copy-start | bytes 6148
  3.5 10.4 %collective-permute-start.3 = (f32[16,1,512]{2,1,0:T(1,128)S(1)}, f32[16,1,512]{2,1,0:T(1,128)S(1)}, u32[]{:S(2)}, u32[]{:S(2)}) collective-permute-start(f32[16,1,512]{2,1,0:T(1,128)S(1)} %get-tuple-element.282), channel_id=1, source_target_pairs={{4,0},{8,4},{12,8},{16,12},{20,16},{24,20},{28,24},{5,1},{9,5},{13... | collective-permute-start | bytes 98312 | tf_op jit(solution)/shard_map/ppermute | solution.py:15
  7.2 4.9 %collective-permute-start = (f32[16,128,1]{1,0,2:T(8,128)S(1)}, f32[16,128,1]{1,0,2:T(8,128)S(1)}, u32[]{:S(2)}, u32[]{:S(2)}) collective-permute-start(f32[16,128,1]{1,0,2:T(8,128)S(1)} %copy.114), channel_id=1, source_target_pairs={{0,1},{1,2},{2,3},{3,0},{4,5},{5,6},{6,7},{7,4},{8,9},{9,10},{10,1... | collective-permute-start | bytes 24584 | tf_op jit(solution)/shard_map/ppermute | solution.py:14
  9.9 3.7 collective-permute-start.1
  26.0 54.2 %all-to-all-start = ((f32[16,128,512]{2,1,0:T(8,128)}), f32[16,128,512]{2,1,0:T(8,128)}, u32[]{:S(2)}, u32[]{:S(2)}) async-start(f32[16,128,512]{2,1,0:T(8,128)} %fusion.7), calls=%async_computation | async-start | bytes 8388608 | tf_op jit(solution)/shard_map/all_to_all | solution.py:94
  93.2 31.6 %copy-start = (f32[4,16,8,2048]{3,2,1,0:T(8,128)S(1)}, f32[4,16,8,2048]{3,2,1,0:T(8,128)}, u32[]{:S(2)}) copy-start(f32[4,16,8,2048]{3,2,1,0:T(8,128)} %negate_bitcast_fusion) | copy-start | bytes 12582916
  170.8 6.0 %copy-start.7 = (f32[4,16,1,2048]{3,2,1,0:T(1,128)S(1)}, f32[4,16,1,2048]{3,2,1,0:T(1,128)}, u32[]{:S(2)}) copy-start(f32[4,16,1,2048]{3,2,1,0:T(1,128)} %copy-done.6) | copy-start | bytes 1572868
  170.8 6.0 %copy-start.26 = (f32[4,16,1,2048]{3,2,1,0:T(1,128)S(1)}, f32[4,16,1,2048]{3,2,1,0:T(1,128)}, u32[]{:S(2)}) copy-start(f32[4,16,1,2048]{3,2,1,0:T(1,128)} %copy-done.25) | copy-start | bytes 1572868
  170.8 6.0 %copy-start.28 = (f32[4,16,1,2048]{3,2,1,0:T(1,128)S(1)}, f32[4,16,1,2048]{3,2,1,0:T(1,128)}, u32[]{:S(2)}) copy-start(f32[4,16,1,2048]{3,2,1,0:T(1,128)} %copy-done.27) | copy-start | bytes 1572868
  182.8 4.5 %copy-start.73 = (f32[4,1,2048]{2,1,0:T(1,128)S(1)}, f32[4,1,2048]{2,1,0:T(1,128)}, u32[]{:S(2)}) copy-start(f32[4,1,2048]{2,1,0:T(1,128)} %get-tuple-element.194) | copy-start | bytes 98308
  182.8 4.5 %copy-start.74 = (f32[4,1,2048]{2,1,0:T(1,128)S(1)}, f32[4,1,2048]{2,1,0:T(1,128)}, u32[]{:S(2)}) copy-start(f32[4,1,2048]{2,1,0:T(1,128)} %get-tuple-element.195) | copy-start | bytes 98308
  182.8 4.5 %copy-start.75 = (f32[4,1,2048]{2,1,0:T(1,128)S(1)}, f32[4,1,2048]{2,1,0:T(1,128)}, u32[]{:S(2)}) copy-start(f32[4,1,2048]{2,1,0:T(1,128)} %get-tuple-element.196) | copy-start | bytes 98308
  210.0 16.9 %copy-start.1 = (f32[4,16,8,2048]{3,2,1,0:T(8,128)S(1)}, f32[4,16,8,2048]{3,2,1,0:T(8,128)}, u32[]{:S(2)}) copy-start(f32[4,16,8,2048]{3,2,1,0:T(8,128)} %get-tuple-element.266) | copy-start | bytes 12582916
  226.9 10.7 %copy-start.4 = (f32[4,16,1,2048]{3,2,1,0:T(1,128)}, f32[4,16,1,2048]{3,2,1,0:T(1,128)S(1)}, u32[]{:S(2)}) copy-start(f32[4,16,1,2048]{3,2,1,0:T(1,128)S(1)} %get-tuple-element.258) | copy-start | bytes 1572868
  230.0 7.7 %copy-start.2 = (f32[4,16,1,2048]{3,2,1,0:T(1,128)}, f32[4,16,1,2048]{3,2,1,0:T(1,128)S(1)}, u32[]{:S(2)}) copy-start(f32[4,16,1,2048]{3,2,1,0:T(1,128)S(1)} %get-tuple-element.294) | copy-start | bytes 1572868
  230.0 7.7 %copy-start.5 = (f32[4,16,1,2048]{3,2,1,0:T(1,128)}, f32[4,16,1,2048]{3,2,1,0:T(1,128)S(1)}, u32[]{:S(2)}) copy-start(f32[4,16,1,2048]{3,2,1,0:T(1,128)S(1)} %get-tuple-element.296) | copy-start | bytes 1572868
  283.6 5.0 %copy-start.20 = (f32[4,16,1,2048]{3,1,0,2:T(8,128)S(1)}, f32[4,16,1,2048]{3,1,0,2:T(8,128)}, u32[]{:S(2)}) copy-start(f32[4,16,1,2048]{3,1,0,2:T(8,128)} %get-tuple-element.191) | copy-start | bytes 1572868
  283.6 5.9 %copy-start.3 = (f32[4,16,1,2048]{3,2,1,0:T(1,128)S(1)}, f32[4,16,1,2048]{3,2,1,0:T(1,128)}, u32[]{:S(2)}) copy-start(f32[4,16,1,2048]{3,2,1,0:T(1,128)} %copy-done.2) | copy-start | bytes 1572868
  283.6 5.9 %copy-start.18 = (f32[4,16,1,2048]{3,1,0,2:T(8,128)S(1)}, f32[4,16,1,2048]{3,1,0,2:T(8,128)}, u32[]{:S(2)}) copy-start(f32[4,16,1,2048]{3,1,0,2:T(8,128)} %get-tuple-element.192) | copy-start | bytes 1572868
  283.6 5.9 %copy-start.19 = (f32[4,16,1,2048]{3,1,0,2:T(8,128)S(1)}, f32[4,16,1,2048]{3,1,0,2:T(8,128)}, u32[]{:S(2)}) copy-start(f32[4,16,1,2048]{3,1,0,2:T(8,128)} %get-tuple-element.256) | copy-start | bytes 1572868
  286.7 5.9 %copy-start.17 = (f32[4,16,1,2048]{3,1,0,2:T(8,128)S(1)}, f32[4,16,1,2048]{3,1,0,2:T(8,128)}, u32[]{:S(2)}) copy-start(f32[4,16,1,2048]{3,1,0,2:T(8,128)} %get-tuple-element.193) | copy-start | bytes 1572868
  292.6 5.6 %copy-start.31 = (f32[4,1,2048]{2,1,0:T(1,128)S(1)}, f32[4,1,2048]{2,1,0:T(1,128)}, u32[]{:S(2)}) copy-start(f32[4,1,2048]{2,1,0:T(1,128)} %get-tuple-element.234) | copy-start | bytes 98308
  292.6 5.6 %copy-start.32 = (f32[4,1,2048]{2,1,0:T(1,128)S(1)}, f32[4,1,2048]{2,1,0:T(1,128)}, u32[]{:S(2)}) copy-start(f32[4,1,2048]{2,1,0:T(1,128)} %get-tuple-element.235) | copy-start | bytes 98308
  292.6 5.6 %copy-start.33 = (f32[4,1,2048]{2,1,0:T(1,128)S(1)}, f32[4,1,2048]{2,1,0:T(1,128)}, u32[]{:S(2)}) copy-start(f32[4,1,2048]{2,1,0:T(1,128)} %get-tuple-element.236) | copy-start | bytes 98308
  292.6 5.6 %copy-start.34 = (f32[4,1,2048]{2,1,0:T(1,128)S(1)}, f32[4,1,2048]{2,1,0:T(1,128)}, u32[]{:S(2)}) copy-start(f32[4,1,2048]{2,1,0:T(1,128)} %get-tuple-element.237) | copy-start | bytes 98308
  292.6 5.6 %copy-start.35 = (f32[4,1,2048]{2,1,0:T(1,128)S(1)}, f32[4,1,2048]{2,1,0:T(1,128)}, u32[]{:S(2)}) copy-start(f32[4,1,2048]{2,1,0:T(1,128)} %get-tuple-element.238) | copy-start | bytes 98308
  292.6 5.6 %copy-start.36 = (f32[4,1,2048]{2,1,0:T(1,128)S(1)}, f32[4,1,2048]{2,1,0:T(1,128)}, u32[]{:S(2)}) copy-start(f32[4,1,2048]{2,1,0:T(1,128)} %get-tuple-element.239) | copy-start | bytes 98308
  292.6 5.6 %copy-start.37 = (f32[4,1,2048]{2,1,0:T(1,128)S(1)}, f32[4,1,2048]{2,1,0:T(1,128)}, u32[]{:S(2)}) copy-start(f32[4,1,2048]{2,1,0:T(1,128)} %get-tuple-element.240) | copy-start | bytes 98308
  292.6 5.6 %copy-start.38 = (f32[4,1,2048]{2,1,0:T(1,128)S(1)}, f32[4,1,2048]{2,1,0:T(1,128)}, u32[]{:S(2)}) copy-start(f32[4,1,2048]{2,1,0:T(1,128)} %get-tuple-element.241) | copy-start | bytes 98308
  292.6 5.6 %copy-start.39 = (f32[4,1,2048]{2,1,0:T(1,128)S(1)}, f32[4,1,2048]{2,1,0:T(1,128)}, u32[]{:S(2)}) copy-start(f32[4,1,2048]{2,1,0:T(1,128)} %get-tuple-element.242) | copy-start | bytes 98308
  292.7 5.6 %copy-start.40 = (f32[4,1,2048]{2,1,0:T(1,128)S(1)}, f32[4,1,2048]{2,1,0:T(1,128)}, u32[]{:S(2)}) copy-start(f32[4,1,2048]{2,1,0:T(1,128)} %get-tuple-element.243) | copy-start | bytes 98308
  292.7 5.6 %copy-start.41 = (f32[4,1,2048]{2,1,0:T(1,128)S(1)}, f32[4,1,2048]{2,1,0:T(1,128)}, u32[]{:S(2)}) copy-start(f32[4,1,2048]{2,1,0:T(1,128)} %get-tuple-element.244) | copy-start | bytes 98308
  292.7 5.6 %copy-start.42 = (f32[4,1,2048]{2,1,0:T(1,128)S(1)}, f32[4,1,2048]{2,1,0:T(1,128)}, u32[]{:S(2)}) copy-start(f32[4,1,2048]{2,1,0:T(1,128)} %get-tuple-element.245) | copy-start | bytes 98308
  292.7 5.6 %copy-start.43 = (f32[4,1,2048]{2,1,0:T(1,128)S(1)}, f32[4,1,2048]{2,1,0:T(1,128)}, u32[]{:S(2)}) copy-start(f32[4,1,2048]{2,1,0:T(1,128)} %get-tuple-element.246) | copy-start | bytes 98308
  292.7 5.6 %copy-start.44 = (f32[4,1,2048]{2,1,0:T(1,128)S(1)}, f32[4,1,2048]{2,1,0:T(1,128)}, u32[]{:S(2)}) copy-start(f32[4,1,2048]{2,1,0:T(1,128)} %get-tuple-element.323) | copy-start | bytes 98308
  292.7 6.4 %copy-start.45 = (f32[4,1,2048]{2,1,0:T(1,128)S(1)}, f32[4,1,2048]{2,1,0:T(1,128)}, u32[]{:S(2)}) copy-start(f32[4,1,2048]{2,1,0:T(1,128)} %get-tuple-element.175) | copy-start | bytes 98308
  292.7 6.4 %copy-start.46 = (f32[4,1,2048]{2,1,0:T(1,128)S(1)}, f32[4,1,2048]{2,1,0:T(1,128)}, u32[]{:S(2)}) copy-start(f32[4,1,2048]{2,1,0:T(1,128)} %get-tuple-element.176) | copy-start | bytes 98308
  292.7 6.4 %copy-start.47 = (f32[4,1,2048]{2,1,0:T(1,128)S(1)}, f32[4,1,2048]{2,1,0:T(1,128)}, u32[]{:S(2)}) copy-start(f32[4,1,2048]{2,1,0:T(1,128)} %get-tuple-element.177) | copy-start | bytes 98308
  292.7 6.4 %copy-start.48 = (f32[4,1,2048]{2,1,0:T(1,128)S(1)}, f32[4,1,2048]{2,1,0:T(1,128)}, u32[]{:S(2)}) copy-start(f32[4,1,2048]{2,1,0:T(1,128)} %get-tuple-element.178) | copy-start | bytes 98308
  292.7 6.4 %copy-start.49 = (f32[4,1,2048]{2,1,0:T(1,128)S(1)}, f32[4,1,2048]{2,1,0:T(1,128)}, u32[]{:S(2)}) copy-start(f32[4,1,2048]{2,1,0:T(1,128)} %get-tuple-element.179) | copy-start | bytes 98308
  292.8 6.4 %copy-start.50 = (f32[4,1,2048]{2,1,0:T(1,128)S(1)}, f32[4,1,2048]{2,1,0:T(1,128)}, u32[]{:S(2)}) copy-start(f32[4,1,2048]{2,1,0:T(1,128)} %get-tuple-element.180) | copy-start | bytes 98308
  292.8 6.4 %copy-start.51 = (f32[4,1,2048]{2,1,0:T(1,128)S(1)}, f32[4,1,2048]{2,1,0:T(1,128)}, u32[]{:S(2)}) copy-start(f32[4,1,2048]{2,1,0:T(1,128)} %get-tuple-element.181) | copy-start | bytes 98308
  292.8 6.4 %copy-start.52 = (f32[4,1,2048]{2,1,0:T(1,128)S(1)}, f32[4,1,2048]{2,1,0:T(1,128)}, u32[]{:S(2)}) copy-start(f32[4,1,2048]{2,1,0:T(1,128)} %get-tuple-element.182) | copy-start | bytes 98308
  292.8 6.4 %copy-start.53 = (f32[4,1,2048]{2,1,0:T(1,128)S(1)}, f32[4,1,2048]{2,1,0:T(1,128)}, u32[]{:S(2)}) copy-start(f32[4,1,2048]{2,1,0:T(1,128)} %get-tuple-element.183) | copy-start | bytes 98308
  292.8 6.4 %copy-start.54 = (f32[4,1,2048]{2,1,0:T(1,128)S(1)}, f32[4,1,2048]{2,1,0:T(1,128)}, u32[]{:S(2)}) copy-start(f32[4,1,2048]{2,1,0:T(1,128)} %get-tuple-element.184) | copy-start | bytes 98308
  (46 other events, 188.5 us)
where the time goes:
time: 423 us; the launch traced here: 419 us
  blocking collectives  118 us (28%)
  other arithmetic  94.3 us (22%)
  matrix products  81.7 us (19%)
  local copies, waits for them, and re-layouts  63.8 us (15%)
  waiting for transfers between devices  46.3 us (11%)
  starting transfers between devices  12.5 us (3%)
    all_gather x4, blocking collectives, prefix(): gathered = jax.tree.map(lambda a: lax.all_gather(a, axis), part)  64.8 us
    all_to_all x1, blocking collectives, per_device(): lax.all_to_all(on_grid, 'lon', split_axis=2, concat_axis=0, tiled=True)  53.5 us
    dot_general x1, matrix products, per_device(): jnp.einsum('kjm,im->kji', modal, eigen_basis, precision=lax.Precision.HIG...  50.1 us
    all_to_all x1, waiting for transfers between devices, per_device(): lax.all_to_all(weighted, 'lon', split_axis=0, concat_axis=2, tiled=True)  44 us
    dot_general x1, matrix products, per_device(): jnp.einsum('kji,im->kjm', lax.all_to_all(weighted, 'lon', split_axis=0, c...  31.6 us
    unnamed x11, other arithmetic  26.9 us
    slice x2, local copies, waits for them, and re-layouts, band_recurrence(): source_blocks[:, :, position, :]  23.2 us
    reshape x1, other arithmetic, band_recurrence(): source_blocks = source.reshape(modes, groups, block, columns)  15 us
  transfers between devices with their start and end apart: 5, of which 3 were waited for; matrix products, arithmetic and copies ran while one was open for 2% of the time, Pallas kernels for 0%

commit v1 on v0

v1 whole, which is shorter than its diff:
```python
import functools

import jax
import jax.numpy as jnp
from jax import lax
from jax.experimental import pallas as pl
from jax.experimental.pallas import tpu as pltpu
from jax.sharding import PartitionSpec as P


F32 = jnp.float32
BF16 = jnp.bfloat16


def params(mib, **kw):
    return pltpu.CompilerParams(vmem_limit_bytes=mib * 1024 * 1024, **kw)


VMEM = pl.BlockSpec(memory_space=pltpu.VMEM)


def near(*arrays):
    return [pltpu.with_memory_space_constraint(a, pltpu.VMEM) for a in arrays]


def far(*arrays):
    return [pltpu.with_memory_space_constraint(a, pltpu.HBM) for a in arrays]


def exchange(a, axis, x):
    count = lax.axis_size(axis)
    return lax.ppermute(a, axis, [(i, i ^ x) for i in range(count)])


def groups_of(local):
    return 2 if local % 2 == 0 else 1


def farthest(count):
    return sorted(range(1, count), key=lambda x: -bin(x).count("1"))


def split(v):
    hi = v.astype(BF16)
    return hi, (v - hi.astype(F32)).astype(BF16)


def stencil_body(count, me_ref, *refs):
    f_refs = refs[:count]
    west, east, south, north = (refs[count * (1 + i) : count * (2 + i)] for i in range(4))
    mlon_ref, mlat_ref, w_ref = refs[5 * count : 5 * count + 3]
    outs = refs[5 * count + 3 :]
    rows, cols = mlon_ref.shape
    lane = lax.broadcasted_iota(jnp.int32, (8, cols), 1)
    row = lax.broadcasted_iota(jnp.int32, (8, cols), 0)
    weight = jnp.broadcast_to(w_ref[...], (8, cols))
    i = pl.program_id(0)
    for x in range(count):
        f_ref = f_refs[x]
        for t in range(rows // 8):
            at = pl.ds(8 * t, 8)
            f = f_ref[0, 0, at]
            below = f_ref[0, 0, 8 * t - 1 : 8 * t] if t else south[x][0, 0]
            above = f_ref[0, 0, 8 * t + 8 : 8 * t + 9] if 8 * t + 8 < rows else north[x][0, 0]
            w = jnp.where(lane == 0, west[x][0, 0, at], pltpu.roll(f, 1, 1))
            e = jnp.where(lane == cols - 1, east[x][0, 0, at], pltpu.roll(f, cols - 1, 1))
            s = jnp.where(row == 0, below, pltpu.roll(f, 1, 0))
            n = jnp.where(row == 7, above, pltpu.roll(f, 7, 0))
            outs[x][i, at] = (f + mlon_ref[at] * (w + e) + mlat_ref[at] * (s + n)) * weight


def stencil(me, forcing, halos, mlon, mlat, weights, count, first, size):
    modes, rows, cols = forcing.shape
    local = modes // count
    f4 = forcing.reshape(count, local, rows, cols)
    h4 = [h.reshape(count, local, *h.shape[1:]) for h in halos]

    def spec(shape, x):
        return pl.BlockSpec(
            (1, 1) + shape, lambda i, m, x=x: (m[0] ^ x, first + i) + (0,) * len(shape)
        )

    args, specs = [], []
    for a in [f4] + h4:
        for x in range(count):
            args.append(far(a)[0] if a is f4 else a)
            specs.append(spec(a.shape[2:], x))
    whole = pl.BlockSpec((rows, cols), lambda i, m: (0, 0))
    return pl.pallas_call(
        functools.partial(stencil_body, count),
        grid_spec=pltpu.PrefetchScalarGridSpec(
            num_scalar_prefetch=1,
            grid=(size,),
            in_specs=specs + [whole, whole, pl.BlockSpec((1, cols), lambda i, m: (0, 0))],
            out_specs=[VMEM] * count,
        ),
        out_shape=[pltpu.VMEM((size, rows, cols), F32)] * count,
        compiler_params=params(12),
        cost_estimate=pl.CostEstimate(
            flops=12 * size * count * rows * cols,
            bytes_accessed=8 * size * count * rows * cols,
            transcendentals=0,
        ),
        name="stencil",
    )(me, *args, mlon, mlat, weights)


def basis_body(e_ref, hi_ref, lo_ref):
    t = e_ref.shape[0]
    at = pl.ds(pl.multiple_of(pl.program_id(0) * t, t), t)
    hi_ref[at], lo_ref[at] = split(e_ref[...])


def basis_parts(basis):
    n, m = basis.shape
    t = min(256, n)
    spec = pl.BlockSpec((t, m), lambda i: (i, 0))
    return pl.pallas_call(
        basis_body,
        grid=(n // t,),
        in_specs=[spec],
        out_specs=[VMEM, VMEM],
        out_shape=[pltpu.VMEM((n, m), BF16)] * 2,
        compiler_params=params(8),
        cost_estimate=pl.CostEstimate(flops=4 * n * m, bytes_accessed=8 * n * m, transcendentals=0),
        name="basis",
    )(*far(basis))


def block_solve(x, a, carry, up):
    sub = lax.broadcasted_iota(jnp.int32, x.shape, 0)
    edge = sub == (7 if up else 0)
    one, two = (7, 6) if up else (1, 2)
    x = x + jnp.where(edge, a, 0.0) * carry
    a = jnp.where(edge, 0.0, a)
    x = x + a * pltpu.roll(x, one, 0)
    a = a * pltpu.roll(a, one, 0)
    x = x + a * pltpu.roll(x, two, 0)
    a = a * pltpu.roll(a, two, 0)
    x = x + a * pltpu.roll(x, 4, 0)
    return x


def last_row(x, up):
    r = 0 if up else 7
    return jnp.broadcast_to(x[r : r + 1], x.shape)


def block_product(a, up):
    sub = lax.broadcasted_iota(jnp.int32, a.shape, 0)
    for d in (1, 2, 4):
        keep = sub < 8 - d if up else sub >= d
        a = a * jnp.where(keep, pltpu.roll(a, 8 - d if up else d, 0), 1.0)
    return a


def factors_body(wide, l_ref, p_ref, u_ref, h_ref, r_ref, c_ref, y_ref):
    _, rows, m = l_ref.shape
    blocks = rows // 8
    k = pl.program_id(0)

    def columns(n, _):
        here = pl.ds(pl.multiple_of(n * wide, wide), wide)
        carry = jnp.ones((8, wide), F32)
        for t in range(blocks):
            at = pl.ds(8 * t, 8)
            scale = block_product(-l_ref[0, at, here], False) * carry
            carry = last_row(scale, False)
            y_ref[at] = p_ref[0, at, here] * scale
        end = carry
        carry_h, carry_r = jnp.zeros((8, wide), F32), jnp.ones((8, wide), F32)
        for t in reversed(range(blocks)):
            at = pl.ds(8 * t, 8)
            f = -(u_ref[0, at, here] * p_ref[0, at, here])
            h = block_solve(y_ref[at], f, carry_h, True)
            r = block_product(f, True) * carry_r
            h_ref[k, at, here] = h
            r_ref[k, at, here] = r
            carry_h, carry_r = last_row(h, True), last_row(r, True)
        sub = lax.broadcasted_iota(jnp.int32, (8, wide), 0)
        c_ref[k, :, here] = jnp.where(sub == 0, end, jnp.where(sub == 1, carry_h, carry_r))[:4]
        return 0

    lax.fori_loop(0, m // wide, columns, 0)


def factors(lower, pinv, upper):
    modes, rows, m = lower.shape
    t = min(512, m)
    spec = pl.BlockSpec((1, rows, m), lambda k: (k, 0, 0))
    return pl.pallas_call(
        functools.partial(factors_body, t),
        grid=(modes,),
        in_specs=[spec] * 3,
        out_specs=[VMEM] * 3,
        out_shape=[pltpu.VMEM((modes, rows, m), F32)] * 2 + [pltpu.VMEM((modes, 4, m), F32)],
        scratch_shapes=[pltpu.VMEM((rows, t), F32)],
        compiler_params=params(8),
        cost_estimate=pl.CostEstimate(
            flops=60 * modes * rows * m, bytes_accessed=20 * modes * rows * m, transcendentals=0
        ),
        name="factors",
    )(*far(lower, pinv, upper))


def forward_body(count, me_ref, *refs):
    x_refs = refs[:count]
    hi_ref, lo_ref, l_ref, p_ref, u_ref, g_ref, s_ref, x_all, spec = refs[count:]
    size, rows, cols = x_refs[0].shape
    tall = size * rows
    wide = spec.shape[1]
    here = pl.ds(pl.multiple_of(pl.program_id(0) * wide, wide), wide)

    @pl.when(pl.program_id(0) == 0)
    def _():
        me = me_ref[0]
        for x in range(count):
            at = pl.ds(pl.multiple_of((me ^ x) * cols, 128), cols)
            hi, lo = split(x_refs[x][...].reshape(tall, cols))
            x_all[0:tall, at] = hi
            x_all[tall : 2 * tall, at] = lo

    both = jnp.dot(x_all[...], hi_ref[:, here], preferred_element_type=F32)
    spec[...] = (
        both[:tall]
        + both[tall:]
        + jnp.dot(x_all[0:tall, :], lo_ref[:, here], preferred_element_type=F32)
    )
    blocks = rows // 8
    carry = [jnp.zeros((8, wide), F32)] * size
    for t in range(blocks):
        for k in range(size):
            at = pl.ds(8 * t, 8)
            into = pl.ds(k * rows + 8 * t, 8)
            s = block_solve(spec[into], -l_ref[k, at], carry[k], False)
            carry[k] = last_row(s, False)
            spec[into] = p_ref[k, at] * s
    ends = carry
    carry = [jnp.zeros((8, wide), F32)] * size
    for t in reversed(range(blocks)):
        for k in range(size):
            at = pl.ds(8 * t, 8)
            f = -(u_ref[k, at] * p_ref[k, at])
            g = block_solve(spec[pl.ds(k * rows + 8 * t, 8)], f, carry[k], True)
            g_ref[k, at, here] = g
            carry[k] = last_row(g, True)
    for k in range(size):
        s_ref[2 * k : 2 * k + 1, here] = ends[k][0:1]
        s_ref[2 * k + 1 : 2 * k + 2, here] = carry[k][0:1]


def forward(me, xs, hi, lo, lower, pinv, upper, part):
    count = len(xs)
    size, rows, _ = xs[0].shape
    n, m = hi.shape
    t = min(512, m)
    fac = pl.BlockSpec((size, rows, t), lambda i, me: (part, 0, i))
    return pl.pallas_call(
        functools.partial(forward_body, count),
        grid_spec=pltpu.PrefetchScalarGridSpec(
            num_scalar_prefetch=1,
            grid=(m // t,),
            in_specs=[VMEM] * (count + 2) + [fac, fac, fac],
            out_specs=[VMEM, VMEM],
            scratch_shapes=[
                pltpu.VMEM((2 * size * rows, n), BF16),
                pltpu.VMEM((size * rows, t), F32),
            ],
        ),
        out_shape=[pltpu.VMEM((size, rows, m), F32), pltpu.VMEM((2 * size, m), F32)],
        compiler_params=params(16),
        cost_estimate=pl.CostEstimate(
            flops=6 * size * rows * n * m, bytes_accessed=4 * n * m, transcendentals=0
        ),
        name="forward",
    )(me, *near(*xs, hi, lo), *far(lower, pinv, upper))


def join_coefs_body(me_ref, own_ref, other_ref, out_ref):
    low = (me_ref[1] & 1) == 0
    for k in range(own_ref.shape[0]):
        a, b = own_ref[k], other_ref[k]
        lo, hi = jnp.where(low, a, b), jnp.where(low, b, a)
        p, h, r = lo[0:1], lo[1:2], lo[2:3]
        out_ref[k, 0:1] = hi[0:1] * p
        out_ref[k, 1:2] = h + r * (hi[1:2] * p)
        out_ref[k, 2:3] = r * hi[2:3]
        out_ref[k, 3:4] = r


def join_sums_body(first, me_ref, own_ref, other_ref, c_own_ref, c_other_ref, out_ref):
    low = (me_ref[1] & 1) == 0
    for k in range(own_ref.shape[0] // 2):
        a, b = own_ref[2 * k : 2 * k + 2], other_ref[2 * k : 2 * k + 2]
        lo, hi = jnp.where(low, a, b), jnp.where(low, b, a)
        c, d = c_own_ref[first + k], c_other_ref[first + k]
        r = jnp.where(low, c, d)[2:3]
        d = jnp.where(low, d, c)
        out_ref[2 * k : 2 * k + 1] = hi[0:1] + d[0:1] * lo[0:1]
        out_ref[2 * k + 1 : 2 * k + 2] = lo[1:2] + r * (hi[1:2] + d[1:2] * lo[0:1])


def small_call(body, me, args, shape):
    return pl.pallas_call(
        body,
        grid_spec=pltpu.PrefetchScalarGridSpec(
            num_scalar_prefetch=1, grid=(1,), in_specs=[VMEM] * len(args), out_specs=VMEM
        ),
        out_shape=pltpu.VMEM(shape, F32),
        compiler_params=params(4),
        cost_estimate=pl.CostEstimate(flops=1 << 20, bytes_accessed=1 << 18, transcendentals=0),
    )(me, *near(*args))


def spread(a, axis):
    return [a] + [exchange(a, axis, x) for x in range(2, lax.axis_size(axis), 2)]


def modal_body(chips, wide, first, me_ref, *refs):
    s_refs = refs[:chips]
    c_refs = refs[chips : 2 * chips]
    s_own, s_oth, c_own, c_oth, g_ref, h_ref, r_ref, out_ref = refs[2 * chips : 2 * chips + 8]
    s_all, c_all, enter, arrive = refs[2 * chips + 8 :]
    size, rows, _ = g_ref.shape
    tall = size * rows
    me = lax.shift_right_logical(me_ref[1], 1)
    low = (me_ref[1] & 1) == 0
    here = pl.ds(pl.multiple_of(pl.program_id(0) * wide, wide), wide)
    for b in range(chips):
        s_all[b] = s_refs[b][:, here]
        for k in range(size):
            c_all[b, k] = c_refs[b][first + k, :, here]
    for k in range(size):
        e = jnp.zeros((1, wide), F32)
        for b in range(chips):
            enter[b] = e
            if b + 1 < chips:
                src = me ^ b
                e = s_all[src, 2 * k : 2 * k + 1] + c_all[src, k, 0:1] * e
        a = jnp.zeros((1, wide), F32)
        for b in reversed(range(chips)):
            arrive[b] = a
            if b:
                src = me ^ b
                a = (
                    s_all[src, 2 * k + 1 : 2 * k + 2]
                    + c_all[src, k, 1:2] * enter[b]
                    + c_all[src, k, 2:3] * a
                )
        e, a = enter[me], arrive[me]
        own, oth = s_own[2 * k : 2 * k + 2, here], s_oth[2 * k : 2 * k + 2, here]
        c, d = c_own[first + k, :, here], c_oth[first + k, :, here]
        beyond = oth[1:2] + d[1:2] * (own[0:1] + c[0:1] * e) + d[2:3] * a
        before = oth[0:1] + d[0:1] * e
        e, a = jnp.where(low, e, before), jnp.where(low, beyond, a)
        modal = g_ref[k, :, here] + h_ref[first + k, :, here] * e + r_ref[first + k, :, here] * a
        hi, lo = split(modal)
        out_ref[k * rows : (k + 1) * rows, here] = hi
        out_ref[tall + k * rows : tall + (k + 1) * rows, here] = lo


def modal_parts(me, summaries, coefs, own, g, h, r, part):
    chips = len(summaries)
    size, rows, m = g.shape
    t = min(512, m)
    return pl.pallas_call(
        functools.partial(modal_body, chips, t, part * size),
        grid_spec=pltpu.PrefetchScalarGridSpec(
            num_scalar_prefetch=1,
            grid=(m // t,),
            in_specs=[VMEM] * (2 * chips + 7),
            out_specs=VMEM,
            scratch_shapes=[
                pltpu.VMEM((chips, 2 * size, t), F32),
                pltpu.VMEM((chips, size, 4, t), F32),
                pltpu.VMEM((chips, 1, t), F32),
                pltpu.VMEM((chips, 1, t), F32),
            ],
        ),
        out_shape=pltpu.VMEM((2 * size * rows, m), BF16),
        compiler_params=params(6),
        cost_estimate=pl.CostEstimate(
            flops=10 * size * rows * m, bytes_accessed=16 * size * rows * m, transcendentals=0
        ),
        name="modal",
    )(me, *near(*summaries, *coefs, *own, g, h, r))


def back_body(x, t, me_ref, m_ref, hi_ref, lo_ref, out_ref):
    size, rows, sector = out_ref.shape
    tall = size * rows
    i = pl.program_id(0)
    dims = (((1,), (1,)), ((), ()))
    at = pl.ds(pl.multiple_of((me_ref[0] ^ x) * sector + i * t, t), t)
    both = lax.dot_general(m_ref[...], hi_ref[at, :], dims, preferred_element_type=F32)
    third = lax.dot_general(m_ref[0:tall, :], lo_ref[at, :], dims, preferred_element_type=F32)
    out_ref[:, :, pl.ds(pl.multiple_of(i * t, t), t)] = (
        both[:tall] + both[tall:] + third
    ).reshape(size, rows, t)


def back(me, parts, hi, lo, x, size, rows, sector):
    _, m = hi.shape
    t = min(256, sector)
    return pl.pallas_call(
        functools.partial(back_body, x, t),
        grid_spec=pltpu.PrefetchScalarGridSpec(
            num_scalar_prefetch=1,
            grid=(sector // t,),
            in_specs=[VMEM] * 3,
            out_specs=VMEM,
        ),
        out_shape=pltpu.VMEM((size, rows, sector), F32),
        compiler_params=params(6),
        cost_estimate=pl.CostEstimate(
            flops=6 * size * rows * sector * m, bytes_accessed=4 * sector * m, transcendentals=0
        ),
        name="back",
    )(me, *near(parts, hi, lo))


def place_body(count, local, first, me_ref, *refs):
    pieces, (out_ref, sems) = refs[:count], refs[-2:]
    size = pieces[0].shape[0]
    copies = [
        pltpu.make_async_copy(
            pieces[x],
            out_ref.at[pl.ds((me_ref[0] ^ x) * local + first, size)],
            sems.at[x],
        )
        for x in range(count)
    ]
    for c in copies:
        c.start()
    for c in copies:
        c.wait()


def place(me, pieces, out, shape, local, first):
    count = len(pieces)
    extra = [] if out is None else far(out)
    return pl.pallas_call(
        functools.partial(place_body, count, local, first),
        grid_spec=pltpu.PrefetchScalarGridSpec(
            num_scalar_prefetch=1,
            grid=(1,),
            in_specs=[VMEM] * count + [pl.BlockSpec(memory_space=pl.ANY)] * len(extra),
            out_specs=pl.BlockSpec(memory_space=pl.ANY),
            scratch_shapes=[pltpu.SemaphoreType.DMA((count,))],
        ),
        out_shape=pltpu.HBM(shape, F32),
        input_output_aliases={count + 1: 0} if extra else {},
        compiler_params=params(2),
        cost_estimate=pl.CostEstimate(
            flops=0, bytes_accessed=8 * pieces[0].size * count, transcendentals=0
        ),
        name="place",
    )(me, *near(*pieces), *extra)


def per_device(forcing, mlon, mlat, weights, basis, lower, pinv, upper):
    count = lax.axis_size("lon")
    bands = lax.axis_size("lat")
    lon, lat = lax.axis_index("lon"), lax.axis_index("lat")
    me = jnp.stack([lon, lat]).astype(jnp.int32)
    modes, rows, sector = forcing.shape
    local = modes // count
    groups = groups_of(local)
    size = local // groups

    ring = [(i, (i + 1) % count) for i in range(count)]
    line = [(i, i + 1) for i in range(bands - 1)]
    south = lax.ppermute(forcing[:, rows - 1 :, :], "lat", line)
    north = lax.ppermute(forcing[:, :1, :], "lat", [(j, i) for i, j in line])
    west = lax.ppermute(forcing[:, :, sector - 1 :], "lon", ring)
    east = lax.ppermute(forcing[:, :, :1], "lon", [(j, i) for i, j in ring])
    halos = (west, east, south, north)

    order = farthest(count)
    sources = []
    for part in range(groups):
        mine = stencil(
            me, forcing, halos, mlon, mlat, weights.reshape(1, -1), count, part * size, size
        )
        me, mine = lax.optimization_barrier((me, mine))
        got = {x: exchange(mine[x], "lon", x) for x in order}
        sources.append([mine[0]] + [got[x] for x in range(1, count)])
    me, basis, lower = lax.optimization_barrier((me, basis, lower))
    hi, lo = basis_parts(basis)
    h, r, coef = factors(lower, pinv, upper)
    coef_other = exchange(coef, "lat", 1)
    joined = small_call(join_coefs_body, me, (coef, coef_other), coef.shape)
    coefs = spread(joined, "lat")

    out = None
    for part in range(groups):
        g, summary = forward(me, sources[part], hi, lo, lower, pinv, upper, part)
        other = exchange(summary, "lat", 1)
        joined = small_call(
            functools.partial(join_sums_body, part * size),
            me,
            (summary, other, coef, coef_other),
            summary.shape,
        )
        summaries = spread(joined, "lat")
        own = (summary, other, coef, coef_other)
        parts = modal_parts(me, summaries, coefs, own, g, h, r, part)
        pieces = {}
        for x in order + [0]:
            pieces[x] = back(me, parts, hi, lo, x, size, rows, sector)
        me, pieces[0] = lax.optimization_barrier((me, pieces[0]))
        pieces = [exchange(pieces[x], "lon", x) if x else pieces[x] for x in range(count)]
        out = place(me, pieces, out, (modes, rows, sector), local, part * size)
    return out


def solution(mesh):
    placed = (
        P(None, "lat", "lon"),
        P("lat", "lon"),
        P("lat", "lon"),
        P("lon"),
        P(),
        P("lon", "lat", None),
        P("lon", "lat", None),
        P("lon", "lat", None),
    )

    return jax.shard_map(
        per_device, mesh=mesh, in_specs=placed, out_specs=P(None, "lat", "lon"), check_vma=False
    )
```

time: 423 us -> 163 us (0.39)
  blocking collectives: 118 us -> 0 us
  other arithmetic: 94.3 us -> 0.07 us
  matrix products: 81.7 us -> 0 us
  Pallas kernels: 0 us -> 78.6 us
  local copies, waits for them, and re-layouts: 63.8 us -> 4.41 us
  starting transfers between devices: 12.5 us -> 32.8 us
    dot_general x2 -> x0, matrix products: 81.7 us -> none  [the longest x1 50.1 us: per_device(): jnp.einsum('kjm,im->kji', modal, eigen_basis, precision=lax.Precision.HIG...]
    pallas_call x0 -> x21, Pallas kernels: none -> 78.6 us  [the longest x2 24.8 us: forward(): pl.pallas_call(functools.partial(forward_body, count), grid_spec=pltpu.Pr...]
    all_gather x4 -> x0, blocking collectives: 64.8 us -> none  [prefix(): gathered = jax.tree.map(lambda a: lax.all_gather(a, axis), part)]
    all_to_all x1 -> x0, blocking collectives: 53.5 us -> none  [per_device(): lax.all_to_all(on_grid, 'lon', split_axis=2, concat_axis=0, tiled=True)]
    ppermute x4 -> x28, waiting for transfers between devices: 2.31 us -> 46.7 us  [the longest x24 44 us: exchange(): return lax.ppermute(a, axis, [(i, i ^ x) for i in range(count)])]
    all_to_all x1 -> x0, waiting for transfers between devices: 44 us -> none  [per_device(): lax.all_to_all(weighted, 'lon', split_axis=0, concat_axis=2, tiled=True)]
    add x15 -> x0, other arithmetic: 29.2 us -> none  [the longest x2 11.3 us: band_recurrence(): local_shift + local_scale * group_shift]
    unnamed x11 -> x0, other arithmetic: 26.9 us -> none
  transfers between devices with their start and end apart: 5 -> 28, of which waited for: 3 -> 8; matrix products, arithmetic and copies ran while one was open for 2% -> 2% of each run, Pallas kernels for 0% -> 37%
where the time goes in v1:
time: 163 us
  Pallas kernels  78.6 us (48%)
  waiting for transfers between devices  46.7 us (29%)
  starting transfers between devices  32.8 us (20%)
  local copies, waits for them, and re-layouts  4.41 us (3%)
    ppermute x24, waiting for transfers between devices, exchange(): return lax.ppermute(a, axis, [(i, i ^ x) for i in range(count)])  44 us
    pallas_call x2, Pallas kernels, forward(): pl.pallas_call(functools.partial(forward_body, count), grid_spec=pltpu.Pr...  24.8 us
    ppermute x24, starting transfers between devices, exchange(): return lax.ppermute(a, axis, [(i, i ^ x) for i in range(count)])  24.4 us
    pallas_call x8, Pallas kernels, back(): pl.pallas_call(functools.partial(back_body, x, t), grid_spec=pltpu.Prefet...  21 us
    pallas_call x1, Pallas kernels, basis_parts(): pl.pallas_call(basis_body, grid=(n // t,), in_specs=[spec], out_specs=[VM...  8.65 us
    pallas_call x1, Pallas kernels, factors(): pl.pallas_call(functools.partial(factors_body, t), grid=(modes,), in_spec...  8.42 us
    pallas_call x2, Pallas kernels, stencil(): pl.pallas_call(functools.partial(stencil_body, count), grid_spec=pltpu.Pr...  6.68 us
    pallas_call x2, Pallas kernels, place(): pl.pallas_call(functools.partial(place_body, count, local, first), grid_s...  3.78 us
  transfers between devices with their start and end apart: 28, of which 8 were waited for; matrix products, arithmetic and copies ran while one was open for 2% of the time, Pallas kernels for 37%

profile of v1, /device:TPU:0, one launch (start us, length us, event | category | flops | bytes accessed | tf_op | source)
XLA Modules:
  0.0 163.1 jit_solution(9918591404799725495)
XLA Ops:
  0.0 1.1 fusion
  1.1 1.3 collective-permute-start.3
  2.4 3.2 %collective-permute-start.2 = (f32[16,1,512]{2,1,0:T(1,128)S(1)}, f32[16,1,512]{2,1,0:T(1,128)S(1)}, u32[]{:S(2)}, u32[]{:S(2)}) collective-permute-start(f32[16,1,512]{2,1,0:T(1,128)S(1)} %get-tuple-element.74), channel_id=1, source_target_pairs={{0,4},{4,8},{8,12},{12,16},{16,20},{20,24},{24,28},{1,5},{5,9},{9,... | collective-permute-start | bytes 98312 | tf_op jit(solution)/shard_map/ppermute | solution.py:473
  5.6 1.9 %fusion.1 = (f32[16,128,1]{2,1,0:T(8,128)S(1)}, f32[16,128,1]{2,1,0:T(8,128)S(1)}) fusion(f32[16,128,512]{2,1,0:T(8,128)} %param.8), kind=kLoop, calls=%fused_computation.2 | loop fusion | bytes 32768 | tf_op jit(solution)/shard_map/slice | solution.py:476
  7.8 3.0 %collective-permute-start = (f32[16,128,1]{1,0,2:T(8,128)S(1)}, f32[16,128,1]{1,0,2:T(8,128)S(1)}, u32[]{:S(2)}, u32[]{:S(2)}) collective-permute-start(f32[16,128,1]{1,0,2:T(8,128)S(1)} %copy.30), channel_id=1, source_target_pairs={{0,1},{1,2},{2,3},{3,0},{4,5},{5,6},{6,7},{7,4},{8,9},{9,10},{10,1... | collective-permute-start | bytes 24584 | tf_op jit(solution)/shard_map/ppermute | solution.py:475
  11.2 1.0 collective-permute-start.1
  12.2 2.6 %collective-permute-done.1 = f32[16,128,1]{1,0,2:T(8,128)S(1)} collective-permute-done((f32[16,128,1]{1,0,2:T(8,128)S(1)}, f32[16,128,1]{1,0,2:T(8,128)S(1)}, u32[]{:S(2)}, u32[]{:S(2)}) %collective-permute-start.1) | collective-permute-done | bytes 8224 | tf_op jit(solution)/shard_map/ppermute | solution.py:476
  15.7 3.4 %stencil.2 = (f32[2,128,512]{2,1,0:T(8,128)S(1)}, f32[2,128,512]{2,1,0:T(8,128)S(1)}, f32[2,128,512]{2,1,0:T(8,128)S(1)}, f32[2,128,512]{2,1,0:T(8,128)S(1)}) custom-call(s32[2]{0:T(128)S(1)} %pad_add_fusion.me_ref, f32[4,4,128,512]{3,2,1,0:T(8,128)} %bitcast.26, f32[4,4,128,512]{3,2,1,0:T(8,128)} %bitcast.27, f32[4,4,128,512]{3,2,1,0:T(8,128)} %bitcast.28, ...), custom_call_target="tpu_custom_call" | custom-call | flops 6291456 | bytes 4194304 | tf_op jit(solution)/shard_map/stencil/pallas_call | solution.py:89
  19.0 2.5 %collective-permute-start.4 = (f32[2,128,512]{2,1,0:T(8,128)S(1)}, f32[2,128,512]{2,1,0:T(8,128)S(1)}, u32[]{:S(2)}, u32[]{:S(2)}) collective-permute-start(f32[2,128,512]{2,1,0:T(8,128)S(1)} %get-tuple-element.51), channel_id=1, source_target_pairs={{0,1},{1,0},{2,3},{3,2},{4,5},{5,4},{6,7},{7,6},{8,9},{9,8},{10,11... | collective-permute-start | bytes 1572872 | tf_op jit(solution)/shard_map/ppermute | solution.py:32
  21.5 1.5 collective-permute-start.6
  23.0 3.3 %stencil.3 = (f32[2,128,512]{2,1,0:T(8,128)S(1)}, f32[2,128,512]{2,1,0:T(8,128)S(1)}, f32[2,128,512]{2,1,0:T(8,128)S(1)}, f32[2,128,512]{2,1,0:T(8,128)S(1)}) custom-call(s32[2]{0:T(128)S(1)} %pad_add_fusion.me_ref, f32[4,4,128,512]{3,2,1,0:T(8,128)} %bitcast.30, f32[4,4,128,512]{3,2,1,0:T(8,128)} %bitcast.31, f32[4,4,128,512]{3,2,1,0:T(8,128)} %bitcast.32, ...), custom_call_target="tpu_custom_call" | custom-call | flops 6291456 | bytes 4194304 | tf_op jit(solution)/shard_map/stencil/pallas_call | solution.py:89
  26.4 8.4 %factors.1 = (f32[4,128,2048]{2,1,0:T(8,128)S(1)}, f32[4,128,2048]{2,1,0:T(8,128)S(1)}, f32[4,4,2048]{2,1,0:T(4,128)S(1)}) custom-call(f32[4,128,2048]{2,1,0:T(8,128)} %refs_6_.1, f32[4,128,2048]{2,1,0:T(8,128)} %refs_7_.3, f32[4,128,2048]{2,1,0:T(8,128)} %refs_8_.3), custom_call_target="tpu_custom_call" | custom-call | flops 62914560 | bytes 20971520 | tf_op jit(solution)/shard_map/factors/pallas_call | solution.py:191
  34.9 2.0 %collective-permute-start.15 = (f32[2,128,512]{2,1,0:T(8,128)S(1)}, f32[2,128,512]{2,1,0:T(8,128)S(1)}, u32[]{:S(2)}, u32[]{:S(2)}) collective-permute-start(f32[2,128,512]{2,1,0:T(8,128)S(1)} %get-tuple-element.65), channel_id=1, source_target_pairs={{0,1},{1,0},{2,3},{3,2},{4,5},{5,4},{6,7},{7,6},{8,9},{9,8},{10,11... | collective-permute-start | bytes 1572872 | tf_op jit(solution)/shard_map/ppermute | solution.py:32
  36.9 8.6 %basis.1 = (bf16[2048,2048]{1,0:T(8,128)(2,1)S(1)}, bf16[2048,2048]{1,0:T(8,128)(2,1)S(1)}) custom-call(f32[2048,2048]{1,0:T(8,128)} %e_ref), custom_call_target="tpu_custom_call" | custom-call | flops 16777216 | bytes 33554432 | tf_op jit(solution)/shard_map/basis/pallas_call | solution.py:118
  45.6 0.6 shard_map.83.refs_4_
  46.3 1.6 collective-permute-start.17
  47.9 3.6 %collective-permute-start.14 = (f32[4,4,2048]{2,1,0:T(4,128)S(1)}, f32[4,4,2048]{2,1,0:T(4,128)S(1)}, u32[]{:S(2)}, u32[]{:S(2)}) collective-permute-start(f32[4,4,2048]{2,1,0:T(4,128)S(1)} %shard_map.83.refs_4_), channel_id=1, source_target_pairs={{0,24},{4,28},{8,16},{12,20},{16,8},{20,12},{24,0},{28,4},{1,25},{... | collective-permute-start | bytes 393224 | tf_op jit(solution)/shard_map/ppermute | solution.py:32
  51.4 12.5 %forward.2 = (f32[2,128,2048]{2,1,0:T(8,128)S(1)}, f32[4,2048]{1,0:T(4,128)S(1)}) custom-call(s32[2]{0:T(128)S(1)} %pad_add_fusion.me_ref, f32[2,128,512]{2,1,0:T(8,128)S(1)} %get-tuple-element.50.refs_0_, f32[2,128,512]{2,1,0:T(8,128)S(1)} %collective-permute-done.4.refs_1_, f32[2,128,512]{2,1,0:T(8,128)S(1)} %collective-permute-done.5.refs_2_, ...), custom_call_target="tpu_custom_call" | custom-call | flops 6442450944 | bytes 16777216 | tf_op jit(solution)/shard_map/forward/pallas_call | solution.py:258
  64.1 1.1 collective-permute-done.7.other_ref.refs_9_
  65.2 0.6 shard_map.82.refs_0_
  65.8 6.9 %collective-permute-done.13.refs_6_ = f32[4,4,2048]{2,1,0:T(4,128)S(1)} collective-permute-done((f32[4,4,2048]{2,1,0:T(4,128)S(1)}, f32[4,4,2048]{2,1,0:T(4,128)S(1)}, u32[]{:S(2)}, u32[]{:S(2)}) %collective-permute-start.13) | collective-permute-done | bytes 131104 | tf_op jit(solution)/shard_map/ppermute | solution.py:32
  72.7 1.2 collective-permute-start.11
  74.0 4.5 %collective-permute-done.11.refs_3_ = f32[4,2048]{1,0:T(4,128)S(1)} collective-permute-done((f32[4,2048]{1,0:T(4,128)S(1)}, f32[4,2048]{1,0:T(4,128)S(1)}, u32[]{:S(2)}, u32[]{:S(2)}) %collective-permute-start.11) | collective-permute-done | bytes 32800 | tf_op jit(solution)/shard_map/ppermute | solution.py:32
  78.4 0.7 collective-permute-done.10.refs_2_
  79.1 3.2 %collective-permute-done.9.refs_1_ = f32[4,2048]{1,0:T(4,128)S(1)} collective-permute-done((f32[4,2048]{1,0:T(4,128)S(1)}, f32[4,2048]{1,0:T(4,128)S(1)}, u32[]{:S(2)}, u32[]{:S(2)}) %collective-permute-start.9) | collective-permute-done | bytes 32800 | tf_op jit(solution)/shard_map/ppermute | solution.py:32
  82.4 1.7 %modal.2.m_ref = bf16[512,2048]{1,0:T(8,128)(2,1)S(1)} custom-call(s32[2]{0:T(128)S(1)} %pad_add_fusion.me_ref, f32[4,2048]{1,0:T(4,128)S(1)} %shard_map.82.refs_0_, f32[4,2048]{1,0:T(4,128)S(1)} %collective-permute-done.9.refs_1_, f32[4,2048]{1,0:T(4,128)S(1)} %collective-permute-done.10.refs_2_, f32[4,2048]{1,0:T(4,128)S(1)} %collective-permute-done.11.refs_3_, ...), custom_call_target="tpu_custom_call" | custom-call | flops 5242880 | bytes 8388608 | tf_op jit(solution)/shard_map/modal/pallas_call | solution.py:366
  84.1 2.6 %back.8.refs_0_ = f32[2,128,512]{2,1,0:T(8,128)S(1)} custom-call(s32[2]{0:T(128)S(1)} %pad_add_fusion.me_ref, bf16[512,2048]{1,0:T(8,128)(2,1)S(1)} %modal.2.m_ref, bf16[2048,2048]{1,0:T(8,128)(2,1)S(1)} %get-tuple-element.55.refs_4_.hi_ref, bf16[2048,2048]{1,0:T(8,128)(2,1)S(1)} %get-tuple-element.56.refs_5_.lo_ref), custom_call_target="tpu_custom_call" | custom-call | flops 1610612736 | bytes 4194304 | tf_op jit(solution)/shard_map/back/pallas_call | solution.py:405
  86.7 2.6 %back.15 = f32[2,128,512]{2,1,0:T(8,128)S(1)} custom-call(s32[2]{0:T(128)S(1)} %pad_add_fusion.me_ref, bf16[512,2048]{1,0:T(8,128)(2,1)S(1)} %modal.2.m_ref, bf16[2048,2048]{1,0:T(8,128)(2,1)S(1)} %get-tuple-element.55.refs_4_.hi_ref, bf16[2048,2048]{1,0:T(8,128)(2,1)S(1)} %get-tuple-element.56.refs_5_.lo_ref), custom_call_target="tpu_custom_call" | custom-call | flops 1610612736 | bytes 4194304 | tf_op jit(solution)/shard_map/back/pallas_call | solution.py:405
  89.3 12.3 %forward.3 = (f32[2,128,2048]{2,1,0:T(8,128)S(1)}, f32[4,2048]{1,0:T(4,128)S(1)}) custom-call(s32[2]{0:T(128)S(1)} %pad_add_fusion.me_ref, f32[2,128,512]{2,1,0:T(8,128)S(1)} %get-tuple-element.64.refs_0_, f32[2,128,512]{2,1,0:T(8,128)S(1)} %collective-permute-done.15.refs_1_, f32[2,128,512]{2,1,0:T(8,128)S(1)} %collective-permute-done.16.refs_2_, ...), custom_call_target="tpu_custom_call" | custom-call | flops 6442450944 | bytes 16777216 | tf_op jit(solution)/shard_map/forward/pallas_call | solution.py:258
  101.8 2.6 %back.13 = f32[2,128,512]{2,1,0:T(8,128)S(1)} custom-call(s32[2]{0:T(128)S(1)} %pad_add_fusion.me_ref, bf16[512,2048]{1,0:T(8,128)(2,1)S(1)} %modal.2.m_ref, bf16[2048,2048]{1,0:T(8,128)(2,1)S(1)} %get-tuple-element.55.refs_4_.hi_ref, bf16[2048,2048]{1,0:T(8,128)(2,1)S(1)} %get-tuple-element.56.refs_5_.lo_ref), custom_call_target="tpu_custom_call" | custom-call | flops 1610612736 | bytes 4194304 | tf_op jit(solution)/shard_map/back/pallas_call | solution.py:405
  104.4 2.0 %collective-permute-start.25 = (f32[2,128,512]{2,1,0:T(8,128)S(1)}, f32[2,128,512]{2,1,0:T(8,128)S(1)}, u32[]{:S(2)}, u32[]{:S(2)}) collective-permute-start(f32[2,128,512]{2,1,0:T(8,128)S(1)} %back.13), channel_id=1, source_target_pairs={{0,1},{1,0},{2,3},{3,2},{4,5},{5,4},{6,7},{7,6},{8,9},{9,8},{10,11... | collective-permute-start | bytes 1572872 | tf_op jit(solution)/shard_map/ppermute | solution.py:32
  106.4 0.6 shard_map.84.refs_0_
  107.0 1.3 collective-permute-start.21
  108.5 2.9 %collective-permute-start.19 = (f32[4,2048]{1,0:T(4,128)S(1)}, f32[4,2048]{1,0:T(4,128)S(1)}, u32[]{:S(2)}, u32[]{:S(2)}) collective-permute-start(f32[4,2048]{1,0:T(4,128)S(1)} %shard_map.84.refs_0_), channel_id=1, source_target_pairs={{0,8},{4,12},{8,0},{12,4},{16,24},{20,28},{24,16},{28,20},{1,9},{5... | collective-permute-start | bytes 98312 | tf_op jit(solution)/shard_map/ppermute | solution.py:32
  111.5 2.6 %back.14 = f32[2,128,512]{2,1,0:T(8,128)S(1)} custom-call(s32[2]{0:T(128)S(1)} %pad_add_fusion.me_ref, bf16[512,2048]{1,0:T(8,128)(2,1)S(1)} %modal.2.m_ref, bf16[2048,2048]{1,0:T(8,128)(2,1)S(1)} %get-tuple-element.55.refs_4_.hi_ref, bf16[2048,2048]{1,0:T(8,128)(2,1)S(1)} %get-tuple-element.56.refs_5_.lo_ref), custom_call_target="tpu_custom_call" | custom-call | flops 1610612736 | bytes 4194304 | tf_op jit(solution)/shard_map/back/pallas_call | solution.py:405
  114.1 0.6 collective-permute-start.26
  114.7 1.0 collective-permute-start.27
  115.7 1.7 %modal.3.m_ref = bf16[512,2048]{1,0:T(8,128)(2,1)S(1)} custom-call(s32[2]{0:T(128)S(1)} %pad_add_fusion.me_ref, f32[4,2048]{1,0:T(4,128)S(1)} %shard_map.84.refs_0_, f32[4,2048]{1,0:T(4,128)S(1)} %collective-permute-done.19.refs_1_, f32[4,2048]{1,0:T(4,128)S(1)} %collective-permute-done.20.refs_2_, f32[4,2048]{1,0:T(4,128)S(1)} %collective-permute-done.21.refs_3_, ...), custom_call_target="tpu_custom_call" | custom-call | flops 5242880 | bytes 8388608 | tf_op jit(solution)/shard_map/modal/pallas_call | solution.py:366
  117.4 2.8 %back.12 = f32[2,128,512]{2,1,0:T(8,128)S(1)} custom-call(s32[2]{0:T(128)S(1)} %pad_add_fusion.me_ref, bf16[512,2048]{1,0:T(8,128)(2,1)S(1)} %modal.3.m_ref, bf16[2048,2048]{1,0:T(8,128)(2,1)S(1)} %get-tuple-element.55.refs_4_.hi_ref, bf16[2048,2048]{1,0:T(8,128)(2,1)S(1)} %get-tuple-element.56.refs_5_.lo_ref), custom_call_target="tpu_custom_call" | custom-call | flops 1610612736 | bytes 4194304 | tf_op jit(solution)/shard_map/back/pallas_call | solution.py:405
  120.2 2.6 %back.11 = f32[2,128,512]{2,1,0:T(8,128)S(1)} custom-call(s32[2]{0:T(128)S(1)} %pad_add_fusion.me_ref, bf16[512,2048]{1,0:T(8,128)(2,1)S(1)} %modal.3.m_ref, bf16[2048,2048]{1,0:T(8,128)(2,1)S(1)} %get-tuple-element.55.refs_4_.hi_ref, bf16[2048,2048]{1,0:T(8,128)(2,1)S(1)} %get-tuple-element.56.refs_5_.lo_ref), custom_call_target="tpu_custom_call" | custom-call | flops 1610612736 | bytes 4194304 | tf_op jit(solution)/shard_map/back/pallas_call | solution.py:405
  122.8 2.6 %back.10 = f32[2,128,512]{2,1,0:T(8,128)S(1)} custom-call(s32[2]{0:T(128)S(1)} %pad_add_fusion.me_ref, bf16[512,2048]{1,0:T(8,128)(2,1)S(1)} %modal.3.m_ref, bf16[2048,2048]{1,0:T(8,128)(2,1)S(1)} %get-tuple-element.55.refs_4_.hi_ref, bf16[2048,2048]{1,0:T(8,128)(2,1)S(1)} %get-tuple-element.56.refs_5_.lo_ref), custom_call_target="tpu_custom_call" | custom-call | flops 1610612736 | bytes 4194304 | tf_op jit(solution)/shard_map/back/pallas_call | solution.py:405
  125.4 2.0 %collective-permute-start.22 = (f32[2,128,512]{2,1,0:T(8,128)S(1)}, f32[2,128,512]{2,1,0:T(8,128)S(1)}, u32[]{:S(2)}, u32[]{:S(2)}) collective-permute-start(f32[2,128,512]{2,1,0:T(8,128)S(1)} %back.10), channel_id=1, source_target_pairs={{0,1},{1,0},{2,3},{3,2},{4,5},{5,4},{6,7},{7,6},{8,9},{9,8},{10,11... | collective-permute-start | bytes 1572872 | tf_op jit(solution)/shard_map/ppermute | solution.py:32
  128.0 1.0 collective-permute-start.24
  129.0 2.6 %back.9.refs_0_ = f32[2,128,512]{2,1,0:T(8,128)S(1)} custom-call(s32[2]{0:T(128)S(1)} %pad_add_fusion.me_ref, bf16[512,2048]{1,0:T(8,128)(2,1)S(1)} %modal.3.m_ref, bf16[2048,2048]{1,0:T(8,128)(2,1)S(1)} %get-tuple-element.55.refs_4_.hi_ref, bf16[2048,2048]{1,0:T(8,128)(2,1)S(1)} %get-tuple-element.56.refs_5_.lo_ref), custom_call_target="tpu_custom_call" | custom-call | flops 1610612736 | bytes 4194304 | tf_op jit(solution)/shard_map/back/pallas_call | solution.py:405
  131.6 8.6 %collective-permute-done.26.refs_2_ = f32[2,128,512]{2,1,0:T(8,128)S(1)} collective-permute-done((f32[2,128,512]{2,1,0:T(8,128)S(1)}, f32[2,128,512]{2,1,0:T(8,128)S(1)}, u32[]{:S(2)}, u32[]{:S(2)}) %collective-permute-start.26) | collective-permute-done | bytes 524320 | tf_op jit(solution)/shard_map/ppermute | solution.py:32
  140.2 1.9 %place.2.refs_4_ = f32[16,128,512]{2,1,0:T(8,128)} custom-call(s32[2]{0:T(128)S(1)} %pad_add_fusion.me_ref, f32[2,128,512]{2,1,0:T(8,128)S(1)} %back.8.refs_0_, f32[2,128,512]{2,1,0:T(8,128)S(1)} %collective-permute-done.25.refs_1_, f32[2,128,512]{2,1,0:T(8,128)S(1)} %collective-permute-done.26.refs_2_, f32[2,128,512]{2,1,0:T(8,128)S(1)} %collective-permute-done.27.refs_3_), custom_call_target="tpu_custom_call" | custom-call | bytes 4194304 | tf_op jit(solution)/shard_map/place/pallas_call | solution.py:442
  142.1 19.0 %collective-permute-done.23.refs_2_ = f32[2,128,512]{2,1,0:T(8,128)S(1)} collective-permute-done((f32[2,128,512]{2,1,0:T(8,128)S(1)}, f32[2,128,512]{2,1,0:T(8,128)S(1)}, u32[]{:S(2)}, u32[]{:S(2)}) %collective-permute-start.23) | collective-permute-done | bytes 524320 | tf_op jit(solution)/shard_map/ppermute | solution.py:32
  161.0 1.9 %place.3 = f32[16,128,512]{2,1,0:T(8,128)} custom-call(s32[2]{0:T(128)S(1)} %pad_add_fusion.me_ref, f32[2,128,512]{2,1,0:T(8,128)S(1)} %back.9.refs_0_, f32[2,128,512]{2,1,0:T(8,128)S(1)} %collective-permute-done.22.refs_1_, f32[2,128,512]{2,1,0:T(8,128)S(1)} %collective-permute-done.23.refs_2_, ...), custom_call_target="tpu_custom_call", output_to_operand_aliasing={{}: (5, {})} | custom-call | bytes 4194304 | tf_op jit(solution)/shard_map/place/pallas_call | solution.py:442
  (42 shorter events, 2.7 us)
Async XLA Ops:
  1.1 14.5 %collective-permute-start.3 = (f32[16,1,512]{2,1,0:T(1,128)S(1)}, f32[16,1,512]{2,1,0:T(1,128)S(1)}, u32[]{:S(2)}, u32[]{:S(2)}) collective-permute-start(f32[16,1,512]{2,1,0:T(1,128)S(1)} %get-tuple-element.73), channel_id=1, source_target_pairs={{4,0},{8,4},{12,8},{16,12},{20,16},{24,20},{28,24},{5,1},{9,5},{13... | collective-permute-start | bytes 98312 | tf_op jit(solution)/shard_map/ppermute | solution.py:474
  2.4 13.3 %copy-start = (f32[128,512]{1,0:T(8,128)S(1)}, f32[128,512]{1,0:T(8,128)}, u32[]{:S(2)}) copy-start(f32[128,512]{1,0:T(8,128)} %refs_20_.3) | copy-start | bytes 786436
  2.4 13.3 %copy-start.1 = (f32[128,512]{1,0:T(8,128)S(1)}, f32[128,512]{1,0:T(8,128)}, u32[]{:S(2)}) copy-start(f32[128,512]{1,0:T(8,128)} %refs_21_.3) | copy-start | bytes 786436
  2.4 13.3 %copy-start.2 = (f32[512]{0:T(512)S(1)}, f32[512]{0:T(512)}, u32[]{:S(2)}) copy-start(f32[512]{0:T(512)} %param.11) | copy-start | bytes 6148
  2.4 13.2 %collective-permute-start.2 = (f32[16,1,512]{2,1,0:T(1,128)S(1)}, f32[16,1,512]{2,1,0:T(1,128)S(1)}, u32[]{:S(2)}, u32[]{:S(2)}) collective-permute-start(f32[16,1,512]{2,1,0:T(1,128)S(1)} %get-tuple-element.74), channel_id=1, source_target_pairs={{0,4},{4,8},{8,12},{12,16},{16,20},{20,24},{24,28},{1,5},{5,9},{9,... | collective-permute-start | bytes 98312 | tf_op jit(solution)/shard_map/ppermute | solution.py:473
  7.8 7.4 %collective-permute-start = (f32[16,128,1]{1,0,2:T(8,128)S(1)}, f32[16,128,1]{1,0,2:T(8,128)S(1)}, u32[]{:S(2)}, u32[]{:S(2)}) collective-permute-start(f32[16,128,1]{1,0,2:T(8,128)S(1)} %copy.30), channel_id=1, source_target_pairs={{0,1},{1,2},{2,3},{3,0},{4,5},{5,6},{6,7},{7,4},{8,9},{9,10},{10,1... | collective-permute-start | bytes 24584 | tf_op jit(solution)/shard_map/ppermute | solution.py:475
  11.2 3.7 %collective-permute-start.1 = (f32[16,128,1]{1,0,2:T(8,128)S(1)}, f32[16,128,1]{1,0,2:T(8,128)S(1)}, u32[]{:S(2)}, u32[]{:S(2)}) collective-permute-start(f32[16,128,1]{1,0,2:T(8,128)S(1)} %copy.31), channel_id=1, source_target_pairs={{1,0},{2,1},{3,2},{0,3},{5,4},{6,5},{7,6},{4,7},{9,8},{10,9},{11,1... | collective-permute-start | bytes 24584 | tf_op jit(solution)/shard_map/ppermute | solution.py:476
  19.0 27.2 %collective-permute-start.4 = (f32[2,128,512]{2,1,0:T(8,128)S(1)}, f32[2,128,512]{2,1,0:T(8,128)S(1)}, u32[]{:S(2)}, u32[]{:S(2)}) collective-permute-start(f32[2,128,512]{2,1,0:T(8,128)S(1)} %get-tuple-element.51), channel_id=1, source_target_pairs={{0,1},{1,0},{2,3},{3,2},{4,5},{5,4},{6,7},{7,6},{8,9},{9,8},{10,11... | collective-permute-start | bytes 1572872 | tf_op jit(solution)/shard_map/ppermute | solution.py:32
  21.5 26.4 %collective-permute-start.5 = (f32[2,128,512]{2,1,0:T(8,128)S(1)}, f32[2,128,512]{2,1,0:T(8,128)S(1)}, u32[]{:S(2)}, u32[]{:S(2)}) collective-permute-start(f32[2,128,512]{2,1,0:T(8,128)S(1)} %get-tuple-element.52), channel_id=1, source_target_pairs={{0,2},{1,3},{2,0},{3,1},{4,6},{5,7},{6,4},{7,5},{8,10},{9,11},{10,... | collective-permute-start | bytes 1572872 | tf_op jit(solution)/shard_map/ppermute | solution.py:32
  21.5 29.9 %collective-permute-start.6 = (f32[2,128,512]{2,1,0:T(8,128)S(1)}, f32[2,128,512]{2,1,0:T(8,128)S(1)}, u32[]{:S(2)}, u32[]{:S(2)}) collective-permute-start(f32[2,128,512]{2,1,0:T(8,128)S(1)} %get-tuple-element.53), channel_id=1, source_target_pairs={{0,3},{1,2},{2,1},{3,0},{4,7},{5,6},{6,5},{7,4},{8,11},{9,10},{10,... | collective-permute-start | bytes 1572872 | tf_op jit(solution)/shard_map/ppermute | solution.py:32
  34.8 10.8 %collective-permute-start.8 = (f32[4,4,2048]{2,1,0:T(4,128)S(1)}, f32[4,4,2048]{2,1,0:T(4,128)S(1)}, u32[]{:S(2)}, u32[]{:S(2)}) collective-permute-start(f32[4,4,2048]{2,1,0:T(4,128)S(1)} %get-tuple-element.59.c_own_ref.own_ref.refs_10_), channel_id=1, source_target_pairs={{0,4},{4,0},{8,12},{12,8},{16,20},{20,16},{24,28},{28,24},{1,5},{5... | collective-permute-start | bytes 393224 | tf_op jit(solution)/shard_map/ppermute | solution.py:32
  34.9 54.4 %collective-permute-start.15 = (f32[2,128,512]{2,1,0:T(8,128)S(1)}, f32[2,128,512]{2,1,0:T(8,128)S(1)}, u32[]{:S(2)}, u32[]{:S(2)}) collective-permute-start(f32[2,128,512]{2,1,0:T(8,128)S(1)} %get-tuple-element.65), channel_id=1, source_target_pairs={{0,1},{1,0},{2,3},{3,2},{4,5},{5,4},{6,7},{7,6},{8,9},{9,8},{10,11... | collective-permute-start | bytes 1572872 | tf_op jit(solution)/shard_map/ppermute | solution.py:32
  45.6 43.8 %collective-permute-start.16 = (f32[2,128,512]{2,1,0:T(8,128)S(1)}, f32[2,128,512]{2,1,0:T(8,128)S(1)}, u32[]{:S(2)}, u32[]{:S(2)}) collective-permute-start(f32[2,128,512]{2,1,0:T(8,128)S(1)} %get-tuple-element.66), channel_id=1, source_target_pairs={{0,2},{1,3},{2,0},{3,1},{4,6},{5,7},{6,4},{7,5},{8,10},{9,11},{10,... | collective-permute-start | bytes 1572872 | tf_op jit(solution)/shard_map/ppermute | solution.py:32
  46.3 43.1 %collective-permute-start.17 = (f32[2,128,512]{2,1,0:T(8,128)S(1)}, f32[2,128,512]{2,1,0:T(8,128)S(1)}, u32[]{:S(2)}, u32[]{:S(2)}) collective-permute-start(f32[2,128,512]{2,1,0:T(8,128)S(1)} %get-tuple-element.67), channel_id=1, source_target_pairs={{0,3},{1,2},{2,1},{3,0},{4,7},{5,6},{6,5},{7,4},{8,11},{9,10},{10,... | collective-permute-start | bytes 1572872 | tf_op jit(solution)/shard_map/ppermute | solution.py:32
  47.9 16.1 %collective-permute-start.14 = (f32[4,4,2048]{2,1,0:T(4,128)S(1)}, f32[4,4,2048]{2,1,0:T(4,128)S(1)}, u32[]{:S(2)}, u32[]{:S(2)}) collective-permute-start(f32[4,4,2048]{2,1,0:T(4,128)S(1)} %shard_map.83.refs_4_), channel_id=1, source_target_pairs={{0,24},{4,28},{8,16},{12,20},{16,8},{20,12},{24,0},{28,4},{1,25},{... | collective-permute-start | bytes 393224 | tf_op jit(solution)/shard_map/ppermute | solution.py:32
  63.9 1.3 collective-permute-start.7
  64.0 8.7 %collective-permute-start.13 = (f32[4,4,2048]{2,1,0:T(4,128)S(1)}, f32[4,4,2048]{2,1,0:T(4,128)S(1)}, u32[]{:S(2)}, u32[]{:S(2)}) collective-permute-start(f32[4,4,2048]{2,1,0:T(4,128)S(1)} %shard_map.83.refs_4_), channel_id=1, source_target_pairs={{0,16},{4,20},{8,24},{12,28},{16,0},{20,4},{24,8},{28,12},{1,17},{... | collective-permute-start | bytes 393224 | tf_op jit(solution)/shard_map/ppermute | solution.py:32
  65.2 8.8 %collective-permute-start.12 = (f32[4,4,2048]{2,1,0:T(4,128)S(1)}, f32[4,4,2048]{2,1,0:T(4,128)S(1)}, u32[]{:S(2)}, u32[]{:S(2)}) collective-permute-start(f32[4,4,2048]{2,1,0:T(4,128)S(1)} %shard_map.83.refs_4_), channel_id=1, source_target_pairs={{0,8},{4,12},{8,0},{12,4},{16,24},{20,28},{24,16},{28,20},{1,9},{5... | collective-permute-start | bytes 393224 | tf_op jit(solution)/shard_map/ppermute | solution.py:32
  72.7 5.7 %collective-permute-start.11 = (f32[4,2048]{1,0:T(4,128)S(1)}, f32[4,2048]{1,0:T(4,128)S(1)}, u32[]{:S(2)}, u32[]{:S(2)}) collective-permute-start(f32[4,2048]{1,0:T(4,128)S(1)} %shard_map.82.refs_0_), channel_id=1, source_target_pairs={{0,24},{4,28},{8,16},{12,20},{16,8},{20,12},{24,0},{28,4},{1,25},{... | collective-permute-start | bytes 98312 | tf_op jit(solution)/shard_map/ppermute | solution.py:32
  74.0 5.2 %collective-permute-start.10 = (f32[4,2048]{1,0:T(4,128)S(1)}, f32[4,2048]{1,0:T(4,128)S(1)}, u32[]{:S(2)}, u32[]{:S(2)}) collective-permute-start(f32[4,2048]{1,0:T(4,128)S(1)} %shard_map.82.refs_0_), channel_id=1, source_target_pairs={{0,16},{4,20},{8,24},{12,28},{16,0},{20,4},{24,8},{28,12},{1,17},{... | collective-permute-start | bytes 98312 | tf_op jit(solution)/shard_map/ppermute | solution.py:32
  78.4 3.9 %collective-permute-start.9 = (f32[4,2048]{1,0:T(4,128)S(1)}, f32[4,2048]{1,0:T(4,128)S(1)}, u32[]{:S(2)}, u32[]{:S(2)}) collective-permute-start(f32[4,2048]{1,0:T(4,128)S(1)} %shard_map.82.refs_0_), channel_id=1, source_target_pairs={{0,8},{4,12},{8,0},{12,4},{16,24},{20,28},{24,16},{28,20},{1,9},{5... | collective-permute-start | bytes 98312 | tf_op jit(solution)/shard_map/ppermute | solution.py:32
  101.7 4.7 %collective-permute-start.18 = (f32[4,2048]{1,0:T(4,128)S(1)}, f32[4,2048]{1,0:T(4,128)S(1)}, u32[]{:S(2)}, u32[]{:S(2)}) collective-permute-start(f32[4,2048]{1,0:T(4,128)S(1)} %get-tuple-element.68.own_ref.refs_8_), channel_id=1, source_target_pairs={{0,4},{4,0},{8,12},{12,8},{16,20},{20,16},{24,28},{28,24},{1,5},{5... | collective-permute-start | bytes 98312 | tf_op jit(solution)/shard_map/ppermute | solution.py:32
  104.4 23.6 %collective-permute-start.25 = (f32[2,128,512]{2,1,0:T(8,128)S(1)}, f32[2,128,512]{2,1,0:T(8,128)S(1)}, u32[]{:S(2)}, u32[]{:S(2)}) collective-permute-start(f32[2,128,512]{2,1,0:T(8,128)S(1)} %back.13), channel_id=1, source_target_pairs={{0,1},{1,0},{2,3},{3,2},{4,5},{5,4},{6,7},{7,6},{8,9},{9,8},{10,11... | collective-permute-start | bytes 1572872 | tf_op jit(solution)/shard_map/ppermute | solution.py:32
  107.0 7.7 %collective-permute-start.21 = (f32[4,2048]{1,0:T(4,128)S(1)}, f32[4,2048]{1,0:T(4,128)S(1)}, u32[]{:S(2)}, u32[]{:S(2)}) collective-permute-start(f32[4,2048]{1,0:T(4,128)S(1)} %shard_map.84.refs_0_), channel_id=1, source_target_pairs={{0,24},{4,28},{8,16},{12,20},{16,8},{20,12},{24,0},{28,4},{1,25},{... | collective-permute-start | bytes 98312 | tf_op jit(solution)/shard_map/ppermute | solution.py:32
  108.3 7.4 %collective-permute-start.20 = (f32[4,2048]{1,0:T(4,128)S(1)}, f32[4,2048]{1,0:T(4,128)S(1)}, u32[]{:S(2)}, u32[]{:S(2)}) collective-permute-start(f32[4,2048]{1,0:T(4,128)S(1)} %shard_map.84.refs_0_), channel_id=1, source_target_pairs={{0,16},{4,20},{8,24},{12,28},{16,0},{20,4},{24,8},{28,12},{1,17},{... | collective-permute-start | bytes 98312 | tf_op jit(solution)/shard_map/ppermute | solution.py:32
  108.5 7.2 %collective-permute-start.19 = (f32[4,2048]{1,0:T(4,128)S(1)}, f32[4,2048]{1,0:T(4,128)S(1)}, u32[]{:S(2)}, u32[]{:S(2)}) collective-permute-start(f32[4,2048]{1,0:T(4,128)S(1)} %shard_map.84.refs_0_), channel_id=1, source_target_pairs={{0,8},{4,12},{8,0},{12,4},{16,24},{20,28},{24,16},{28,20},{1,9},{5... | collective-permute-start | bytes 98312 | tf_op jit(solution)/shard_map/ppermute | solution.py:32
  114.1 26.1 %collective-permute-start.26 = (f32[2,128,512]{2,1,0:T(8,128)S(1)}, f32[2,128,512]{2,1,0:T(8,128)S(1)}, u32[]{:S(2)}, u32[]{:S(2)}) collective-permute-start(f32[2,128,512]{2,1,0:T(8,128)S(1)} %back.14), channel_id=1, source_target_pairs={{0,2},{1,3},{2,0},{3,1},{4,6},{5,7},{6,4},{7,5},{8,10},{9,11},{10,... | collective-permute-start | bytes 1572872 | tf_op jit(solution)/shard_map/ppermute | solution.py:32
  114.7 25.5 %collective-permute-start.27 = (f32[2,128,512]{2,1,0:T(8,128)S(1)}, f32[2,128,512]{2,1,0:T(8,128)S(1)}, u32[]{:S(2)}, u32[]{:S(2)}) collective-permute-start(f32[2,128,512]{2,1,0:T(8,128)S(1)} %back.15), channel_id=1, source_target_pairs={{0,3},{1,2},{2,1},{3,0},{4,7},{5,6},{6,5},{7,4},{8,11},{9,10},{10,... | collective-permute-start | bytes 1572872 | tf_op jit(solution)/shard_map/ppermute | solution.py:32
  125.4 16.6 %collective-permute-start.22 = (f32[2,128,512]{2,1,0:T(8,128)S(1)}, f32[2,128,512]{2,1,0:T(8,128)S(1)}, u32[]{:S(2)}, u32[]{:S(2)}) collective-permute-start(f32[2,128,512]{2,1,0:T(8,128)S(1)} %back.10), channel_id=1, source_target_pairs={{0,1},{1,0},{2,3},{3,2},{4,5},{5,4},{6,7},{7,6},{8,9},{9,8},{10,11... | collective-permute-start | bytes 1572872 | tf_op jit(solution)/shard_map/ppermute | solution.py:32
  127.4 33.6 %collective-permute-start.23 = (f32[2,128,512]{2,1,0:T(8,128)S(1)}, f32[2,128,512]{2,1,0:T(8,128)S(1)}, u32[]{:S(2)}, u32[]{:S(2)}) collective-permute-start(f32[2,128,512]{2,1,0:T(8,128)S(1)} %back.11), channel_id=1, source_target_pairs={{0,2},{1,3},{2,0},{3,1},{4,6},{5,7},{6,4},{7,5},{8,10},{9,11},{10,... | collective-permute-start | bytes 1572872 | tf_op jit(solution)/shard_map/ppermute | solution.py:32
  128.0 33.1 %collective-permute-start.24 = (f32[2,128,512]{2,1,0:T(8,128)S(1)}, f32[2,128,512]{2,1,0:T(8,128)S(1)}, u32[]{:S(2)}, u32[]{:S(2)}) collective-permute-start(f32[2,128,512]{2,1,0:T(8,128)S(1)} %back.12), channel_id=1, source_target_pairs={{0,3},{1,2},{2,1},{3,0},{4,7},{5,6},{6,5},{7,4},{8,11},{9,10},{10,... | collective-permute-start | bytes 1572872 | tf_op jit(solution)/shard_map/ppermute | solution.py:32

commit v2 on v1

--- a/solution.py
+++ b/solution.py
@@ -45,96 +45,121 @@
     return hi, (v - hi.astype(F32)).astype(BF16)
 
 
-def stencil_body(count, me_ref, *refs):
-    f_refs = refs[:count]
-    west, east, south, north = (refs[count * (1 + i) : count * (2 + i)] for i in range(4))
-    mlon_ref, mlat_ref, w_ref = refs[5 * count : 5 * count + 3]
-    outs = refs[5 * count + 3 :]
-    rows, cols = mlon_ref.shape
+def small_call(body, me, args, shapes, mib=4):
+    return pl.pallas_call(
+        body,
+        grid_spec=pltpu.PrefetchScalarGridSpec(
+            num_scalar_prefetch=1,
+            grid=(1,),
+            in_specs=[VMEM] * len(args),
+            out_specs=[VMEM] * len(shapes),
+        ),
+        out_shape=[pltpu.VMEM(shape, F32) for shape in shapes],
+        compiler_params=params(mib),
+        cost_estimate=pl.CostEstimate(flops=1 << 20, bytes_accessed=1 << 18, transcendentals=0),
+    )(me, *near(*args))
+
+
+def diagonal(rows):
+    at = [lax.broadcasted_iota(jnp.int32, (rows, rows), d) for d in (0, 1)]
+    return at[0] == at[1]
+
+
+def rim_body(me_ref, f_ref, last_ref, first_ref, top_ref, bottom_ref):
+    modes, rows, cols = f_ref.shape
+    eye = diagonal(rows)
+    for k in range(modes):
+        for c, out in ((cols - 1, last_ref), (0, first_ref)):
+            column = jnp.broadcast_to(f_ref[k, :, c : c + 1], (rows, rows))
+            out[k : k + 1] = jnp.sum(jnp.where(eye, column, 0.0), axis=0, keepdims=True)
+        top_ref[k : k + 1] = f_ref[k, rows - 1 : rows]
+        bottom_ref[k : k + 1] = f_ref[k, 0:1]
+
+
+def stencil_body(count, first, size, me_ref, f_ref, west_ref, east_ref, south_ref, north_ref, *refs):
+    mlon_ref, mlat_ref, w_ref = refs[:3]
+    outs = refs[3:]
+    modes, rows, cols = f_ref.shape
+    local = modes // count
+    eye = diagonal(rows)
     lane = lax.broadcasted_iota(jnp.int32, (8, cols), 1)
     row = lax.broadcasted_iota(jnp.int32, (8, cols), 0)
     weight = jnp.broadcast_to(w_ref[...], (8, cols))
-    i = pl.program_id(0)
-    for x in range(count):
-        f_ref = f_refs[x]
-        for t in range(rows // 8):
-            at = pl.ds(8 * t, 8)
-            f = f_ref[0, 0, at]
-            below = f_ref[0, 0, 8 * t - 1 : 8 * t] if t else south[x][0, 0]
-            above = f_ref[0, 0, 8 * t + 8 : 8 * t + 9] if 8 * t + 8 < rows else north[x][0, 0]
-            w = jnp.where(lane == 0, west[x][0, 0, at], pltpu.roll(f, 1, 1))
-            e = jnp.where(lane == cols - 1, east[x][0, 0, at], pltpu.roll(f, cols - 1, 1))
-            s = jnp.where(row == 0, below, pltpu.roll(f, 1, 0))
-            n = jnp.where(row == 7, above, pltpu.roll(f, 7, 0))
-            outs[x][i, at] = (f + mlon_ref[at] * (w + e) + mlat_ref[at] * (s + n)) * weight
+
+    def column(ref, k):
+        spread = jnp.broadcast_to(ref[pl.ds(k, 1), :], (rows, rows))
+        return jnp.sum(jnp.where(eye, spread, 0.0), axis=1, keepdims=True)
+
+    def one(i, _):
+        for x in range(count):
+            k = (me_ref[0] ^ x) * local + first + i
+            west, east = column(west_ref, k), column(east_ref, k)
+            for t in range(rows // 8):
+                at = slice(8 * t, 8 * t + 8)
+                f = f_ref[k, at]
+                below = f_ref[k, 8 * t - 1 : 8 * t] if t else south_ref[pl.ds(k, 1), :]
+                above = (
+                    f_ref[k, 8 * t + 8 : 8 * t + 9]
+                    if 8 * t + 8 < rows
+                    else north_ref[pl.ds(k, 1), :]
+                )
+                w = jnp.where(lane == 0, west[at], pltpu.roll(f, 1, 1))
+                e = jnp.where(lane == cols - 1, east[at], pltpu.roll(f, cols - 1, 1))
+                s = jnp.where(row == 0, below, pltpu.roll(f, 1, 0))
+                n = jnp.where(row == 7, above, pltpu.roll(f, 7, 0))
+                outs[x][i, at] = (f + mlon_ref[at] * (w + e) + mlat_ref[at] * (s + n)) * weight
+        return 0
+
+    lax.fori_loop(0, size, one, 0)
 
 
 def stencil(me, forcing, halos, mlon, mlat, weights, count, first, size):
-    modes, rows, cols = forcing.shape
-    local = modes // count
-    f4 = forcing.reshape(count, local, rows, cols)
-    h4 = [h.reshape(count, local, *h.shape[1:]) for h in halos]
-
-    def spec(shape, x):
-        return pl.BlockSpec(
-            (1, 1) + shape, lambda i, m, x=x: (m[0] ^ x, first + i) + (0,) * len(shape)
-        )
-
-    args, specs = [], []
-    for a in [f4] + h4:
-        for x in range(count):
-            args.append(far(a)[0] if a is f4 else a)
-            specs.append(spec(a.shape[2:], x))
-    whole = pl.BlockSpec((rows, cols), lambda i, m: (0, 0))
-    return pl.pallas_call(
-        functools.partial(stencil_body, count),
+    rows, cols = mlon.shape
+    return small_call(
+        functools.partial(stencil_body, count, first, size),
+        me,
+        (forcing, *halos, mlon, mlat, weights),
+        [(size, rows, cols)] * count,
+    )
+
+
+def basis_body(me_ref, e_ref, hi_ref, lo_ref):
+    n, m = e_ref.shape
+    wide = min(512, m)
+
+    def rows(i, _):
+        at = pl.ds(pl.multiple_of(i * 32, 32), 32)
+        for c in range(0, m, wide):
+            hi, lo = split(e_ref[at, c : c + wide])
+            hi_ref[at, c : c + wide] = hi
+            lo_ref[at, c : c + wide] = lo
+        return 0
+
+    lax.fori_loop(0, n // 32, rows, 0)
+
+
+def basis_parts(me, basis):
+    n, m = basis.shape
+    return pl.pallas_call(
+        basis_body,
         grid_spec=pltpu.PrefetchScalarGridSpec(
-            num_scalar_prefetch=1,
-            grid=(size,),
-            in_specs=specs + [whole, whole, pl.BlockSpec((1, cols), lambda i, m: (0, 0))],
-            out_specs=[VMEM] * count,
-        ),
-        out_shape=[pltpu.VMEM((size, rows, cols), F32)] * count,
-        compiler_params=params(12),
-        cost_estimate=pl.CostEstimate(
-            flops=12 * size * count * rows * cols,
-            bytes_accessed=8 * size * count * rows * cols,
-            transcendentals=0,
-        ),
-        name="stencil",
-    )(me, *args, mlon, mlat, weights)
-
-
-def basis_body(e_ref, hi_ref, lo_ref):
-    t = e_ref.shape[0]
-    at = pl.ds(pl.multiple_of(pl.program_id(0) * t, t), t)
-    hi_ref[at], lo_ref[at] = split(e_ref[...])
-
-
-def basis_parts(basis):
-    n, m = basis.shape
-    t = min(256, n)
-    spec = pl.BlockSpec((t, m), lambda i: (i, 0))
-    return pl.pallas_call(
-        basis_body,
-        grid=(n // t,),
-        in_specs=[spec],
-        out_specs=[VMEM, VMEM],
+            num_scalar_prefetch=1, grid=(1,), in_specs=[VMEM], out_specs=[VMEM, VMEM]
+        ),
         out_shape=[pltpu.VMEM((n, m), BF16)] * 2,
-        compiler_params=params(8),
+        compiler_params=params(4),
         cost_estimate=pl.CostEstimate(flops=4 * n * m, bytes_accessed=8 * n * m, transcendentals=0),
         name="basis",
-    )(*far(basis))
-
-
-def block_solve(x, a, carry, up):
+    )(me, *near(basis))
+
+
+def block_solve(x, b, carry, up):
     sub = lax.broadcasted_iota(jnp.int32, x.shape, 0)
     edge = sub == (7 if up else 0)
     one, two = (7, 6) if up else (1, 2)
-    x = x + jnp.where(edge, a, 0.0) * carry
-    a = jnp.where(edge, 0.0, a)
-    x = x + a * pltpu.roll(x, one, 0)
-    a = a * pltpu.roll(a, one, 0)
+    x = x - jnp.where(edge, b, 0.0) * carry
+    b = jnp.where(edge, 0.0, b)
+    x = x - b * pltpu.roll(x, one, 0)
+    a = b * pltpu.roll(b, one, 0)
     x = x + a * pltpu.roll(x, two, 0)
     a = a * pltpu.roll(a, two, 0)
     x = x + a * pltpu.roll(x, 4, 0)
@@ -171,9 +196,9 @@
         carry_h, carry_r = jnp.zeros((8, wide), F32), jnp.ones((8, wide), F32)
         for t in reversed(range(blocks)):
             at = pl.ds(8 * t, 8)
-            f = -(u_ref[0, at, here] * p_ref[0, at, here])
+            f = u_ref[0, at, here] * p_ref[0, at, here]
             h = block_solve(y_ref[at], f, carry_h, True)
-            r = block_product(f, True) * carry_r
+            r = block_product(-f, True) * carry_r
             h_ref[k, at, here] = h
             r_ref[k, at, here] = r
             carry_h, carry_r = last_row(h, True), last_row(r, True)
@@ -203,50 +228,66 @@
     )(*far(lower, pinv, upper))
 
 
-def forward_body(count, me_ref, *refs):
+def forward_body(count, wide, part, me_ref, *refs):
     x_refs = refs[:count]
-    hi_ref, lo_ref, l_ref, p_ref, u_ref, g_ref, s_ref, x_all, spec = refs[count:]
+    hi_ref, lo_ref, l_hbm, p_hbm, u_hbm, g_ref, s_ref = refs[count : count + 7]
+    x_all, even, odd, l_ref, p_ref, u_ref, sems = refs[count + 7 :]
     size, rows, cols = x_refs[0].shape
     tall = size * rows
-    wide = spec.shape[1]
-    here = pl.ds(pl.multiple_of(pl.program_id(0) * wide, wide), wide)
-
-    @pl.when(pl.program_id(0) == 0)
-    def _():
-        me = me_ref[0]
-        for x in range(count):
-            at = pl.ds(pl.multiple_of((me ^ x) * cols, 128), cols)
-            hi, lo = split(x_refs[x][...].reshape(tall, cols))
-            x_all[0:tall, at] = hi
-            x_all[tall : 2 * tall, at] = lo
-
-    both = jnp.dot(x_all[...], hi_ref[:, here], preferred_element_type=F32)
-    spec[...] = (
-        both[:tall]
-        + both[tall:]
-        + jnp.dot(x_all[0:tall, :], lo_ref[:, here], preferred_element_type=F32)
-    )
     blocks = rows // 8
-    carry = [jnp.zeros((8, wide), F32)] * size
-    for t in range(blocks):
+    tiles = s_ref.shape[1] // wide
+    copies = [
+        pltpu.make_async_copy(a.at[pl.ds(part * size, size)], b, sems.at[i])
+        for i, (a, b) in enumerate(((l_hbm, l_ref), (p_hbm, p_ref), (u_hbm, u_ref)))
+    ]
+    for c in copies:
+        c.start()
+    me = me_ref[0]
+    for x in range(count):
+        at = pl.ds(pl.multiple_of((me ^ x) * cols, 128), cols)
         for k in range(size):
-            at = pl.ds(8 * t, 8)
-            into = pl.ds(k * rows + 8 * t, 8)
-            s = block_solve(spec[into], -l_ref[k, at], carry[k], False)
-            carry[k] = last_row(s, False)
-            spec[into] = p_ref[k, at] * s
-    ends = carry
-    carry = [jnp.zeros((8, wide), F32)] * size
-    for t in reversed(range(blocks)):
+            for r in range(0, rows, 16):
+                hi, lo = split(x_refs[x][k, r : r + 16])
+                x_all[k * rows + r : k * rows + r + 16, at] = hi
+                x_all[tall + k * rows + r : tall + k * rows + r + 16, at] = lo
+
+    def transform(n, spec):
+        here = slice(n * wide, (n + 1) * wide)
+        both = jnp.dot(x_all[...], hi_ref[:, here], preferred_element_type=F32)
+        third = jnp.dot(x_all[0:tall, :], lo_ref[:, here], preferred_element_type=F32)
+        spec[...] = both[:tall] + both[tall:] + third
+
+    def sweeps(n, spec):
+        here = slice(n * wide, (n + 1) * wide)
+        carry = [jnp.zeros((8, wide), F32)] * size
+        for t in range(blocks):
+            for k in range(size):
+                at = slice(8 * t, 8 * t + 8)
+                into = slice(k * rows + 8 * t, k * rows + 8 * t + 8)
+                s = block_solve(spec[into], l_ref[k, at, here], carry[k], False)
+                carry[k] = last_row(s, False)
+                spec[into] = p_ref[k, at, here] * s
         for k in range(size):
-            at = pl.ds(8 * t, 8)
-            f = -(u_ref[k, at] * p_ref[k, at])
-            g = block_solve(spec[pl.ds(k * rows + 8 * t, 8)], f, carry[k], True)
-            g_ref[k, at, here] = g
-            carry[k] = last_row(g, True)
-    for k in range(size):
-        s_ref[2 * k : 2 * k + 1, here] = ends[k][0:1]
-        s_ref[2 * k + 1 : 2 * k + 2, here] = carry[k][0:1]
+            s_ref[2 * k : 2 * k + 1, here] = carry[k][0:1]
+        carry = [jnp.zeros((8, wide), F32)] * size
+        for t in reversed(range(blocks)):
+            for k in range(size):
+                at = slice(8 * t, 8 * t + 8)
+                f = u_ref[k, at, here] * p_ref[k, at, here]
+                g = block_solve(spec[k * rows + 8 * t : k * rows + 8 * t + 8], f, carry[k], True)
+                g_ref[k, at, here] = g
+                carry[k] = last_row(g, True)
+        for k in range(size):
+            s_ref[2 * k + 1 : 2 * k + 2, here] = carry[k][0:1]
+
+    specs = (even, odd)
+    transform(0, even)
+    for c in copies:
+        c.wait()
+    for n in range(tiles):
+        if n + 1 < tiles:
+            transform(n + 1, specs[(n + 1) % 2])
+        sweeps(n, specs[n % 2])
 
 
 def forward(me, xs, hi, lo, lower, pinv, upper, part):
@@ -254,21 +295,23 @@
     size, rows, _ = xs[0].shape
     n, m = hi.shape
     t = min(512, m)
-    fac = pl.BlockSpec((size, rows, t), lambda i, me: (part, 0, i))
-    return pl.pallas_call(
-        functools.partial(forward_body, count),
+    return pl.pallas_call(
+        functools.partial(forward_body, count, t, part),
         grid_spec=pltpu.PrefetchScalarGridSpec(
             num_scalar_prefetch=1,
-            grid=(m // t,),
-            in_specs=[VMEM] * (count + 2) + [fac, fac, fac],
+            grid=(1,),
+            in_specs=[VMEM] * (count + 2) + [pl.BlockSpec(memory_space=pl.ANY)] * 3,
             out_specs=[VMEM, VMEM],
             scratch_shapes=[
                 pltpu.VMEM((2 * size * rows, n), BF16),
                 pltpu.VMEM((size * rows, t), F32),
-            ],
+                pltpu.VMEM((size * rows, t), F32),
+            ]
+            + [pltpu.VMEM((size, rows, m), F32)] * 3
+            + [pltpu.SemaphoreType.DMA((3,))],
         ),
         out_shape=[pltpu.VMEM((size, rows, m), F32), pltpu.VMEM((2 * size, m), F32)],
-        compiler_params=params(16),
+        compiler_params=params(18),
         cost_estimate=pl.CostEstimate(
             flops=6 * size * rows * n * m, bytes_accessed=4 * n * m, transcendentals=0
         ),
@@ -298,18 +341,6 @@
         d = jnp.where(low, d, c)
         out_ref[2 * k : 2 * k + 1] = hi[0:1] + d[0:1] * lo[0:1]
         out_ref[2 * k + 1 : 2 * k + 2] = lo[1:2] + r * (hi[1:2] + d[1:2] * lo[0:1])
-
-
-def small_call(body, me, args, shape):
-    return pl.pallas_call(
-        body,
-        grid_spec=pltpu.PrefetchScalarGridSpec(
-            num_scalar_prefetch=1, grid=(1,), in_specs=[VMEM] * len(args), out_specs=VMEM
-        ),
-        out_shape=pltpu.VMEM(shape, F32),
-        compiler_params=params(4),
-        cost_estimate=pl.CostEstimate(flops=1 << 20, bytes_accessed=1 << 18, transcendentals=0),
-    )(me, *near(*args))
 
 
 def spread(a, axis):
@@ -353,10 +384,14 @@
         beyond = oth[1:2] + d[1:2] * (own[0:1] + c[0:1] * e) + d[2:3] * a
         before = oth[0:1] + d[0:1] * e
         e, a = jnp.where(low, e, before), jnp.where(low, beyond, a)
-        modal = g_ref[k, :, here] + h_ref[first + k, :, here] * e + r_ref[first + k, :, here] * a
-        hi, lo = split(modal)
-        out_ref[k * rows : (k + 1) * rows, here] = hi
-        out_ref[tall + k * rows : tall + (k + 1) * rows, here] = lo
+        for r in range(0, rows, 16):
+            at = slice(r, r + 16)
+            modal = (
+                g_ref[k, at, here] + h_ref[first + k, at, here] * e + r_ref[first + k, at, here] * a
+            )
+            hi, lo = split(modal)
+            out_ref[k * rows + r : k * rows + r + 16, here] = hi
+            out_ref[tall + k * rows + r : tall + k * rows + r + 16, here] = lo
 
 
 def modal_parts(me, summaries, coefs, own, g, h, r, part):
@@ -401,7 +436,7 @@
 
 def back(me, parts, hi, lo, x, size, rows, sector):
     _, m = hi.shape
-    t = min(256, sector)
+    t = min(512, sector)
     return pl.pallas_call(
         functools.partial(back_body, x, t),
         grid_spec=pltpu.PrefetchScalarGridSpec(
@@ -419,16 +454,14 @@
     )(me, *near(parts, hi, lo))
 
 
-def place_body(count, local, first, me_ref, *refs):
-    pieces, (out_ref, sems) = refs[:count], refs[-2:]
+def place_body(xs, local, first, me_ref, *refs):
+    pieces, (out_ref, sems) = refs[: len(xs)], refs[-2:]
     size = pieces[0].shape[0]
     copies = [
         pltpu.make_async_copy(
-            pieces[x],
-            out_ref.at[pl.ds((me_ref[0] ^ x) * local + first, size)],
-            sems.at[x],
+            piece, out_ref.at[pl.ds((me_ref[0] ^ x) * local + first, size)], sems.at[i]
         )
-        for x in range(count)
+        for i, (x, piece) in enumerate(zip(xs, pieces))
     ]
     for c in copies:
         c.start()
@@ -437,25 +470,25 @@
 
 
 def place(me, pieces, out, shape, local, first):
-    count = len(pieces)
+    xs = tuple(pieces)
     extra = [] if out is None else far(out)
     return pl.pallas_call(
-        functools.partial(place_body, count, local, first),
+        functools.partial(place_body, xs, local, first),
         grid_spec=pltpu.PrefetchScalarGridSpec(
             num_scalar_prefetch=1,
             grid=(1,),
-            in_specs=[VMEM] * count + [pl.BlockSpec(memory_space=pl.ANY)] * len(extra),
+            in_specs=[VMEM] * len(xs) + [pl.BlockSpec(memory_space=pl.ANY)] * len(extra),
             out_specs=pl.BlockSpec(memory_space=pl.ANY),
-            scratch_shapes=[pltpu.SemaphoreType.DMA((count,))],
+            scratch_shapes=[pltpu.SemaphoreType.DMA((len(xs),))],
         ),
         out_shape=pltpu.HBM(shape, F32),
-        input_output_aliases={count + 1: 0} if extra else {},
+        input_output_aliases={len(xs) + 1: 0} if extra else {},
         compiler_params=params(2),
         cost_estimate=pl.CostEstimate(
-            flops=0, bytes_accessed=8 * pieces[0].size * count, transcendentals=0
+            flops=0, bytes_accessed=8 * pieces[xs[0]].size * len(xs), transcendentals=0
         ),
         name="place",
-    )(me, *near(*pieces), *extra)
+    )(me, *near(*pieces.values()), *extra)
 
 
 def per_device(forcing, mlon, mlat, weights, basis, lower, pinv, upper):
@@ -470,10 +503,13 @@
 
     ring = [(i, (i + 1) % count) for i in range(count)]
     line = [(i, i + 1) for i in range(bands - 1)]
-    south = lax.ppermute(forcing[:, rows - 1 :, :], "lat", line)
-    north = lax.ppermute(forcing[:, :1, :], "lat", [(j, i) for i, j in line])
-    west = lax.ppermute(forcing[:, :, sector - 1 :], "lon", ring)
-    east = lax.ppermute(forcing[:, :, :1], "lon", [(j, i) for i, j in ring])
+    last, first, top, bottom = small_call(
+        rim_body, me, (forcing,), [(modes, rows)] * 2 + [(modes, sector)] * 2
+    )
+    west = lax.ppermute(last, "lon", ring)
+    east = lax.ppermute(first, "lon", [(j, i) for i, j in ring])
+    south = lax.ppermute(top, "lat", line)
+    north = lax.ppermute(bottom, "lat", [(j, i) for i, j in line])
     halos = (west, east, south, north)
 
     order = farthest(count)
@@ -485,22 +521,22 @@
         me, mine = lax.optimization_barrier((me, mine))
         got = {x: exchange(mine[x], "lon", x) for x in order}
         sources.append([mine[0]] + [got[x] for x in range(1, count)])
-    me, basis, lower = lax.optimization_barrier((me, basis, lower))
-    hi, lo = basis_parts(basis)
+    me, lower = lax.optimization_barrier((me, lower))
+    hi, lo = basis_parts(me, basis)
     h, r, coef = factors(lower, pinv, upper)
     coef_other = exchange(coef, "lat", 1)
-    joined = small_call(join_coefs_body, me, (coef, coef_other), coef.shape)
+    (joined,) = small_call(join_coefs_body, me, (coef, coef_other), [coef.shape])
     coefs = spread(joined, "lat")
 
     out = None
     for part in range(groups):
         g, summary = forward(me, sources[part], hi, lo, lower, pinv, upper, part)
         other = exchange(summary, "lat", 1)
-        joined = small_call(
+        (joined,) = small_call(
             functools.partial(join_sums_body, part * size),
             me,
             (summary, other, coef, coef_other),
-            summary.shape,
+            [summary.shape],
         )
         summaries = spread(joined, "lat")
         own = (summary, other, coef, coef_other)
@@ -508,9 +544,14 @@
         pieces = {}
         for x in order + [0]:
             pieces[x] = back(me, parts, hi, lo, x, size, rows, sector)
-        me, pieces[0] = lax.optimization_barrier((me, pieces[0]))
-        pieces = [exchange(pieces[x], "lon", x) if x else pieces[x] for x in range(count)]
-        out = place(me, pieces, out, (modes, rows, sector), local, part * size)
+        last = order[max(0, len(order) - 2)]
+        me, pieces[last] = lax.optimization_barrier((me, pieces[last]))
+        got = {x: exchange(pieces[x], "lon", x) for x in order}
+        sets = [{0: pieces[0], order[0]: got[order[0]]}, {x: got[x] for x in order[1:]}]
+        if part + 1 < groups:
+            sets = [sets[0] | sets[1]]
+        for some in sets:
+            out = place(me, some, out, (modes, rows, sector), local, part * size)
     return out
 
 

time: 163 us -> 152 us (0.933)
  Pallas kernels: 78.6 us -> 69.3 us
  waiting for transfers between devices: 46.7 us -> 44 us
  starting transfers between devices: 32.8 us -> 35.3 us
  local copies, waits for them, and re-layouts: 4.41 us -> 2.2 us
    pallas_call x7 -> x6, Pallas kernels: 43.9 us -> 29.6 us  [the longest x2 21.9 us: forward(): pl.pallas_call(functools.partial(forward_body, count, t, part), grid_spec...]
    pallas_call x3 -> x6, Pallas kernels: 1.8 us -> 8.41 us  [small_call(): pl.pallas_call(body, grid_spec=pltpu.PrefetchScalarGridSpec(num_scalar_pr...]
    ppermute x24, starting transfers between devices: 24.4 us -> 28.3 us  [exchange(): return lax.ppermute(a, axis, [(i, i ^ x) for i in range(count)])]
    slice x2 -> x0, local copies, waits for them, and re-layouts: 3 us -> none  [the longest x1 1.92 us: per_device(): east = lax.ppermute(forcing[:, :, :1], 'lon', [(j, i) for i, j in ring])]
    ppermute x24, waiting for transfers between devices: 44 us -> 41.4 us  [exchange(): return lax.ppermute(a, axis, [(i, i ^ x) for i in range(count)])]
    pallas_call x8, Pallas kernels: 21 us -> 18.9 us  [back(): pl.pallas_call(functools.partial(back_body, x, t), grid_spec=pltpu.Prefet...]
  transfers between devices with their start and end apart: 28 -> 28, of which waited for: 8 -> 9; matrix products, arithmetic and copies ran while one was open for 2% -> 0% of each run, Pallas kernels for 37% -> 35%
where the time goes in v2:
time: 152 us; the launch traced here: 151 us
  Pallas kernels  69.3 us (46%)
  waiting for transfers between devices  44 us (29%)
  starting transfers between devices  35.3 us (23%)
  local copies, waits for them, and re-layouts  2.2 us (1%)
    ppermute x24, waiting for transfers between devices, exchange(): return lax.ppermute(a, axis, [(i, i ^ x) for i in range(count)])  41.4 us
    ppermute x24, starting transfers between devices, exchange(): return lax.ppermute(a, axis, [(i, i ^ x) for i in range(count)])  28.3 us
    pallas_call x2, Pallas kernels, forward(): pl.pallas_call(functools.partial(forward_body, count, t, part), grid_spec...  21.9 us
    pallas_call x8, Pallas kernels, back(): pl.pallas_call(functools.partial(back_body, x, t), grid_spec=pltpu.Prefet...  18.9 us
    pallas_call x1, Pallas kernels, factors(): pl.pallas_call(functools.partial(factors_body, t), grid=(modes,), in_spec...  9.15 us
    pallas_call x6, Pallas kernels, small_call(): pl.pallas_call(body, grid_spec=pltpu.PrefetchScalarGridSpec(num_scalar_pr...  8.41 us
    pallas_call x3, Pallas kernels, place(): pl.pallas_call(functools.partial(place_body, xs, local, first), grid_spec...  4.94 us
    pallas_call x2, Pallas kernels, modal_parts(): pl.pallas_call(functools.partial(modal_body, chips, t, part * size), grid...  3.18 us
  transfers between devices with their start and end apart: 28, of which 9 were waited for; matrix products, arithmetic and copies ran while one was open for 0% of the time, Pallas kernels for 35%

profile of v2, /device:TPU:0, one launch (start us, length us, event | category | flops | bytes accessed | tf_op | source)
XLA Modules:
  0.0 151.4 jit_solution(16169317603940030600)
XLA Ops:
  0.1 2.2 %copy-done = f32[16,128,512]{2,1,0:T(8,128)S(1)} copy-done((f32[16,128,512]{2,1,0:T(8,128)S(1)}, f32[16,128,512]{2,1,0:T(8,128)}, u32[]{:S(2)}) %copy-start) | copy-done | bytes 4194328
  2.3 1.2 shard_map.82
  3.5 2.4 %collective-permute-start.2 = (f32[16,512]{1,0:T(8,128)S(1)}, f32[16,512]{1,0:T(8,128)S(1)}, u32[]{:S(2)}, u32[]{:S(2)}) collective-permute-start(f32[16,512]{1,0:T(8,128)S(1)} %get-tuple-element.44), channel_id=1, source_target_pairs={{0,4},{4,8},{8,12},{12,16},{16,20},{20,24},{24,28},{1,5},{5,9},{9,... | collective-permute-start | bytes 98312 | tf_op jit(solution)/shard_map/ppermute | solution.py:511
  5.9 1.3 collective-permute-start.3
  7.2 2.4 %collective-permute-start = (f32[16,128]{1,0:T(8,128)S(1)}, f32[16,128]{1,0:T(8,128)S(1)}, u32[]{:S(2)}, u32[]{:S(2)}) collective-permute-start(f32[16,128]{1,0:T(8,128)S(1)} %get-tuple-element.42), channel_id=1, source_target_pairs={{0,1},{1,2},{2,3},{3,0},{4,5},{5,6},{6,7},{7,4},{8,9},{9,10},{10,1... | collective-permute-start | bytes 24584 | tf_op jit(solution)/shard_map/ppermute | solution.py:509
  9.5 1.0 collective-permute-start.1
  10.6 1.6 %collective-permute-done.west_ref = f32[16,128]{1,0:T(8,128)S(1)} collective-permute-done((f32[16,128]{1,0:T(8,128)S(1)}, f32[16,128]{1,0:T(8,128)S(1)}, u32[]{:S(2)}, u32[]{:S(2)}) %collective-permute-start) | collective-permute-done | bytes 8224 | tf_op jit(solution)/shard_map/ppermute | solution.py:509
  12.1 1.1 collective-permute-done.1.east_ref
  13.2 2.3 %shard_map.83 = (f32[2,128,512]{2,1,0:T(8,128)S(1)}, f32[2,128,512]{2,1,0:T(8,128)S(1)}, f32[2,128,512]{2,1,0:T(8,128)S(1)}, f32[2,128,512]{2,1,0:T(8,128)S(1)}) custom-call(s32[2]{0:T(128)S(1)} %pad_add_fusion.me_ref, f32[16,128,512]{2,1,0:T(8,128)S(1)} %copy-done, f32[16,128]{1,0:T(8,128)S(1)} %collective-permute-done.west_ref, ...), custom_call_target="tpu_custom_call" | custom-call | flops 1048576 | bytes 262144 | tf_op jit(solution)/shard_map/pallas_call | solution.py:49
  15.6 2.5 %collective-permute-start.4 = (f32[2,128,512]{2,1,0:T(8,128)S(1)}, f32[2,128,512]{2,1,0:T(8,128)S(1)}, u32[]{:S(2)}, u32[]{:S(2)}) collective-permute-start(f32[2,128,512]{2,1,0:T(8,128)S(1)} %get-tuple-element.58), channel_id=1, source_target_pairs={{0,1},{1,0},{2,3},{3,2},{4,5},{5,4},{6,7},{7,6},{8,9},{9,8},{10,11... | collective-permute-start | bytes 1572872 | tf_op jit(solution)/shard_map/ppermute | solution.py:32
  18.1 1.4 collective-permute-start.6
  19.6 3.1 %shard_map.84 = (f32[2,128,512]{2,1,0:T(8,128)S(1)}, f32[2,128,512]{2,1,0:T(8,128)}, f32[2,128,512]{2,1,0:T(8,128)S(1)}, f32[2,128,512]{2,1,0:T(8,128)S(1)}) custom-call(s32[2]{0:T(128)S(1)} %pad_add_fusion.me_ref, f32[16,128,512]{2,1,0:T(8,128)S(1)} %copy-done, f32[16,128]{1,0:T(8,128)S(1)} %collective-permute-done.west_ref, ...), custom_call_target="tpu_custom_call" | custom-call | flops 1048576 | bytes 262144 | tf_op jit(solution)/shard_map/pallas_call | solution.py:49
  22.6 9.2 %factors.1 = (f32[4,128,2048]{2,1,0:T(8,128)S(1)}, f32[4,128,2048]{2,1,0:T(8,128)S(1)}, f32[4,4,2048]{2,1,0:T(4,128)S(1)}) custom-call(f32[4,128,2048]{2,1,0:T(8,128)} %refs_6_.1, f32[4,128,2048]{2,1,0:T(8,128)} %refs_7_.3, f32[4,128,2048]{2,1,0:T(8,128)} %refs_8_.3), custom_call_target="tpu_custom_call" | custom-call | flops 62914560 | bytes 20971520 | tf_op jit(solution)/shard_map/factors/pallas_call | solution.py:216
  32.4 1.7 %collective-permute-start.15 = (f32[2,128,512]{2,1,0:T(8,128)}, f32[2,128,512]{2,1,0:T(8,128)S(1)}, u32[]{:S(2)}, u32[]{:S(2)}) collective-permute-start(f32[2,128,512]{2,1,0:T(8,128)} %get-tuple-element.71), channel_id=1, source_target_pairs={{0,1},{1,0},{2,3},{3,2},{4,5},{5,4},{6,7},{7,6},{8,9},{9,8},{10,11... | collective-permute-start | bytes 1572872 | tf_op jit(solution)/shard_map/ppermute | solution.py:32
  34.0 2.8 %basis.1 = (bf16[2048,2048]{1,0:T(8,128)(2,1)S(1)}, bf16[2048,2048]{1,0:T(8,128)(2,1)S(1)}) custom-call(s32[2]{0:T(128)S(1)} %pad_add_fusion.me_ref, f32[2048,2048]{1,0:T(8,128)S(1)} %copy-done.1), custom_call_target="tpu_custom_call" | custom-call | flops 16777216 | bytes 33554432 | tf_op jit(solution)/shard_map/basis/pallas_call | solution.py:143
  38.1 1.4 collective-permute-start.17
  39.4 4.6 %collective-permute-done.5.refs_2_ = f32[2,128,512]{2,1,0:T(8,128)S(1)} collective-permute-done((f32[2,128,512]{2,1,0:T(8,128)S(1)}, f32[2,128,512]{2,1,0:T(8,128)S(1)}, u32[]{:S(2)}, u32[]{:S(2)}) %collective-permute-start.5) | collective-permute-done | bytes 524320 | tf_op jit(solution)/shard_map/ppermute | solution.py:32
  44.0 1.1 collective-permute-start.14
  45.2 10.9 %forward.2 = (f32[2,128,2048]{2,1,0:T(8,128)S(1)}, f32[4,2048]{1,0:T(4,128)S(1)}) custom-call(s32[2]{0:T(128)S(1)} %pad_add_fusion.me_ref, f32[2,128,512]{2,1,0:T(8,128)S(1)} %get-tuple-element.57.refs_0_, f32[2,128,512]{2,1,0:T(8,128)S(1)} %collective-permute-done.4.refs_1_, f32[2,128,512]{2,1,0:T(8,128)S(1)} %collective-permute-done.5.refs_2_, ...), custom_call_target="tpu_custom_call" | custom-call | flops 6442450944 | bytes 16777216 | tf_op jit(solution)/shard_map/forward/pallas_call | solution.py:298
  56.2 2.7 %collective-permute-start.13 = (f32[4,4,2048]{2,1,0:T(4,128)S(1)}, f32[4,4,2048]{2,1,0:T(4,128)S(1)}, u32[]{:S(2)}, u32[]{:S(2)}) collective-permute-start(f32[4,4,2048]{2,1,0:T(4,128)S(1)} %shard_map.86.refs_4_), channel_id=1, source_target_pairs={{0,16},{4,20},{8,24},{12,28},{16,0},{20,4},{24,8},{28,12},{1,17},{... | collective-permute-start | bytes 393224 | tf_op jit(solution)/shard_map/ppermute | solution.py:32
  58.9 1.3 collective-permute-start.12
  60.8 5.1 %collective-permute-done.13.refs_6_ = f32[4,4,2048]{2,1,0:T(4,128)S(1)} collective-permute-done((f32[4,4,2048]{2,1,0:T(4,128)S(1)}, f32[4,4,2048]{2,1,0:T(4,128)S(1)}, u32[]{:S(2)}, u32[]{:S(2)}) %collective-permute-start.13) | collective-permute-done | bytes 131104 | tf_op jit(solution)/shard_map/ppermute | solution.py:32
  65.9 3.2 %collective-permute-start.11 = (f32[4,2048]{1,0:T(4,128)S(1)}, f32[4,2048]{1,0:T(4,128)S(1)}, u32[]{:S(2)}, u32[]{:S(2)}) collective-permute-start(f32[4,2048]{1,0:T(4,128)S(1)} %shard_map.85.refs_0_), channel_id=1, source_target_pairs={{0,24},{4,28},{8,16},{12,20},{16,8},{20,12},{24,0},{28,4},{1,25},{... | collective-permute-start | bytes 98312 | tf_op jit(solution)/shard_map/ppermute | solution.py:32
  69.1 2.5 %collective-permute-done.11.refs_3_ = f32[4,2048]{1,0:T(4,128)S(1)} collective-permute-done((f32[4,2048]{1,0:T(4,128)S(1)}, f32[4,2048]{1,0:T(4,128)S(1)}, u32[]{:S(2)}, u32[]{:S(2)}) %collective-permute-start.11) | collective-permute-done | bytes 32800 | tf_op jit(solution)/shard_map/ppermute | solution.py:32
  71.6 2.3 %collective-permute-done.10.refs_2_ = f32[4,2048]{1,0:T(4,128)S(1)} collective-permute-done((f32[4,2048]{1,0:T(4,128)S(1)}, f32[4,2048]{1,0:T(4,128)S(1)}, u32[]{:S(2)}, u32[]{:S(2)}) %collective-permute-start.10) | collective-permute-done | bytes 32800 | tf_op jit(solution)/shard_map/ppermute | solution.py:32
  73.9 1.6 %collective-permute-done.9.refs_1_ = f32[4,2048]{1,0:T(4,128)S(1)} collective-permute-done((f32[4,2048]{1,0:T(4,128)S(1)}, f32[4,2048]{1,0:T(4,128)S(1)}, u32[]{:S(2)}, u32[]{:S(2)}) %collective-permute-start.9) | collective-permute-done | bytes 32800 | tf_op jit(solution)/shard_map/ppermute | solution.py:32
  75.5 1.6 %modal.2.m_ref = bf16[512,2048]{1,0:T(8,128)(2,1)S(1)} custom-call(s32[2]{0:T(128)S(1)} %pad_add_fusion.me_ref, f32[4,2048]{1,0:T(4,128)S(1)} %shard_map.85.refs_0_, f32[4,2048]{1,0:T(4,128)S(1)} %collective-permute-done.9.refs_1_, f32[4,2048]{1,0:T(4,128)S(1)} %collective-permute-done.10.refs_2_, f32[4,2048]{1,0:T(4,128)S(1)} %collective-permute-done.11.refs_3_, ...), custom_call_target="tpu_custom_call" | custom-call | flops 5242880 | bytes 8388608 | tf_op jit(solution)/shard_map/modal/pallas_call | solution.py:401
  77.1 2.4 %back.8 = f32[2,128,512]{2,1,0:T(8,128)S(1)} custom-call(s32[2]{0:T(128)S(1)} %pad_add_fusion.me_ref, bf16[512,2048]{1,0:T(8,128)(2,1)S(1)} %modal.2.m_ref, bf16[2048,2048]{1,0:T(8,128)(2,1)S(1)} %get-tuple-element.61.refs_4_.hi_ref, bf16[2048,2048]{1,0:T(8,128)(2,1)S(1)} %get-tuple-element.62.refs_5_.lo_ref), custom_call_target="tpu_custom_call" | custom-call | flops 1610612736 | bytes 4194304 | tf_op jit(solution)/shard_map/back/pallas_call | solution.py:440
  79.5 10.9 %forward.3 = (f32[2,128,2048]{2,1,0:T(8,128)S(1)}, f32[4,2048]{1,0:T(4,128)S(1)}) custom-call(s32[2]{0:T(128)S(1)} %pad_add_fusion.me_ref, f32[2,128,512]{2,1,0:T(8,128)S(1)} %get-tuple-element.70.refs_0_, f32[2,128,512]{2,1,0:T(8,128)S(1)} %collective-permute-done.15.refs_1_, f32[2,128,512]{2,1,0:T(8,128)S(1)} %collective-permute-done.16.refs_2_, ...), custom_call_target="tpu_custom_call" | custom-call | flops 6442450944 | bytes 16777216 | tf_op jit(solution)/shard_map/forward/pallas_call | solution.py:298
  90.5 2.4 %back.15 = f32[2,128,512]{2,1,0:T(8,128)S(1)} custom-call(s32[2]{0:T(128)S(1)} %pad_add_fusion.me_ref, bf16[512,2048]{1,0:T(8,128)(2,1)S(1)} %modal.2.m_ref, bf16[2048,2048]{1,0:T(8,128)(2,1)S(1)} %get-tuple-element.61.refs_4_.hi_ref, bf16[2048,2048]{1,0:T(8,128)(2,1)S(1)} %get-tuple-element.62.refs_5_.lo_ref), custom_call_target="tpu_custom_call" | custom-call | flops 1610612736 | bytes 4194304 | tf_op jit(solution)/shard_map/back/pallas_call | solution.py:440
  92.9 2.0 %collective-permute-start.26 = (f32[2,128,512]{2,1,0:T(8,128)S(1)}, f32[2,128,512]{2,1,0:T(8,128)S(1)}, u32[]{:S(2)}, u32[]{:S(2)}) collective-permute-start(f32[2,128,512]{2,1,0:T(8,128)S(1)} %back.8), channel_id=1, source_target_pairs={{0,1},{1,0},{2,3},{3,2},{4,5},{5,4},{6,7},{7,6},{8,9},{9,8},{10,11... | collective-permute-start | bytes 1572872 | tf_op jit(solution)/shard_map/ppermute | solution.py:32
  95.5 2.7 %collective-permute-start.21 = (f32[4,2048]{1,0:T(4,128)S(1)}, f32[4,2048]{1,0:T(4,128)S(1)}, u32[]{:S(2)}, u32[]{:S(2)}) collective-permute-start(f32[4,2048]{1,0:T(4,128)S(1)} %shard_map.87.refs_0_), channel_id=1, source_target_pairs={{0,24},{4,28},{8,16},{12,20},{16,8},{20,12},{24,0},{28,4},{1,25},{... | collective-permute-start | bytes 98312 | tf_op jit(solution)/shard_map/ppermute | solution.py:32
  98.2 1.7 %collective-permute-start.19 = (f32[4,2048]{1,0:T(4,128)S(1)}, f32[4,2048]{1,0:T(4,128)S(1)}, u32[]{:S(2)}, u32[]{:S(2)}) collective-permute-start(f32[4,2048]{1,0:T(4,128)S(1)} %shard_map.87.refs_0_), channel_id=1, source_target_pairs={{0,8},{4,12},{8,0},{12,4},{16,24},{20,28},{24,16},{28,20},{1,9},{5... | collective-permute-start | bytes 98312 | tf_op jit(solution)/shard_map/ppermute | solution.py:32
  100.0 2.4 %back.14 = f32[2,128,512]{2,1,0:T(8,128)S(1)} custom-call(s32[2]{0:T(128)S(1)} %pad_add_fusion.me_ref, bf16[512,2048]{1,0:T(8,128)(2,1)S(1)} %modal.2.m_ref, bf16[2048,2048]{1,0:T(8,128)(2,1)S(1)} %get-tuple-element.61.refs_4_.hi_ref, bf16[2048,2048]{1,0:T(8,128)(2,1)S(1)} %get-tuple-element.62.refs_5_.lo_ref), custom_call_target="tpu_custom_call" | custom-call | flops 1610612736 | bytes 4194304 | tf_op jit(solution)/shard_map/back/pallas_call | solution.py:440
  103.0 0.9 collective-permute-start.27
  104.0 1.6 %modal.3.m_ref = bf16[512,2048]{1,0:T(8,128)(2,1)S(1)} custom-call(s32[2]{0:T(128)S(1)} %pad_add_fusion.me_ref, f32[4,2048]{1,0:T(4,128)S(1)} %shard_map.87.refs_0_, f32[4,2048]{1,0:T(4,128)S(1)} %collective-permute-done.19.refs_1_, f32[4,2048]{1,0:T(4,128)S(1)} %collective-permute-done.20.refs_2_, f32[4,2048]{1,0:T(4,128)S(1)} %collective-permute-done.21.refs_3_, ...), custom_call_target="tpu_custom_call" | custom-call | flops 5242880 | bytes 8388608 | tf_op jit(solution)/shard_map/modal/pallas_call | solution.py:401
  105.6 2.4 %back.12 = f32[2,128,512]{2,1,0:T(8,128)S(1)} custom-call(s32[2]{0:T(128)S(1)} %pad_add_fusion.me_ref, bf16[512,2048]{1,0:T(8,128)(2,1)S(1)} %modal.3.m_ref, bf16[2048,2048]{1,0:T(8,128)(2,1)S(1)} %get-tuple-element.61.refs_4_.hi_ref, bf16[2048,2048]{1,0:T(8,128)(2,1)S(1)} %get-tuple-element.62.refs_5_.lo_ref), custom_call_target="tpu_custom_call" | custom-call | flops 1610612736 | bytes 4194304 | tf_op jit(solution)/shard_map/back/pallas_call | solution.py:440
  108.0 2.4 %back.10 = f32[2,128,512]{2,1,0:T(8,128)S(1)} custom-call(s32[2]{0:T(128)S(1)} %pad_add_fusion.me_ref, bf16[512,2048]{1,0:T(8,128)(2,1)S(1)} %modal.3.m_ref, bf16[2048,2048]{1,0:T(8,128)(2,1)S(1)} %get-tuple-element.61.refs_4_.hi_ref, bf16[2048,2048]{1,0:T(8,128)(2,1)S(1)} %get-tuple-element.62.refs_5_.lo_ref), custom_call_target="tpu_custom_call" | custom-call | flops 1610612736 | bytes 4194304 | tf_op jit(solution)/shard_map/back/pallas_call | solution.py:440
  110.3 2.4 %back.9 = f32[2,128,512]{2,1,0:T(8,128)S(1)} custom-call(s32[2]{0:T(128)S(1)} %pad_add_fusion.me_ref, bf16[512,2048]{1,0:T(8,128)(2,1)S(1)} %modal.3.m_ref, bf16[2048,2048]{1,0:T(8,128)(2,1)S(1)} %get-tuple-element.61.refs_4_.hi_ref, bf16[2048,2048]{1,0:T(8,128)(2,1)S(1)} %get-tuple-element.62.refs_5_.lo_ref), custom_call_target="tpu_custom_call" | custom-call | flops 1610612736 | bytes 4194304 | tf_op jit(solution)/shard_map/back/pallas_call | solution.py:440
  112.7 2.3 %collective-permute-start.24 = (f32[2,128,512]{2,1,0:T(8,128)S(1)}, f32[2,128,512]{2,1,0:T(8,128)S(1)}, u32[]{:S(2)}, u32[]{:S(2)}) collective-permute-start(f32[2,128,512]{2,1,0:T(8,128)S(1)} %back.12), channel_id=1, source_target_pairs={{0,3},{1,2},{2,1},{3,0},{4,7},{5,6},{6,5},{7,4},{8,11},{9,10},{10,... | collective-permute-start | bytes 1572872 | tf_op jit(solution)/shard_map/ppermute | solution.py:32
  115.3 0.9 collective-permute-start.23
  116.2 2.4 %back.13.refs_0_ = f32[2,128,512]{2,1,0:T(8,128)S(1)} custom-call(s32[2]{0:T(128)S(1)} %pad_add_fusion.me_ref, bf16[512,2048]{1,0:T(8,128)(2,1)S(1)} %modal.2.m_ref, bf16[2048,2048]{1,0:T(8,128)(2,1)S(1)} %get-tuple-element.61.refs_4_.hi_ref, bf16[2048,2048]{1,0:T(8,128)(2,1)S(1)} %get-tuple-element.62.refs_5_.lo_ref), custom_call_target="tpu_custom_call" | custom-call | flops 1610612736 | bytes 4194304 | tf_op jit(solution)/shard_map/back/pallas_call | solution.py:440
  118.6 2.4 %back.11.refs_0_ = f32[2,128,512]{2,1,0:T(8,128)S(1)} custom-call(s32[2]{0:T(128)S(1)} %pad_add_fusion.me_ref, bf16[512,2048]{1,0:T(8,128)(2,1)S(1)} %modal.3.m_ref, bf16[2048,2048]{1,0:T(8,128)(2,1)S(1)} %get-tuple-element.61.refs_4_.hi_ref, bf16[2048,2048]{1,0:T(8,128)(2,1)S(1)} %get-tuple-element.62.refs_5_.lo_ref), custom_call_target="tpu_custom_call" | custom-call | flops 1610612736 | bytes 4194304 | tf_op jit(solution)/shard_map/back/pallas_call | solution.py:440
  121.0 19.3 %collective-permute-done.27.refs_3_ = f32[2,128,512]{2,1,0:T(8,128)S(1)} collective-permute-done((f32[2,128,512]{2,1,0:T(8,128)S(1)}, f32[2,128,512]{2,1,0:T(8,128)S(1)}, u32[]{:S(2)}, u32[]{:S(2)}) %collective-permute-start.27) | collective-permute-done | bytes 524320 | tf_op jit(solution)/shard_map/ppermute | solution.py:32
  140.3 1.9 %place.3.refs_2_ = f32[16,128,512]{2,1,0:T(8,128)} custom-call(s32[2]{0:T(128)S(1)} %pad_add_fusion.me_ref, f32[2,128,512]{2,1,0:T(8,128)S(1)} %back.13.refs_0_, f32[2,128,512]{2,1,0:T(8,128)S(1)} %collective-permute-done.25.refs_1_, f32[2,128,512]{2,1,0:T(8,128)S(1)} %collective-permute-done.26.refs_2_, f32[2,128,512]{2,1,0:T(8,128)S(1)} %collective-permute-done.27.refs_3_), custom_call_target="tpu_custom_call" | custom-call | bytes 4194304 | tf_op jit(solution)/shard_map/place/pallas_call | solution.py:475
  142.2 1.5 %place.4.refs_2_ = f32[16,128,512]{2,1,0:T(8,128)} custom-call(s32[2]{0:T(128)S(1)} %pad_add_fusion.me_ref, f32[2,128,512]{2,1,0:T(8,128)S(1)} %back.11.refs_0_, f32[2,128,512]{2,1,0:T(8,128)S(1)} %collective-permute-done.24.refs_1_, f32[16,128,512]{2,1,0:T(8,128)} %place.3.refs_2_), custom_call_target="tpu_custom_call", output_to_operand_aliasing={{}: (3, {})} | custom-call | bytes 2097152 | tf_op jit(solution)/shard_map/place/pallas_call | solution.py:475
  143.7 5.9 %collective-permute-done.23.refs_1_ = f32[2,128,512]{2,1,0:T(8,128)S(1)} collective-permute-done((f32[2,128,512]{2,1,0:T(8,128)S(1)}, f32[2,128,512]{2,1,0:T(8,128)S(1)}, u32[]{:S(2)}, u32[]{:S(2)}) %collective-permute-start.23) | collective-permute-done | bytes 524320 | tf_op jit(solution)/shard_map/ppermute | solution.py:32
  149.7 1.5 %place.5 = f32[16,128,512]{2,1,0:T(8,128)} custom-call(s32[2]{0:T(128)S(1)} %pad_add_fusion.me_ref, f32[2,128,512]{2,1,0:T(8,128)S(1)} %collective-permute-done.22.refs_0_, f32[2,128,512]{2,1,0:T(8,128)S(1)} %collective-permute-done.23.refs_1_, f32[16,128,512]{2,1,0:T(8,128)} %place.4.refs_2_), custom_call_target="tpu_custom_call", output_to_operand_aliasing={{}: (3, {})} | custom-call | bytes 2097152 | tf_op jit(solution)/shard_map/place/pallas_call | solution.py:475
  (42 shorter events, 4.3 us)
Async XLA Ops:
  0.0 13.2 %copy-start.4 = (f32[512]{0:T(512)S(1)}, f32[512]{0:T(512)}, u32[]{:S(2)}) copy-start(f32[512]{0:T(512)} %param.11) | copy-start | bytes 6148
  0.1 2.2 %copy-start = (f32[16,128,512]{2,1,0:T(8,128)S(1)}, f32[16,128,512]{2,1,0:T(8,128)}, u32[]{:S(2)}) copy-start(f32[16,128,512]{2,1,0:T(8,128)} %f_ref.5) | copy-start | bytes 12582916
  2.3 10.9 %copy-start.2 = (f32[128,512]{1,0:T(8,128)S(1)}, f32[128,512]{1,0:T(8,128)}, u32[]{:S(2)}) copy-start(f32[128,512]{1,0:T(8,128)} %refs_0_.3) | copy-start | bytes 786436
  2.3 11.0 %copy-start.3 = (f32[128,512]{1,0:T(8,128)S(1)}, f32[128,512]{1,0:T(8,128)}, u32[]{:S(2)}) copy-start(f32[128,512]{1,0:T(8,128)} %refs_1_.3) | copy-start | bytes 786436
  3.5 9.7 %collective-permute-start.2 = (f32[16,512]{1,0:T(8,128)S(1)}, f32[16,512]{1,0:T(8,128)S(1)}, u32[]{:S(2)}, u32[]{:S(2)}) collective-permute-start(f32[16,512]{1,0:T(8,128)S(1)} %get-tuple-element.44), channel_id=1, source_target_pairs={{0,4},{4,8},{8,12},{12,16},{16,20},{20,24},{24,28},{1,5},{5,9},{9,... | collective-permute-start | bytes 98312 | tf_op jit(solution)/shard_map/ppermute | solution.py:511
  5.9 7.3 %collective-permute-start.3 = (f32[16,512]{1,0:T(8,128)S(1)}, f32[16,512]{1,0:T(8,128)S(1)}, u32[]{:S(2)}, u32[]{:S(2)}) collective-permute-start(f32[16,512]{1,0:T(8,128)S(1)} %get-tuple-element.45), channel_id=1, source_target_pairs={{4,0},{8,4},{12,8},{16,12},{20,16},{24,20},{28,24},{5,1},{9,5},{13... | collective-permute-start | bytes 98312 | tf_op jit(solution)/shard_map/ppermute | solution.py:512
  7.2 4.9 %collective-permute-start = (f32[16,128]{1,0:T(8,128)S(1)}, f32[16,128]{1,0:T(8,128)S(1)}, u32[]{:S(2)}, u32[]{:S(2)}) collective-permute-start(f32[16,128]{1,0:T(8,128)S(1)} %get-tuple-element.42), channel_id=1, source_target_pairs={{0,1},{1,2},{2,3},{3,0},{4,5},{5,6},{6,7},{7,4},{8,9},{9,10},{10,1... | collective-permute-start | bytes 24584 | tf_op jit(solution)/shard_map/ppermute | solution.py:509
  9.5 3.7 %collective-permute-start.1 = (f32[16,128]{1,0:T(8,128)S(1)}, f32[16,128]{1,0:T(8,128)S(1)}, u32[]{:S(2)}, u32[]{:S(2)}) collective-permute-start(f32[16,128]{1,0:T(8,128)S(1)} %get-tuple-element.43), channel_id=1, source_target_pairs={{1,0},{2,1},{3,2},{0,3},{5,4},{6,5},{7,6},{4,7},{9,8},{10,9},{11,1... | collective-permute-start | bytes 24584 | tf_op jit(solution)/shard_map/ppermute | solution.py:510
  15.6 22.5 %collective-permute-start.4 = (f32[2,128,512]{2,1,0:T(8,128)S(1)}, f32[2,128,512]{2,1,0:T(8,128)S(1)}, u32[]{:S(2)}, u32[]{:S(2)}) collective-permute-start(f32[2,128,512]{2,1,0:T(8,128)S(1)} %get-tuple-element.58), channel_id=1, source_target_pairs={{0,1},{1,0},{2,3},{3,2},{4,5},{5,4},{6,7},{7,6},{8,9},{9,8},{10,11... | collective-permute-start | bytes 1572872 | tf_op jit(solution)/shard_map/ppermute | solution.py:32
  18.0 26.0 %collective-permute-start.5 = (f32[2,128,512]{2,1,0:T(8,128)S(1)}, f32[2,128,512]{2,1,0:T(8,128)S(1)}, u32[]{:S(2)}, u32[]{:S(2)}) collective-permute-start(f32[2,128,512]{2,1,0:T(8,128)S(1)} %get-tuple-element.59), channel_id=1, source_target_pairs={{0,2},{1,3},{2,0},{3,1},{4,6},{5,7},{6,4},{7,5},{8,10},{9,11},{10,... | collective-permute-start | bytes 1572872 | tf_op jit(solution)/shard_map/ppermute | solution.py:32
  18.1 27.1 %collective-permute-start.6 = (f32[2,128,512]{2,1,0:T(8,128)S(1)}, f32[2,128,512]{2,1,0:T(8,128)S(1)}, u32[]{:S(2)}, u32[]{:S(2)}) collective-permute-start(f32[2,128,512]{2,1,0:T(8,128)S(1)} %get-tuple-element.60), channel_id=1, source_target_pairs={{0,3},{1,2},{2,1},{3,0},{4,7},{5,6},{6,5},{7,4},{8,11},{9,10},{10,... | collective-permute-start | bytes 1572872 | tf_op jit(solution)/shard_map/ppermute | solution.py:32
  19.6 14.5 %copy-start.1 = (f32[2048,2048]{1,0:T(8,128)S(1)}, f32[2048,2048]{1,0:T(8,128)}, u32[]{:S(2)}) copy-start(f32[2048,2048]{1,0:T(8,128)} %e_ref.1) | copy-start | bytes 50331652
  31.8 5.0 %collective-permute-start.8 = (f32[4,4,2048]{2,1,0:T(4,128)S(1)}, f32[4,4,2048]{2,1,0:T(4,128)S(1)}, u32[]{:S(2)}, u32[]{:S(2)}) collective-permute-start(f32[4,4,2048]{2,1,0:T(4,128)S(1)} %get-tuple-element.65.c_own_ref.own_ref.refs_10_), channel_id=1, source_target_pairs={{0,4},{4,0},{8,12},{12,8},{16,20},{20,16},{24,28},{28,24},{1,5},{5... | collective-permute-start | bytes 393224 | tf_op jit(solution)/shard_map/ppermute | solution.py:32
  32.4 47.1 %collective-permute-start.15 = (f32[2,128,512]{2,1,0:T(8,128)}, f32[2,128,512]{2,1,0:T(8,128)S(1)}, u32[]{:S(2)}, u32[]{:S(2)}) collective-permute-start(f32[2,128,512]{2,1,0:T(8,128)} %get-tuple-element.71), channel_id=1, source_target_pairs={{0,1},{1,0},{2,3},{3,2},{4,5},{5,4},{6,7},{7,6},{8,9},{9,8},{10,11... | collective-permute-start | bytes 1572872 | tf_op jit(solution)/shard_map/ppermute | solution.py:32
  36.9 42.6 %collective-permute-start.16 = (f32[2,128,512]{2,1,0:T(8,128)S(1)}, f32[2,128,512]{2,1,0:T(8,128)S(1)}, u32[]{:S(2)}, u32[]{:S(2)}) collective-permute-start(f32[2,128,512]{2,1,0:T(8,128)S(1)} %get-tuple-element.72), channel_id=1, source_target_pairs={{0,2},{1,3},{2,0},{3,1},{4,6},{5,7},{6,4},{7,5},{8,10},{9,11},{10,... | collective-permute-start | bytes 1572872 | tf_op jit(solution)/shard_map/ppermute | solution.py:32
  38.1 41.4 %collective-permute-start.17 = (f32[2,128,512]{2,1,0:T(8,128)S(1)}, f32[2,128,512]{2,1,0:T(8,128)S(1)}, u32[]{:S(2)}, u32[]{:S(2)}) collective-permute-start(f32[2,128,512]{2,1,0:T(8,128)S(1)} %get-tuple-element.73), channel_id=1, source_target_pairs={{0,3},{1,2},{2,1},{3,0},{4,7},{5,6},{6,5},{7,4},{8,11},{9,10},{10,... | collective-permute-start | bytes 1572872 | tf_op jit(solution)/shard_map/ppermute | solution.py:32
  44.0 12.1 %collective-permute-start.14 = (f32[4,4,2048]{2,1,0:T(4,128)S(1)}, f32[4,4,2048]{2,1,0:T(4,128)S(1)}, u32[]{:S(2)}, u32[]{:S(2)}) collective-permute-start(f32[4,4,2048]{2,1,0:T(4,128)S(1)} %shard_map.86.refs_4_), channel_id=1, source_target_pairs={{0,24},{4,28},{8,16},{12,20},{16,8},{20,12},{24,0},{28,4},{1,25},{... | collective-permute-start | bytes 393224 | tf_op jit(solution)/shard_map/ppermute | solution.py:32
  56.1 2.8 %collective-permute-start.7 = (f32[4,2048]{1,0:T(4,128)S(1)}, f32[4,2048]{1,0:T(4,128)S(1)}, u32[]{:S(2)}, u32[]{:S(2)}) collective-permute-start(f32[4,2048]{1,0:T(4,128)S(1)} %get-tuple-element.64.own_ref.refs_8_), channel_id=1, source_target_pairs={{0,4},{4,0},{8,12},{12,8},{16,20},{20,16},{24,28},{28,24},{1,5},{5... | collective-permute-start | bytes 98312 | tf_op jit(solution)/shard_map/ppermute | solution.py:32
  56.2 9.7 %collective-permute-start.13 = (f32[4,4,2048]{2,1,0:T(4,128)S(1)}, f32[4,4,2048]{2,1,0:T(4,128)S(1)}, u32[]{:S(2)}, u32[]{:S(2)}) collective-permute-start(f32[4,4,2048]{2,1,0:T(4,128)S(1)} %shard_map.86.refs_4_), channel_id=1, source_target_pairs={{0,16},{4,20},{8,24},{12,28},{16,0},{20,4},{24,8},{28,12},{1,17},{... | collective-permute-start | bytes 393224 | tf_op jit(solution)/shard_map/ppermute | solution.py:32
  58.9 10.2 %collective-permute-start.12 = (f32[4,4,2048]{2,1,0:T(4,128)S(1)}, f32[4,4,2048]{2,1,0:T(4,128)S(1)}, u32[]{:S(2)}, u32[]{:S(2)}) collective-permute-start(f32[4,4,2048]{2,1,0:T(4,128)S(1)} %shard_map.86.refs_4_), channel_id=1, source_target_pairs={{0,8},{4,12},{8,0},{12,4},{16,24},{20,28},{24,16},{28,20},{1,9},{5... | collective-permute-start | bytes 393224 | tf_op jit(solution)/shard_map/ppermute | solution.py:32
  65.9 5.7 %collective-permute-start.11 = (f32[4,2048]{1,0:T(4,128)S(1)}, f32[4,2048]{1,0:T(4,128)S(1)}, u32[]{:S(2)}, u32[]{:S(2)}) collective-permute-start(f32[4,2048]{1,0:T(4,128)S(1)} %shard_map.85.refs_0_), channel_id=1, source_target_pairs={{0,24},{4,28},{8,16},{12,20},{16,8},{20,12},{24,0},{28,4},{1,25},{... | collective-permute-start | bytes 98312 | tf_op jit(solution)/shard_map/ppermute | solution.py:32
  69.1 4.8 %collective-permute-start.10 = (f32[4,2048]{1,0:T(4,128)S(1)}, f32[4,2048]{1,0:T(4,128)S(1)}, u32[]{:S(2)}, u32[]{:S(2)}) collective-permute-start(f32[4,2048]{1,0:T(4,128)S(1)} %shard_map.85.refs_0_), channel_id=1, source_target_pairs={{0,16},{4,20},{8,24},{12,28},{16,0},{20,4},{24,8},{28,12},{1,17},{... | collective-permute-start | bytes 98312 | tf_op jit(solution)/shard_map/ppermute | solution.py:32
  71.6 3.9 %collective-permute-start.9 = (f32[4,2048]{1,0:T(4,128)S(1)}, f32[4,2048]{1,0:T(4,128)S(1)}, u32[]{:S(2)}, u32[]{:S(2)}) collective-permute-start(f32[4,2048]{1,0:T(4,128)S(1)} %shard_map.85.refs_0_), channel_id=1, source_target_pairs={{0,8},{4,12},{8,0},{12,4},{16,24},{20,28},{24,16},{28,20},{1,9},{5... | collective-permute-start | bytes 98312 | tf_op jit(solution)/shard_map/ppermute | solution.py:32
  90.5 4.5 %collective-permute-start.18 = (f32[4,2048]{1,0:T(4,128)S(1)}, f32[4,2048]{1,0:T(4,128)S(1)}, u32[]{:S(2)}, u32[]{:S(2)}) collective-permute-start(f32[4,2048]{1,0:T(4,128)S(1)} %get-tuple-element.74.own_ref.refs_8_), channel_id=1, source_target_pairs={{0,4},{4,0},{8,12},{12,8},{16,20},{20,16},{24,28},{28,24},{1,5},{5... | collective-permute-start | bytes 98312 | tf_op jit(solution)/shard_map/ppermute | solution.py:32
  92.9 22.4 %collective-permute-start.26 = (f32[2,128,512]{2,1,0:T(8,128)S(1)}, f32[2,128,512]{2,1,0:T(8,128)S(1)}, u32[]{:S(2)}, u32[]{:S(2)}) collective-permute-start(f32[2,128,512]{2,1,0:T(8,128)S(1)} %back.8), channel_id=1, source_target_pairs={{0,1},{1,0},{2,3},{3,2},{4,5},{5,4},{6,7},{7,6},{8,9},{9,8},{10,11... | collective-permute-start | bytes 1572872 | tf_op jit(solution)/shard_map/ppermute | solution.py:32
  95.5 7.5 %collective-permute-start.21 = (f32[4,2048]{1,0:T(4,128)S(1)}, f32[4,2048]{1,0:T(4,128)S(1)}, u32[]{:S(2)}, u32[]{:S(2)}) collective-permute-start(f32[4,2048]{1,0:T(4,128)S(1)} %shard_map.87.refs_0_), channel_id=1, source_target_pairs={{0,24},{4,28},{8,16},{12,20},{16,8},{20,12},{24,0},{28,4},{1,25},{... | collective-permute-start | bytes 98312 | tf_op jit(solution)/shard_map/ppermute | solution.py:32
  98.2 5.7 %collective-permute-start.20 = (f32[4,2048]{1,0:T(4,128)S(1)}, f32[4,2048]{1,0:T(4,128)S(1)}, u32[]{:S(2)}, u32[]{:S(2)}) collective-permute-start(f32[4,2048]{1,0:T(4,128)S(1)} %shard_map.87.refs_0_), channel_id=1, source_target_pairs={{0,16},{4,20},{8,24},{12,28},{16,0},{20,4},{24,8},{28,12},{1,17},{... | collective-permute-start | bytes 98312 | tf_op jit(solution)/shard_map/ppermute | solution.py:32
  98.2 5.7 %collective-permute-start.19 = (f32[4,2048]{1,0:T(4,128)S(1)}, f32[4,2048]{1,0:T(4,128)S(1)}, u32[]{:S(2)}, u32[]{:S(2)}) collective-permute-start(f32[4,2048]{1,0:T(4,128)S(1)} %shard_map.87.refs_0_), channel_id=1, source_target_pairs={{0,8},{4,12},{8,0},{12,4},{16,24},{20,28},{24,16},{28,20},{1,9},{5... | collective-permute-start | bytes 98312 | tf_op jit(solution)/shard_map/ppermute | solution.py:32
  102.3 18.6 %collective-permute-start.25 = (f32[2,128,512]{2,1,0:T(8,128)S(1)}, f32[2,128,512]{2,1,0:T(8,128)S(1)}, u32[]{:S(2)}, u32[]{:S(2)}) collective-permute-start(f32[2,128,512]{2,1,0:T(8,128)S(1)} %back.14), channel_id=1, source_target_pairs={{0,3},{1,2},{2,1},{3,0},{4,7},{5,6},{6,5},{7,4},{8,11},{9,10},{10,... | collective-permute-start | bytes 1572872 | tf_op jit(solution)/shard_map/ppermute | solution.py:32
  103.0 37.3 %collective-permute-start.27 = (f32[2,128,512]{2,1,0:T(8,128)S(1)}, f32[2,128,512]{2,1,0:T(8,128)S(1)}, u32[]{:S(2)}, u32[]{:S(2)}) collective-permute-start(f32[2,128,512]{2,1,0:T(8,128)S(1)} %back.15), channel_id=1, source_target_pairs={{0,2},{1,3},{2,0},{3,1},{4,6},{5,7},{6,4},{7,5},{8,10},{9,11},{10,... | collective-permute-start | bytes 1572872 | tf_op jit(solution)/shard_map/ppermute | solution.py:32
  112.7 29.5 %collective-permute-start.24 = (f32[2,128,512]{2,1,0:T(8,128)S(1)}, f32[2,128,512]{2,1,0:T(8,128)S(1)}, u32[]{:S(2)}, u32[]{:S(2)}) collective-permute-start(f32[2,128,512]{2,1,0:T(8,128)S(1)} %back.12), channel_id=1, source_target_pairs={{0,3},{1,2},{2,1},{3,0},{4,7},{5,6},{6,5},{7,4},{8,11},{9,10},{10,... | collective-permute-start | bytes 1572872 | tf_op jit(solution)/shard_map/ppermute | solution.py:32
  115.0 28.7 %collective-permute-start.22 = (f32[2,128,512]{2,1,0:T(8,128)S(1)}, f32[2,128,512]{2,1,0:T(8,128)S(1)}, u32[]{:S(2)}, u32[]{:S(2)}) collective-permute-start(f32[2,128,512]{2,1,0:T(8,128)S(1)} %back.9), channel_id=1, source_target_pairs={{0,1},{1,0},{2,3},{3,2},{4,5},{5,4},{6,7},{7,6},{8,9},{9,8},{10,11... | collective-permute-start | bytes 1572872 | tf_op jit(solution)/shard_map/ppermute | solution.py:32
  115.3 34.4 %collective-permute-start.23 = (f32[2,128,512]{2,1,0:T(8,128)S(1)}, f32[2,128,512]{2,1,0:T(8,128)S(1)}, u32[]{:S(2)}, u32[]{:S(2)}) collective-permute-start(f32[2,128,512]{2,1,0:T(8,128)S(1)} %back.10), channel_id=1, source_target_pairs={{0,2},{1,3},{2,0},{3,1},{4,6},{5,7},{6,4},{7,5},{8,10},{9,11},{10,... | collective-permute-start | bytes 1572872 | tf_op jit(solution)/shard_map/ppermute | solution.py:32

commit v3 on v2

--- a/solution.py
+++ b/solution.py
@@ -65,18 +65,25 @@
     return at[0] == at[1]
 
 
-def rim_body(me_ref, f_ref, last_ref, first_ref, top_ref, bottom_ref):
+def rim_body(me_ref, f_ref, lon_in_ref, lon_out_ref, lat_in_ref, lat_out_ref):
     modes, rows, cols = f_ref.shape
     eye = diagonal(rows)
+    lon_even, lat_even = (me_ref[0] & 1) == 0, (me_ref[1] & 1) == 0
+
+    def lanes(k, c):
+        column = jnp.broadcast_to(f_ref[k, :, c : c + 1], (rows, rows))
+        return jnp.sum(jnp.where(eye, column, 0.0), axis=0, keepdims=True)
+
     for k in range(modes):
-        for c, out in ((cols - 1, last_ref), (0, first_ref)):
-            column = jnp.broadcast_to(f_ref[k, :, c : c + 1], (rows, rows))
-            out[k : k + 1] = jnp.sum(jnp.where(eye, column, 0.0), axis=0, keepdims=True)
-        top_ref[k : k + 1] = f_ref[k, rows - 1 : rows]
-        bottom_ref[k : k + 1] = f_ref[k, 0:1]
-
-
-def stencil_body(count, first, size, me_ref, f_ref, west_ref, east_ref, south_ref, north_ref, *refs):
+        last, first = lanes(k, cols - 1), lanes(k, 0)
+        lon_in_ref[k : k + 1] = jnp.where(lon_even, last, first)
+        lon_out_ref[k : k + 1] = jnp.where(lon_even, first, last)
+        last, first = f_ref[k, rows - 1 : rows], f_ref[k, 0:1]
+        lat_in_ref[k : k + 1] = jnp.where(lat_even, last, first)
+        lat_out_ref[k : k + 1] = jnp.where(lat_even, first, last)
+
+
+def stencil_body(count, first, size, me_ref, f_ref, lon_in, lon_out, lat_in, lat_out, *refs):
     mlon_ref, mlat_ref, w_ref = refs[:3]
     outs = refs[3:]
     modes, rows, cols = f_ref.shape
@@ -86,22 +93,28 @@
     row = lax.broadcasted_iota(jnp.int32, (8, cols), 0)
     weight = jnp.broadcast_to(w_ref[...], (8, cols))
 
-    def column(ref, k):
-        spread = jnp.broadcast_to(ref[pl.ds(k, 1), :], (rows, rows))
-        return jnp.sum(jnp.where(eye, spread, 0.0), axis=1, keepdims=True)
+    lon_even, lat_even = (me_ref[0] & 1) == 0, (me_ref[1] & 1) == 0
+
+    def column(v):
+        return jnp.sum(jnp.where(eye, jnp.broadcast_to(v, (rows, rows)), 0.0), axis=1, keepdims=True)
+
+    def sides(even, inner, outer, k):
+        a, b = inner[pl.ds(k, 1), :], outer[pl.ds(k, 1), :]
+        return jnp.where(even, b, a), jnp.where(even, a, b)
 
     def one(i, _):
         for x in range(count):
             k = (me_ref[0] ^ x) * local + first + i
-            west, east = column(west_ref, k), column(east_ref, k)
+            west, east = (column(v) for v in sides(lon_even, lon_in, lon_out, k))
+            south, north = sides(lat_even, lat_in, lat_out, k)
             for t in range(rows // 8):
                 at = slice(8 * t, 8 * t + 8)
                 f = f_ref[k, at]
-                below = f_ref[k, 8 * t - 1 : 8 * t] if t else south_ref[pl.ds(k, 1), :]
+                below = f_ref[k, 8 * t - 1 : 8 * t] if t else south
                 above = (
                     f_ref[k, 8 * t + 8 : 8 * t + 9]
                     if 8 * t + 8 < rows
-                    else north_ref[pl.ds(k, 1), :]
+                    else north
                 )
                 w = jnp.where(lane == 0, west[at], pltpu.roll(f, 1, 1))
                 e = jnp.where(lane == cols - 1, east[at], pltpu.roll(f, cols - 1, 1))
@@ -501,16 +514,19 @@
     groups = groups_of(local)
     size = local // groups
 
-    ring = [(i, (i + 1) % count) for i in range(count)]
-    line = [(i, i + 1) for i in range(bands - 1)]
-    last, first, top, bottom = small_call(
+    def swaps(n, start, wrap):
+        pairs = [(i, (i + 1) % n) for i in range(start, n if wrap else n - 1, 2)]
+        return pairs + [(j, i) for i, j in pairs]
+
+    lon_in, lon_out, lat_in, lat_out = small_call(
         rim_body, me, (forcing,), [(modes, rows)] * 2 + [(modes, sector)] * 2
     )
-    west = lax.ppermute(last, "lon", ring)
-    east = lax.ppermute(first, "lon", [(j, i) for i, j in ring])
-    south = lax.ppermute(top, "lat", line)
-    north = lax.ppermute(bottom, "lat", [(j, i) for i, j in line])
-    halos = (west, east, south, north)
+    halos = (
+        lax.ppermute(lon_in, "lon", swaps(count, 0, True)),
+        lax.ppermute(lon_out, "lon", swaps(count, 1, True)),
+        lax.ppermute(lat_in, "lat", swaps(bands, 0, False)),
+        lax.ppermute(lat_out, "lat", swaps(bands, 1, False)),
+    )
 
     order = farthest(count)
     sources = []

time: 152 us -> 150 us (0.987)
  waiting for transfers between devices: 44 us -> 40.5 us
  starting transfers between devices: 35.3 us -> 36.9 us
    ppermute x24, waiting for transfers between devices: 41.4 us -> 37.4 us  [exchange(): return lax.ppermute(a, axis, [(i, i ^ x) for i in range(count)])]
    ppermute x24, starting transfers between devices: 28.3 us -> 31.6 us  [exchange(): return lax.ppermute(a, axis, [(i, i ^ x) for i in range(count)])]
    ppermute x4, starting transfers between devices: 7.07 us -> 5.26 us  [the longest x1 2.56 us: per_device(): lax.ppermute(lon_in, 'lon', swaps(count, 0, True))]
  transfers between devices with their start and end apart: 28 -> 28, of which waited for: 9 -> 8; matrix products, arithmetic and copies ran while one was open for 0% -> 0% of each run, Pallas kernels for 35% -> 36%
where the time goes in v3:
time: 150 us; the launch traced here: 149 us
  Pallas kernels  69.3 us (46%)
  waiting for transfers between devices  40.5 us (27%)
  starting transfers between devices  36.9 us (25%)
  local copies, waits for them, and re-layouts  2.2 us (1%)
    ppermute x24, waiting for transfers between devices, exchange(): return lax.ppermute(a, axis, [(i, i ^ x) for i in range(count)])  37.4 us
    ppermute x24, starting transfers between devices, exchange(): return lax.ppermute(a, axis, [(i, i ^ x) for i in range(count)])  31.6 us
    pallas_call x2, Pallas kernels, forward(): pl.pallas_call(functools.partial(forward_body, count, t, part), grid_spec...  21.9 us
    pallas_call x8, Pallas kernels, back(): pl.pallas_call(functools.partial(back_body, x, t), grid_spec=pltpu.Prefet...  18.9 us
    pallas_call x1, Pallas kernels, factors(): pl.pallas_call(functools.partial(factors_body, t), grid=(modes,), in_spec...  9.15 us
    pallas_call x6, Pallas kernels, small_call(): pl.pallas_call(body, grid_spec=pltpu.PrefetchScalarGridSpec(num_scalar_pr...  8.46 us
    pallas_call x3, Pallas kernels, place(): pl.pallas_call(functools.partial(place_body, xs, local, first), grid_spec...  4.94 us
    pallas_call x2, Pallas kernels, modal_parts(): pl.pallas_call(functools.partial(modal_body, chips, t, part * size), grid...  3.18 us
  transfers between devices with their start and end apart: 28, of which 8 were waited for; matrix products, arithmetic and copies ran while one was open for 0% of the time, Pallas kernels for 36%

profile of v3, /device:TPU:0, one launch (start us, length us, event | category | flops | bytes accessed | tf_op | source)
XLA Modules:
  0.0 149.4 jit_solution(6041903343198018476)
XLA Ops:
  0.1 2.2 %copy-done = f32[16,128,512]{2,1,0:T(8,128)S(1)} copy-done((f32[16,128,512]{2,1,0:T(8,128)S(1)}, f32[16,128,512]{2,1,0:T(8,128)}, u32[]{:S(2)}) %copy-start) | copy-done | bytes 4194328
  2.3 1.2 shard_map.82
  4.0 0.7 collective-permute-start.3
  4.7 2.6 %collective-permute-start = (f32[16,128]{1,0:T(8,128)S(1)}, f32[16,128]{1,0:T(8,128)S(1)}, u32[]{:S(2)}, u32[]{:S(2)}) collective-permute-start(f32[16,128]{1,0:T(8,128)S(1)} %get-tuple-element.42), channel_id=1, source_target_pairs={{0,1},{2,3},{1,0},{3,2},{4,5},{6,7},{5,4},{7,6},{8,9},{10,11},{9,8... | collective-permute-start | bytes 24584 | tf_op jit(solution)/shard_map/ppermute | solution.py:525
  7.3 1.5 collective-permute-start.1
  8.9 2.9 %collective-permute-done.1.lon_out = f32[16,128]{1,0:T(8,128)S(1)} collective-permute-done((f32[16,128]{1,0:T(8,128)S(1)}, f32[16,128]{1,0:T(8,128)S(1)}, u32[]{:S(2)}, u32[]{:S(2)}) %collective-permute-start.1) | collective-permute-done | bytes 8224 | tf_op jit(solution)/shard_map/ppermute | solution.py:526
  11.8 2.3 %shard_map.83 = (f32[2,128,512]{2,1,0:T(8,128)S(1)}, f32[2,128,512]{2,1,0:T(8,128)S(1)}, f32[2,128,512]{2,1,0:T(8,128)S(1)}, f32[2,128,512]{2,1,0:T(8,128)S(1)}) custom-call(s32[2]{0:T(128)S(1)} %pad_add_fusion.me_ref, f32[16,128,512]{2,1,0:T(8,128)S(1)} %copy-done, f32[16,128]{1,0:T(8,128)S(1)} %collective-permute-done.lon_in, ...), custom_call_target="tpu_custom_call" | custom-call | flops 1048576 | bytes 262144 | tf_op jit(solution)/shard_map/pallas_call | solution.py:49
  14.4 1.9 %collective-permute-start.5 = (f32[2,128,512]{2,1,0:T(8,128)S(1)}, f32[2,128,512]{2,1,0:T(8,128)S(1)}, u32[]{:S(2)}, u32[]{:S(2)}) collective-permute-start(f32[2,128,512]{2,1,0:T(8,128)S(1)} %get-tuple-element.59), channel_id=1, source_target_pairs={{0,2},{1,3},{2,0},{3,1},{4,6},{5,7},{6,4},{7,5},{8,10},{9,11},{10,... | collective-permute-start | bytes 1572872 | tf_op jit(solution)/shard_map/ppermute | solution.py:32
  16.3 1.4 collective-permute-start.6
  17.7 3.1 %shard_map.84 = (f32[2,128,512]{2,1,0:T(8,128)S(1)}, f32[2,128,512]{2,1,0:T(8,128)}, f32[2,128,512]{2,1,0:T(8,128)S(1)}, f32[2,128,512]{2,1,0:T(8,128)S(1)}) custom-call(s32[2]{0:T(128)S(1)} %pad_add_fusion.me_ref, f32[16,128,512]{2,1,0:T(8,128)S(1)} %copy-done, f32[16,128]{1,0:T(8,128)S(1)} %collective-permute-done.lon_in, ...), custom_call_target="tpu_custom_call" | custom-call | flops 1048576 | bytes 262144 | tf_op jit(solution)/shard_map/pallas_call | solution.py:49
  20.9 9.2 %factors.1 = (f32[4,128,2048]{2,1,0:T(8,128)S(1)}, f32[4,128,2048]{2,1,0:T(8,128)S(1)}, f32[4,4,2048]{2,1,0:T(4,128)S(1)}) custom-call(f32[4,128,2048]{2,1,0:T(8,128)} %refs_6_.1, f32[4,128,2048]{2,1,0:T(8,128)} %refs_7_.3, f32[4,128,2048]{2,1,0:T(8,128)} %refs_8_.3), custom_call_target="tpu_custom_call" | custom-call | flops 62914560 | bytes 20971520 | tf_op jit(solution)/shard_map/factors/pallas_call | solution.py:229
  30.0 0.7 collective-permute-start.8
  31.3 2.8 %basis.1 = (bf16[2048,2048]{1,0:T(8,128)(2,1)S(1)}, bf16[2048,2048]{1,0:T(8,128)(2,1)S(1)}) custom-call(s32[2]{0:T(128)S(1)} %pad_add_fusion.me_ref, f32[2048,2048]{1,0:T(8,128)S(1)} %copy-done.1), custom_call_target="tpu_custom_call" | custom-call | flops 16777216 | bytes 33554432 | tf_op jit(solution)/shard_map/basis/pallas_call | solution.py:156
  34.1 1.6 %collective-permute-start.16 = (f32[2,128,512]{2,1,0:T(8,128)S(1)}, f32[2,128,512]{2,1,0:T(8,128)S(1)}, u32[]{:S(2)}, u32[]{:S(2)}) collective-permute-start(f32[2,128,512]{2,1,0:T(8,128)S(1)} %get-tuple-element.72), channel_id=1, source_target_pairs={{0,2},{1,3},{2,0},{3,1},{4,6},{5,7},{6,4},{7,5},{8,10},{9,11},{10,... | collective-permute-start | bytes 1572872 | tf_op jit(solution)/shard_map/ppermute | solution.py:32
  35.7 0.6 shard_map.86.refs_4_
  36.3 1.5 %collective-permute-start.17 = (f32[2,128,512]{2,1,0:T(8,128)S(1)}, f32[2,128,512]{2,1,0:T(8,128)S(1)}, u32[]{:S(2)}, u32[]{:S(2)}) collective-permute-start(f32[2,128,512]{2,1,0:T(8,128)S(1)} %get-tuple-element.73), channel_id=1, source_target_pairs={{0,3},{1,2},{2,1},{3,0},{4,7},{5,6},{6,5},{7,4},{8,11},{9,10},{10,... | collective-permute-start | bytes 1572872 | tf_op jit(solution)/shard_map/ppermute | solution.py:32
  37.8 4.8 %collective-permute-start.14 = (f32[4,4,2048]{2,1,0:T(4,128)S(1)}, f32[4,4,2048]{2,1,0:T(4,128)S(1)}, u32[]{:S(2)}, u32[]{:S(2)}) collective-permute-start(f32[4,4,2048]{2,1,0:T(4,128)S(1)} %shard_map.86.refs_4_), channel_id=1, source_target_pairs={{0,24},{4,28},{8,16},{12,20},{16,8},{20,12},{24,0},{28,4},{1,25},{... | collective-permute-start | bytes 393224 | tf_op jit(solution)/shard_map/ppermute | solution.py:32
  42.6 10.9 %forward.2 = (f32[2,128,2048]{2,1,0:T(8,128)S(1)}, f32[4,2048]{1,0:T(4,128)S(1)}) custom-call(s32[2]{0:T(128)S(1)} %pad_add_fusion.me_ref, f32[2,128,512]{2,1,0:T(8,128)S(1)} %get-tuple-element.57.refs_0_, f32[2,128,512]{2,1,0:T(8,128)S(1)} %collective-permute-done.4.refs_1_, f32[2,128,512]{2,1,0:T(8,128)S(1)} %collective-permute-done.5.refs_2_, ...), custom_call_target="tpu_custom_call" | custom-call | flops 6442450944 | bytes 16777216 | tf_op jit(solution)/shard_map/forward/pallas_call | solution.py:311
  53.7 3.1 %collective-permute-start.13 = (f32[4,4,2048]{2,1,0:T(4,128)S(1)}, f32[4,4,2048]{2,1,0:T(4,128)S(1)}, u32[]{:S(2)}, u32[]{:S(2)}) collective-permute-start(f32[4,4,2048]{2,1,0:T(4,128)S(1)} %shard_map.86.refs_4_), channel_id=1, source_target_pairs={{0,16},{4,20},{8,24},{12,28},{16,0},{20,4},{24,8},{28,12},{1,17},{... | collective-permute-start | bytes 393224 | tf_op jit(solution)/shard_map/ppermute | solution.py:32
  56.8 1.0 collective-permute-start.12
  58.4 5.4 %collective-permute-done.13.refs_6_ = f32[4,4,2048]{2,1,0:T(4,128)S(1)} collective-permute-done((f32[4,4,2048]{2,1,0:T(4,128)S(1)}, f32[4,4,2048]{2,1,0:T(4,128)S(1)}, u32[]{:S(2)}, u32[]{:S(2)}) %collective-permute-start.13) | collective-permute-done | bytes 131104 | tf_op jit(solution)/shard_map/ppermute | solution.py:32
  63.8 3.0 %collective-permute-start.11 = (f32[4,2048]{1,0:T(4,128)S(1)}, f32[4,2048]{1,0:T(4,128)S(1)}, u32[]{:S(2)}, u32[]{:S(2)}) collective-permute-start(f32[4,2048]{1,0:T(4,128)S(1)} %shard_map.85.refs_0_), channel_id=1, source_target_pairs={{0,24},{4,28},{8,16},{12,20},{16,8},{20,12},{24,0},{28,4},{1,25},{... | collective-permute-start | bytes 98312 | tf_op jit(solution)/shard_map/ppermute | solution.py:32
  66.8 2.7 %collective-permute-done.11.refs_3_ = f32[4,2048]{1,0:T(4,128)S(1)} collective-permute-done((f32[4,2048]{1,0:T(4,128)S(1)}, f32[4,2048]{1,0:T(4,128)S(1)}, u32[]{:S(2)}, u32[]{:S(2)}) %collective-permute-start.11) | collective-permute-done | bytes 32800 | tf_op jit(solution)/shard_map/ppermute | solution.py:32
  69.5 2.1 %collective-permute-done.10.refs_2_ = f32[4,2048]{1,0:T(4,128)S(1)} collective-permute-done((f32[4,2048]{1,0:T(4,128)S(1)}, f32[4,2048]{1,0:T(4,128)S(1)}, u32[]{:S(2)}, u32[]{:S(2)}) %collective-permute-start.10) | collective-permute-done | bytes 32800 | tf_op jit(solution)/shard_map/ppermute | solution.py:32
  71.6 1.8 %collective-permute-done.9.refs_1_ = f32[4,2048]{1,0:T(4,128)S(1)} collective-permute-done((f32[4,2048]{1,0:T(4,128)S(1)}, f32[4,2048]{1,0:T(4,128)S(1)}, u32[]{:S(2)}, u32[]{:S(2)}) %collective-permute-start.9) | collective-permute-done | bytes 32800 | tf_op jit(solution)/shard_map/ppermute | solution.py:32
  73.4 1.6 %modal.2.m_ref = bf16[512,2048]{1,0:T(8,128)(2,1)S(1)} custom-call(s32[2]{0:T(128)S(1)} %pad_add_fusion.me_ref, f32[4,2048]{1,0:T(4,128)S(1)} %shard_map.85.refs_0_, f32[4,2048]{1,0:T(4,128)S(1)} %collective-permute-done.9.refs_1_, f32[4,2048]{1,0:T(4,128)S(1)} %collective-permute-done.10.refs_2_, f32[4,2048]{1,0:T(4,128)S(1)} %collective-permute-done.11.refs_3_, ...), custom_call_target="tpu_custom_call" | custom-call | flops 5242880 | bytes 8388608 | tf_op jit(solution)/shard_map/modal/pallas_call | solution.py:414
  75.0 2.4 %back.8 = f32[2,128,512]{2,1,0:T(8,128)S(1)} custom-call(s32[2]{0:T(128)S(1)} %pad_add_fusion.me_ref, bf16[512,2048]{1,0:T(8,128)(2,1)S(1)} %modal.2.m_ref, bf16[2048,2048]{1,0:T(8,128)(2,1)S(1)} %get-tuple-element.61.refs_4_.hi_ref, bf16[2048,2048]{1,0:T(8,128)(2,1)S(1)} %get-tuple-element.62.refs_5_.lo_ref), custom_call_target="tpu_custom_call" | custom-call | flops 1610612736 | bytes 4194304 | tf_op jit(solution)/shard_map/back/pallas_call | solution.py:453
  77.4 10.9 %forward.3 = (f32[2,128,2048]{2,1,0:T(8,128)S(1)}, f32[4,2048]{1,0:T(4,128)S(1)}) custom-call(s32[2]{0:T(128)S(1)} %pad_add_fusion.me_ref, f32[2,128,512]{2,1,0:T(8,128)S(1)} %get-tuple-element.70.refs_0_, f32[2,128,512]{2,1,0:T(8,128)S(1)} %collective-permute-done.15.refs_1_, f32[2,128,512]{2,1,0:T(8,128)S(1)} %collective-permute-done.16.refs_2_, ...), custom_call_target="tpu_custom_call" | custom-call | flops 6442450944 | bytes 16777216 | tf_op jit(solution)/shard_map/forward/pallas_call | solution.py:311
  88.4 2.4 %back.15 = f32[2,128,512]{2,1,0:T(8,128)S(1)} custom-call(s32[2]{0:T(128)S(1)} %pad_add_fusion.me_ref, bf16[512,2048]{1,0:T(8,128)(2,1)S(1)} %modal.2.m_ref, bf16[2048,2048]{1,0:T(8,128)(2,1)S(1)} %get-tuple-element.61.refs_4_.hi_ref, bf16[2048,2048]{1,0:T(8,128)(2,1)S(1)} %get-tuple-element.62.refs_5_.lo_ref), custom_call_target="tpu_custom_call" | custom-call | flops 1610612736 | bytes 4194304 | tf_op jit(solution)/shard_map/back/pallas_call | solution.py:453
  91.9 3.3 %collective-permute-start.21 = (f32[4,2048]{1,0:T(4,128)S(1)}, f32[4,2048]{1,0:T(4,128)S(1)}, u32[]{:S(2)}, u32[]{:S(2)}) collective-permute-start(f32[4,2048]{1,0:T(4,128)S(1)} %shard_map.87.refs_0_), channel_id=1, source_target_pairs={{0,24},{4,28},{8,16},{12,20},{16,8},{20,12},{24,0},{28,4},{1,25},{... | collective-permute-start | bytes 98312 | tf_op jit(solution)/shard_map/ppermute | solution.py:32
  95.2 1.1 collective-permute-start.19
  96.3 2.4 %back.14 = f32[2,128,512]{2,1,0:T(8,128)S(1)} custom-call(s32[2]{0:T(128)S(1)} %pad_add_fusion.me_ref, bf16[512,2048]{1,0:T(8,128)(2,1)S(1)} %modal.2.m_ref, bf16[2048,2048]{1,0:T(8,128)(2,1)S(1)} %get-tuple-element.61.refs_4_.hi_ref, bf16[2048,2048]{1,0:T(8,128)(2,1)S(1)} %get-tuple-element.62.refs_5_.lo_ref), custom_call_target="tpu_custom_call" | custom-call | flops 1610612736 | bytes 4194304 | tf_op jit(solution)/shard_map/back/pallas_call | solution.py:453
  98.7 2.3 %collective-permute-start.25 = (f32[2,128,512]{2,1,0:T(8,128)S(1)}, f32[2,128,512]{2,1,0:T(8,128)S(1)}, u32[]{:S(2)}, u32[]{:S(2)}) collective-permute-start(f32[2,128,512]{2,1,0:T(8,128)S(1)} %back.14), channel_id=1, source_target_pairs={{0,3},{1,2},{2,1},{3,0},{4,7},{5,6},{6,5},{7,4},{8,11},{9,10},{10,... | collective-permute-start | bytes 1572872 | tf_op jit(solution)/shard_map/ppermute | solution.py:32
  101.0 0.8 collective-permute-start.27
  101.8 1.6 %modal.3.m_ref = bf16[512,2048]{1,0:T(8,128)(2,1)S(1)} custom-call(s32[2]{0:T(128)S(1)} %pad_add_fusion.me_ref, f32[4,2048]{1,0:T(4,128)S(1)} %shard_map.87.refs_0_, f32[4,2048]{1,0:T(4,128)S(1)} %collective-permute-done.19.refs_1_, f32[4,2048]{1,0:T(4,128)S(1)} %collective-permute-done.20.refs_2_, f32[4,2048]{1,0:T(4,128)S(1)} %collective-permute-done.21.refs_3_, ...), custom_call_target="tpu_custom_call" | custom-call | flops 5242880 | bytes 8388608 | tf_op jit(solution)/shard_map/modal/pallas_call | solution.py:414
  103.4 2.4 %back.12 = f32[2,128,512]{2,1,0:T(8,128)S(1)} custom-call(s32[2]{0:T(128)S(1)} %pad_add_fusion.me_ref, bf16[512,2048]{1,0:T(8,128)(2,1)S(1)} %modal.3.m_ref, bf16[2048,2048]{1,0:T(8,128)(2,1)S(1)} %get-tuple-element.61.refs_4_.hi_ref, bf16[2048,2048]{1,0:T(8,128)(2,1)S(1)} %get-tuple-element.62.refs_5_.lo_ref), custom_call_target="tpu_custom_call" | custom-call | flops 1610612736 | bytes 4194304 | tf_op jit(solution)/shard_map/back/pallas_call | solution.py:453
  105.8 2.4 %back.10 = f32[2,128,512]{2,1,0:T(8,128)S(1)} custom-call(s32[2]{0:T(128)S(1)} %pad_add_fusion.me_ref, bf16[512,2048]{1,0:T(8,128)(2,1)S(1)} %modal.3.m_ref, bf16[2048,2048]{1,0:T(8,128)(2,1)S(1)} %get-tuple-element.61.refs_4_.hi_ref, bf16[2048,2048]{1,0:T(8,128)(2,1)S(1)} %get-tuple-element.62.refs_5_.lo_ref), custom_call_target="tpu_custom_call" | custom-call | flops 1610612736 | bytes 4194304 | tf_op jit(solution)/shard_map/back/pallas_call | solution.py:453
  108.2 2.4 %back.9 = f32[2,128,512]{2,1,0:T(8,128)S(1)} custom-call(s32[2]{0:T(128)S(1)} %pad_add_fusion.me_ref, bf16[512,2048]{1,0:T(8,128)(2,1)S(1)} %modal.3.m_ref, bf16[2048,2048]{1,0:T(8,128)(2,1)S(1)} %get-tuple-element.61.refs_4_.hi_ref, bf16[2048,2048]{1,0:T(8,128)(2,1)S(1)} %get-tuple-element.62.refs_5_.lo_ref), custom_call_target="tpu_custom_call" | custom-call | flops 1610612736 | bytes 4194304 | tf_op jit(solution)/shard_map/back/pallas_call | solution.py:453
  110.5 2.1 %collective-permute-start.24 = (f32[2,128,512]{2,1,0:T(8,128)S(1)}, f32[2,128,512]{2,1,0:T(8,128)S(1)}, u32[]{:S(2)}, u32[]{:S(2)}) collective-permute-start(f32[2,128,512]{2,1,0:T(8,128)S(1)} %back.12), channel_id=1, source_target_pairs={{0,3},{1,2},{2,1},{3,0},{4,7},{5,6},{6,5},{7,4},{8,11},{9,10},{10,... | collective-permute-start | bytes 1572872 | tf_op jit(solution)/shard_map/ppermute | solution.py:32
  112.6 0.7 collective-permute-start.22
  113.3 0.8 collective-permute-start.23
  114.1 2.4 %back.13.refs_0_ = f32[2,128,512]{2,1,0:T(8,128)S(1)} custom-call(s32[2]{0:T(128)S(1)} %pad_add_fusion.me_ref, bf16[512,2048]{1,0:T(8,128)(2,1)S(1)} %modal.2.m_ref, bf16[2048,2048]{1,0:T(8,128)(2,1)S(1)} %get-tuple-element.61.refs_4_.hi_ref, bf16[2048,2048]{1,0:T(8,128)(2,1)S(1)} %get-tuple-element.62.refs_5_.lo_ref), custom_call_target="tpu_custom_call" | custom-call | flops 1610612736 | bytes 4194304 | tf_op jit(solution)/shard_map/back/pallas_call | solution.py:453
  116.5 2.4 %back.11.refs_0_ = f32[2,128,512]{2,1,0:T(8,128)S(1)} custom-call(s32[2]{0:T(128)S(1)} %pad_add_fusion.me_ref, bf16[512,2048]{1,0:T(8,128)(2,1)S(1)} %modal.3.m_ref, bf16[2048,2048]{1,0:T(8,128)(2,1)S(1)} %get-tuple-element.61.refs_4_.hi_ref, bf16[2048,2048]{1,0:T(8,128)(2,1)S(1)} %get-tuple-element.62.refs_5_.lo_ref), custom_call_target="tpu_custom_call" | custom-call | flops 1610612736 | bytes 4194304 | tf_op jit(solution)/shard_map/back/pallas_call | solution.py:453
  118.8 19.5 %collective-permute-done.27.refs_3_ = f32[2,128,512]{2,1,0:T(8,128)S(1)} collective-permute-done((f32[2,128,512]{2,1,0:T(8,128)S(1)}, f32[2,128,512]{2,1,0:T(8,128)S(1)}, u32[]{:S(2)}, u32[]{:S(2)}) %collective-permute-start.27) | collective-permute-done | bytes 524320 | tf_op jit(solution)/shard_map/ppermute | solution.py:32
  138.3 1.9 %place.3.refs_2_ = f32[16,128,512]{2,1,0:T(8,128)} custom-call(s32[2]{0:T(128)S(1)} %pad_add_fusion.me_ref, f32[2,128,512]{2,1,0:T(8,128)S(1)} %back.13.refs_0_, f32[2,128,512]{2,1,0:T(8,128)S(1)} %collective-permute-done.25.refs_1_, f32[2,128,512]{2,1,0:T(8,128)S(1)} %collective-permute-done.26.refs_2_, f32[2,128,512]{2,1,0:T(8,128)S(1)} %collective-permute-done.27.refs_3_), custom_call_target="tpu_custom_call" | custom-call | bytes 4194304 | tf_op jit(solution)/shard_map/place/pallas_call | solution.py:488
  140.2 1.5 %place.4.refs_2_ = f32[16,128,512]{2,1,0:T(8,128)} custom-call(s32[2]{0:T(128)S(1)} %pad_add_fusion.me_ref, f32[2,128,512]{2,1,0:T(8,128)S(1)} %back.11.refs_0_, f32[2,128,512]{2,1,0:T(8,128)S(1)} %collective-permute-done.24.refs_1_, f32[16,128,512]{2,1,0:T(8,128)} %place.3.refs_2_), custom_call_target="tpu_custom_call", output_to_operand_aliasing={{}: (3, {})} | custom-call | bytes 2097152 | tf_op jit(solution)/shard_map/place/pallas_call | solution.py:488
  141.8 5.9 %collective-permute-done.23.refs_1_ = f32[2,128,512]{2,1,0:T(8,128)S(1)} collective-permute-done((f32[2,128,512]{2,1,0:T(8,128)S(1)}, f32[2,128,512]{2,1,0:T(8,128)S(1)}, u32[]{:S(2)}, u32[]{:S(2)}) %collective-permute-start.23) | collective-permute-done | bytes 524320 | tf_op jit(solution)/shard_map/ppermute | solution.py:32
  147.7 1.5 %place.5 = f32[16,128,512]{2,1,0:T(8,128)} custom-call(s32[2]{0:T(128)S(1)} %pad_add_fusion.me_ref, f32[2,128,512]{2,1,0:T(8,128)S(1)} %collective-permute-done.22.refs_0_, f32[2,128,512]{2,1,0:T(8,128)S(1)} %collective-permute-done.23.refs_1_, f32[16,128,512]{2,1,0:T(8,128)} %place.4.refs_2_), custom_call_target="tpu_custom_call", output_to_operand_aliasing={{}: (3, {})} | custom-call | bytes 2097152 | tf_op jit(solution)/shard_map/place/pallas_call | solution.py:488
  (42 shorter events, 3.4 us)
Async XLA Ops:
  0.0 11.8 %copy-start.4 = (f32[512]{0:T(512)S(1)}, f32[512]{0:T(512)}, u32[]{:S(2)}) copy-start(f32[512]{0:T(512)} %param.11) | copy-start | bytes 6148
  0.1 2.2 %copy-start = (f32[16,128,512]{2,1,0:T(8,128)S(1)}, f32[16,128,512]{2,1,0:T(8,128)}, u32[]{:S(2)}) copy-start(f32[16,128,512]{2,1,0:T(8,128)} %f_ref.5) | copy-start | bytes 12582916
  2.3 9.6 %copy-start.2 = (f32[128,512]{1,0:T(8,128)S(1)}, f32[128,512]{1,0:T(8,128)}, u32[]{:S(2)}) copy-start(f32[128,512]{1,0:T(8,128)} %refs_0_.3) | copy-start | bytes 786436
  2.3 9.6 %copy-start.3 = (f32[128,512]{1,0:T(8,128)S(1)}, f32[128,512]{1,0:T(8,128)}, u32[]{:S(2)}) copy-start(f32[128,512]{1,0:T(8,128)} %refs_1_.3) | copy-start | bytes 786436
  3.5 8.3 %collective-permute-start.2 = (f32[16,512]{1,0:T(8,128)S(1)}, f32[16,512]{1,0:T(8,128)S(1)}, u32[]{:S(2)}, u32[]{:S(2)}) collective-permute-start(f32[16,512]{1,0:T(8,128)S(1)} %get-tuple-element.44), channel_id=1, source_target_pairs={{0,4},{8,12},{16,20},{24,28},{4,0},{12,8},{20,16},{28,24},{1,5},{9... | collective-permute-start | bytes 98312 | tf_op jit(solution)/shard_map/ppermute | solution.py:527
  4.0 7.8 %collective-permute-start.3 = (f32[16,512]{1,0:T(8,128)S(1)}, f32[16,512]{1,0:T(8,128)S(1)}, u32[]{:S(2)}, u32[]{:S(2)}) collective-permute-start(f32[16,512]{1,0:T(8,128)S(1)} %get-tuple-element.45), channel_id=1, source_target_pairs={{4,8},{12,16},{20,24},{8,4},{16,12},{24,20},{5,9},{13,17},{21,25},... | collective-permute-start | bytes 98312 | tf_op jit(solution)/shard_map/ppermute | solution.py:528
  4.7 4.2 %collective-permute-start = (f32[16,128]{1,0:T(8,128)S(1)}, f32[16,128]{1,0:T(8,128)S(1)}, u32[]{:S(2)}, u32[]{:S(2)}) collective-permute-start(f32[16,128]{1,0:T(8,128)S(1)} %get-tuple-element.42), channel_id=1, source_target_pairs={{0,1},{2,3},{1,0},{3,2},{4,5},{6,7},{5,4},{7,6},{8,9},{10,11},{9,8... | collective-permute-start | bytes 24584 | tf_op jit(solution)/shard_map/ppermute | solution.py:525
  7.3 4.5 %collective-permute-start.1 = (f32[16,128]{1,0:T(8,128)S(1)}, f32[16,128]{1,0:T(8,128)S(1)}, u32[]{:S(2)}, u32[]{:S(2)}) collective-permute-start(f32[16,128]{1,0:T(8,128)S(1)} %get-tuple-element.43), channel_id=1, source_target_pairs={{1,2},{3,0},{2,1},{0,3},{5,6},{7,4},{6,5},{4,7},{9,10},{11,8},{10,... | collective-permute-start | bytes 24584 | tf_op jit(solution)/shard_map/ppermute | solution.py:526
  14.2 22.1 %collective-permute-start.4 = (f32[2,128,512]{2,1,0:T(8,128)S(1)}, f32[2,128,512]{2,1,0:T(8,128)S(1)}, u32[]{:S(2)}, u32[]{:S(2)}) collective-permute-start(f32[2,128,512]{2,1,0:T(8,128)S(1)} %get-tuple-element.58), channel_id=1, source_target_pairs={{0,1},{1,0},{2,3},{3,2},{4,5},{5,4},{6,7},{7,6},{8,9},{9,8},{10,11... | collective-permute-start | bytes 1572872 | tf_op jit(solution)/shard_map/ppermute | solution.py:32
  14.4 23.4 %collective-permute-start.5 = (f32[2,128,512]{2,1,0:T(8,128)S(1)}, f32[2,128,512]{2,1,0:T(8,128)S(1)}, u32[]{:S(2)}, u32[]{:S(2)}) collective-permute-start(f32[2,128,512]{2,1,0:T(8,128)S(1)} %get-tuple-element.59), channel_id=1, source_target_pairs={{0,2},{1,3},{2,0},{3,1},{4,6},{5,7},{6,4},{7,5},{8,10},{9,11},{10,... | collective-permute-start | bytes 1572872 | tf_op jit(solution)/shard_map/ppermute | solution.py:32
  16.3 26.3 %collective-permute-start.6 = (f32[2,128,512]{2,1,0:T(8,128)S(1)}, f32[2,128,512]{2,1,0:T(8,128)S(1)}, u32[]{:S(2)}, u32[]{:S(2)}) collective-permute-start(f32[2,128,512]{2,1,0:T(8,128)S(1)} %get-tuple-element.60), channel_id=1, source_target_pairs={{0,3},{1,2},{2,1},{3,0},{4,7},{5,6},{6,5},{7,4},{8,11},{9,10},{10,... | collective-permute-start | bytes 1572872 | tf_op jit(solution)/shard_map/ppermute | solution.py:32
  17.7 13.6 %copy-start.1 = (f32[2048,2048]{1,0:T(8,128)S(1)}, f32[2048,2048]{1,0:T(8,128)}, u32[]{:S(2)}) copy-start(f32[2048,2048]{1,0:T(8,128)} %e_ref.1) | copy-start | bytes 50331652
  30.0 4.1 %collective-permute-start.8 = (f32[4,4,2048]{2,1,0:T(4,128)S(1)}, f32[4,4,2048]{2,1,0:T(4,128)S(1)}, u32[]{:S(2)}, u32[]{:S(2)}) collective-permute-start(f32[4,4,2048]{2,1,0:T(4,128)S(1)} %get-tuple-element.65.c_own_ref.own_ref.refs_10_), channel_id=1, source_target_pairs={{0,4},{4,0},{8,12},{12,8},{16,20},{20,16},{24,28},{28,24},{1,5},{5... | collective-permute-start | bytes 393224 | tf_op jit(solution)/shard_map/ppermute | solution.py:32
  30.8 46.6 %collective-permute-start.15 = (f32[2,128,512]{2,1,0:T(8,128)}, f32[2,128,512]{2,1,0:T(8,128)S(1)}, u32[]{:S(2)}, u32[]{:S(2)}) collective-permute-start(f32[2,128,512]{2,1,0:T(8,128)} %get-tuple-element.71), channel_id=1, source_target_pairs={{0,1},{1,0},{2,3},{3,2},{4,5},{5,4},{6,7},{7,6},{8,9},{9,8},{10,11... | collective-permute-start | bytes 1572872 | tf_op jit(solution)/shard_map/ppermute | solution.py:32
  34.1 43.2 %collective-permute-start.16 = (f32[2,128,512]{2,1,0:T(8,128)S(1)}, f32[2,128,512]{2,1,0:T(8,128)S(1)}, u32[]{:S(2)}, u32[]{:S(2)}) collective-permute-start(f32[2,128,512]{2,1,0:T(8,128)S(1)} %get-tuple-element.72), channel_id=1, source_target_pairs={{0,2},{1,3},{2,0},{3,1},{4,6},{5,7},{6,4},{7,5},{8,10},{9,11},{10,... | collective-permute-start | bytes 1572872 | tf_op jit(solution)/shard_map/ppermute | solution.py:32
  36.3 41.0 %collective-permute-start.17 = (f32[2,128,512]{2,1,0:T(8,128)S(1)}, f32[2,128,512]{2,1,0:T(8,128)S(1)}, u32[]{:S(2)}, u32[]{:S(2)}) collective-permute-start(f32[2,128,512]{2,1,0:T(8,128)S(1)} %get-tuple-element.73), channel_id=1, source_target_pairs={{0,3},{1,2},{2,1},{3,0},{4,7},{5,6},{6,5},{7,4},{8,11},{9,10},{10,... | collective-permute-start | bytes 1572872 | tf_op jit(solution)/shard_map/ppermute | solution.py:32
  37.8 15.8 %collective-permute-start.14 = (f32[4,4,2048]{2,1,0:T(4,128)S(1)}, f32[4,4,2048]{2,1,0:T(4,128)S(1)}, u32[]{:S(2)}, u32[]{:S(2)}) collective-permute-start(f32[4,4,2048]{2,1,0:T(4,128)S(1)} %shard_map.86.refs_4_), channel_id=1, source_target_pairs={{0,24},{4,28},{8,16},{12,20},{16,8},{20,12},{24,0},{28,4},{1,25},{... | collective-permute-start | bytes 393224 | tf_op jit(solution)/shard_map/ppermute | solution.py:32
  53.6 3.2 %collective-permute-start.7 = (f32[4,2048]{1,0:T(4,128)S(1)}, f32[4,2048]{1,0:T(4,128)S(1)}, u32[]{:S(2)}, u32[]{:S(2)}) collective-permute-start(f32[4,2048]{1,0:T(4,128)S(1)} %get-tuple-element.64.own_ref.refs_8_), channel_id=1, source_target_pairs={{0,4},{4,0},{8,12},{12,8},{16,20},{20,16},{24,28},{28,24},{1,5},{5... | collective-permute-start | bytes 98312 | tf_op jit(solution)/shard_map/ppermute | solution.py:32
  53.7 10.1 %collective-permute-start.13 = (f32[4,4,2048]{2,1,0:T(4,128)S(1)}, f32[4,4,2048]{2,1,0:T(4,128)S(1)}, u32[]{:S(2)}, u32[]{:S(2)}) collective-permute-start(f32[4,4,2048]{2,1,0:T(4,128)S(1)} %shard_map.86.refs_4_), channel_id=1, source_target_pairs={{0,16},{4,20},{8,24},{12,28},{16,0},{20,4},{24,8},{28,12},{1,17},{... | collective-permute-start | bytes 393224 | tf_op jit(solution)/shard_map/ppermute | solution.py:32
  56.8 10.0 %collective-permute-start.12 = (f32[4,4,2048]{2,1,0:T(4,128)S(1)}, f32[4,4,2048]{2,1,0:T(4,128)S(1)}, u32[]{:S(2)}, u32[]{:S(2)}) collective-permute-start(f32[4,4,2048]{2,1,0:T(4,128)S(1)} %shard_map.86.refs_4_), channel_id=1, source_target_pairs={{0,8},{4,12},{8,0},{12,4},{16,24},{20,28},{24,16},{28,20},{1,9},{5... | collective-permute-start | bytes 393224 | tf_op jit(solution)/shard_map/ppermute | solution.py:32
  63.8 5.7 %collective-permute-start.11 = (f32[4,2048]{1,0:T(4,128)S(1)}, f32[4,2048]{1,0:T(4,128)S(1)}, u32[]{:S(2)}, u32[]{:S(2)}) collective-permute-start(f32[4,2048]{1,0:T(4,128)S(1)} %shard_map.85.refs_0_), channel_id=1, source_target_pairs={{0,24},{4,28},{8,16},{12,20},{16,8},{20,12},{24,0},{28,4},{1,25},{... | collective-permute-start | bytes 98312 | tf_op jit(solution)/shard_map/ppermute | solution.py:32
  66.8 4.8 %collective-permute-start.10 = (f32[4,2048]{1,0:T(4,128)S(1)}, f32[4,2048]{1,0:T(4,128)S(1)}, u32[]{:S(2)}, u32[]{:S(2)}) collective-permute-start(f32[4,2048]{1,0:T(4,128)S(1)} %shard_map.85.refs_0_), channel_id=1, source_target_pairs={{0,16},{4,20},{8,24},{12,28},{16,0},{20,4},{24,8},{28,12},{1,17},{... | collective-permute-start | bytes 98312 | tf_op jit(solution)/shard_map/ppermute | solution.py:32
  69.5 3.9 %collective-permute-start.9 = (f32[4,2048]{1,0:T(4,128)S(1)}, f32[4,2048]{1,0:T(4,128)S(1)}, u32[]{:S(2)}, u32[]{:S(2)}) collective-permute-start(f32[4,2048]{1,0:T(4,128)S(1)} %shard_map.85.refs_0_), channel_id=1, source_target_pairs={{0,8},{4,12},{8,0},{12,4},{16,24},{20,28},{24,16},{28,20},{1,9},{5... | collective-permute-start | bytes 98312 | tf_op jit(solution)/shard_map/ppermute | solution.py:32
  88.3 3.0 %collective-permute-start.18 = (f32[4,2048]{1,0:T(4,128)S(1)}, f32[4,2048]{1,0:T(4,128)S(1)}, u32[]{:S(2)}, u32[]{:S(2)}) collective-permute-start(f32[4,2048]{1,0:T(4,128)S(1)} %get-tuple-element.74.own_ref.refs_8_), channel_id=1, source_target_pairs={{0,4},{4,0},{8,12},{12,8},{16,20},{20,16},{24,28},{28,24},{1,5},{5... | collective-permute-start | bytes 98312 | tf_op jit(solution)/shard_map/ppermute | solution.py:32
  90.8 22.6 %collective-permute-start.26 = (f32[2,128,512]{2,1,0:T(8,128)S(1)}, f32[2,128,512]{2,1,0:T(8,128)S(1)}, u32[]{:S(2)}, u32[]{:S(2)}) collective-permute-start(f32[2,128,512]{2,1,0:T(8,128)S(1)} %back.8), channel_id=1, source_target_pairs={{0,1},{1,0},{2,3},{3,2},{4,5},{5,4},{6,7},{7,6},{8,9},{9,8},{10,11... | collective-permute-start | bytes 1572872 | tf_op jit(solution)/shard_map/ppermute | solution.py:32
  91.9 9.2 %collective-permute-start.21 = (f32[4,2048]{1,0:T(4,128)S(1)}, f32[4,2048]{1,0:T(4,128)S(1)}, u32[]{:S(2)}, u32[]{:S(2)}) collective-permute-start(f32[4,2048]{1,0:T(4,128)S(1)} %shard_map.87.refs_0_), channel_id=1, source_target_pairs={{0,24},{4,28},{8,16},{12,20},{16,8},{20,12},{24,0},{28,4},{1,25},{... | collective-permute-start | bytes 98312 | tf_op jit(solution)/shard_map/ppermute | solution.py:32
  95.2 6.6 %collective-permute-start.20 = (f32[4,2048]{1,0:T(4,128)S(1)}, f32[4,2048]{1,0:T(4,128)S(1)}, u32[]{:S(2)}, u32[]{:S(2)}) collective-permute-start(f32[4,2048]{1,0:T(4,128)S(1)} %shard_map.87.refs_0_), channel_id=1, source_target_pairs={{0,16},{4,20},{8,24},{12,28},{16,0},{20,4},{24,8},{28,12},{1,17},{... | collective-permute-start | bytes 98312 | tf_op jit(solution)/shard_map/ppermute | solution.py:32
  95.2 6.6 %collective-permute-start.19 = (f32[4,2048]{1,0:T(4,128)S(1)}, f32[4,2048]{1,0:T(4,128)S(1)}, u32[]{:S(2)}, u32[]{:S(2)}) collective-permute-start(f32[4,2048]{1,0:T(4,128)S(1)} %shard_map.87.refs_0_), channel_id=1, source_target_pairs={{0,8},{4,12},{8,0},{12,4},{16,24},{20,28},{24,16},{28,20},{1,9},{5... | collective-permute-start | bytes 98312 | tf_op jit(solution)/shard_map/ppermute | solution.py:32
  98.7 20.1 %collective-permute-start.25 = (f32[2,128,512]{2,1,0:T(8,128)S(1)}, f32[2,128,512]{2,1,0:T(8,128)S(1)}, u32[]{:S(2)}, u32[]{:S(2)}) collective-permute-start(f32[2,128,512]{2,1,0:T(8,128)S(1)} %back.14), channel_id=1, source_target_pairs={{0,3},{1,2},{2,1},{3,0},{4,7},{5,6},{6,5},{7,4},{8,11},{9,10},{10,... | collective-permute-start | bytes 1572872 | tf_op jit(solution)/shard_map/ppermute | solution.py:32
  101.0 37.3 %collective-permute-start.27 = (f32[2,128,512]{2,1,0:T(8,128)S(1)}, f32[2,128,512]{2,1,0:T(8,128)S(1)}, u32[]{:S(2)}, u32[]{:S(2)}) collective-permute-start(f32[2,128,512]{2,1,0:T(8,128)S(1)} %back.15), channel_id=1, source_target_pairs={{0,2},{1,3},{2,0},{3,1},{4,6},{5,7},{6,4},{7,5},{8,10},{9,11},{10,... | collective-permute-start | bytes 1572872 | tf_op jit(solution)/shard_map/ppermute | solution.py:32
  110.5 29.7 %collective-permute-start.24 = (f32[2,128,512]{2,1,0:T(8,128)S(1)}, f32[2,128,512]{2,1,0:T(8,128)S(1)}, u32[]{:S(2)}, u32[]{:S(2)}) collective-permute-start(f32[2,128,512]{2,1,0:T(8,128)S(1)} %back.12), channel_id=1, source_target_pairs={{0,3},{1,2},{2,1},{3,0},{4,7},{5,6},{6,5},{7,4},{8,11},{9,10},{10,... | collective-permute-start | bytes 1572872 | tf_op jit(solution)/shard_map/ppermute | solution.py:32
  112.6 29.1 %collective-permute-start.22 = (f32[2,128,512]{2,1,0:T(8,128)S(1)}, f32[2,128,512]{2,1,0:T(8,128)S(1)}, u32[]{:S(2)}, u32[]{:S(2)}) collective-permute-start(f32[2,128,512]{2,1,0:T(8,128)S(1)} %back.9), channel_id=1, source_target_pairs={{0,1},{1,0},{2,3},{3,2},{4,5},{5,4},{6,7},{7,6},{8,9},{9,8},{10,11... | collective-permute-start | bytes 1572872 | tf_op jit(solution)/shard_map/ppermute | solution.py:32
  113.3 34.3 %collective-permute-start.23 = (f32[2,128,512]{2,1,0:T(8,128)S(1)}, f32[2,128,512]{2,1,0:T(8,128)S(1)}, u32[]{:S(2)}, u32[]{:S(2)}) collective-permute-start(f32[2,128,512]{2,1,0:T(8,128)S(1)} %back.10), channel_id=1, source_target_pairs={{0,2},{1,3},{2,0},{3,1},{4,6},{5,7},{6,4},{7,5},{8,10},{9,11},{10,... | collective-permute-start | bytes 1572872 | tf_op jit(solution)/shard_map/ppermute | solution.py:32
